TPU v7x, 32 devices: a whole 2x2x4 slice. The times are simulated.
32 devices in a mesh: dp: 2 (over x), tp: 4 (over z), cp: 4 (over y, core).
Axes of the slice: x: 2, y: 2, z: 4, core: 2. Of those that a mesh axis runs over, the one named last changes fastest.
Arguments:
- hidden_in: bfloat16 [4096, 3584], P(('dp', 'cp', 'tp')), parts along dimension 0
- positions: int32 [4096], P(('dp', 'cp', 'tp')), parts along dimension 0
- cache_len: int32 [2], P('dp'), parts along dimension 0
- cache_k: bfloat16 [8192, 512], P(('dp', 'cp', 'tp')), parts along dimension 0
- cache_v: bfloat16 [8192, 512], P(('dp', 'cp', 'tp')), parts along dimension 0
- norm1_gain: bfloat16 [3584], replicated
- w_query: bfloat16 [3584, 3584], P(None, 'tp')
- w_key: bfloat16 [3584, 512], P(None, 'tp')
- w_value: bfloat16 [3584, 512], P(None, 'tp')
- w_out: bfloat16 [3584, 3584], P('tp')
- norm2_gain: bfloat16 [3584], replicated
- w_gate: bfloat16 [3584, 18944], P(None, 'tp')
- w_up: bfloat16 [3584, 18944], P(None, 'tp')
- w_down: bfloat16 [18944, 3584], P('tp')
Outputs:
- output: bfloat16 [4096, 3584], P(('dp', 'cp', 'tp')), parts along dimension 0
There are 2 independent parts. A program takes and returns all parts, laid end to end along the dimension named above; an argument that names none is the same for every part.
All inputs are finite; a program needn't handle non-finite values.
Results may differ from a plain program's by a relative error of at most 0.0108171.
Values are sent between devices in bfloat16 or wider.
A program may use at most 1 GiB of HBM per device.

v0:
```python
import functools
import math
import jax
import jax.numpy as jnp
from jax import lax
from jax.experimental import pallas as pl
from jax.experimental.pallas import tpu as pltpu
from jax.sharding import PartitionSpec as P

HEAD_DIM = 128
ROPE_BASE = 500000.0
NORM_EPS = 1e-5
RUN = 64
KV_BLOCK = 512
LOG2E = 1.4426950408889634


def rms_norm(hidden, norm_gain):
    values = hidden.astype(jnp.float32)
    inv_rms = lax.rsqrt(jnp.mean(values * values, axis=-1, keepdims=True) + NORM_EPS)
    return (values * inv_rms * norm_gain.astype(jnp.float32)).astype(jnp.bfloat16)


def rotary(projected, cos_table, sin_table):
    half_dim = HEAD_DIM // 2
    cos_table = cos_table[:, None, :]
    sin_table = sin_table[:, None, :]
    first_half = projected[..., :half_dim]
    second_half = projected[..., half_dim:]
    rotated = jnp.concatenate([first_half * cos_table - second_half * sin_table, second_half * cos_table + first_half * sin_table], axis=-1)
    return rotated.astype(jnp.bfloat16)


def attn_kernel(clen_ref, q_ref, kc_ref, vc_ref, knl_ref, vnl_ref, knh_ref, vnh_ref, o_ref, vt_ref, m_ref, l_ref, acc_ref):
    cp = lax.axis_index('cp')
    scale = LOG2E / math.sqrt(HEAD_DIM)
    half = q_ref.shape[0] // 2
    slots = kc_ref.shape[0]
    fresh = knl_ref.shape[0]
    cache_len = clen_ref[0]

    @pl.when(pl.program_id(0) == 0)
    def _():
        for ref, base in ((vc_ref, 0), (vnl_ref, slots), (vnh_ref, slots + fresh)):
            for j in range(ref.shape[0] // 512):
                block = ref[j * 512:(j + 1) * 512, :].astype(jnp.float32)
                vt_ref[:, base + j * 512:base + (j + 1) * 512] = block.T.astype(jnp.bfloat16)

    m_ref[...] = jnp.full_like(m_ref, -1e30)
    l_ref[...] = jnp.zeros_like(l_ref)
    acc_ref[...] = jnp.zeros_like(acc_ref)

    def update(parts, keys, vt_cols, masks=(None, None)):
        scores = {}
        for part in parts:
            raw = lax.dot_general(keys, q_ref[part * half:(part + 1) * half, :], (((1,), (1,)), ((), ())), preferred_element_type=jnp.float32)
            scores[part] = raw if masks[part] is None else jnp.where(masks[part], raw, -jnp.inf)
        for part in parts:
            cols = slice(part * half, (part + 1) * half)
            m_old = m_ref[:, cols]
            m_new = jnp.maximum(m_old, jnp.max(scores[part], axis=0, keepdims=True))
            probs = jnp.exp2((scores[part] - m_new) * scale)
            alpha = jnp.exp2((m_old - m_new) * scale)
            l_ref[:, cols] = alpha * l_ref[:, cols] + jnp.sum(probs, axis=0, keepdims=True)
            acc_ref[:, cols] = alpha * acc_ref[:, cols] + jnp.dot(vt_ref[:, vt_cols], probs.astype(jnp.bfloat16), preferred_element_type=jnp.float32)
            m_ref[:, cols] = m_new

    full_blocks = cache_len // KV_BLOCK

    def cache_step(j, carry):
        rows = pl.ds(pl.multiple_of(j * KV_BLOCK, KV_BLOCK), KV_BLOCK)
        update((0, 1), kc_ref[rows, :], rows)
        return carry

    lax.fori_loop(0, full_blocks, cache_step, 0)

    @pl.when(full_blocks * KV_BLOCK < cache_len)
    def _():
        rows = pl.ds(pl.multiple_of(full_blocks * KV_BLOCK, KV_BLOCK), KV_BLOCK)
        visible = full_blocks * KV_BLOCK + lax.broadcasted_iota(jnp.int32, (KV_BLOCK, half), 0) < cache_len
        update((0, 1), kc_ref[rows, :], rows, (visible, visible))

    def new_keys(ref, base, j):
        start = pl.multiple_of(j * half, half)
        return ref[pl.ds(start, half), :], pl.ds(pl.multiple_of(base + start, half), half)

    def both_step(j, carry):
        update((0, 1), *new_keys(knl_ref, slots, j))
        return carry

    lax.fori_loop(0, cp, both_step, 0)
    key_id = lax.broadcasted_iota(jnp.int32, (half, half), 0)
    row_id = lax.broadcasted_iota(jnp.int32, (half, half), 1)
    update((0, 1), *new_keys(knl_ref, slots, cp), (key_id <= row_id, None))

    def high_step(j, carry):
        update((1,), *new_keys(knl_ref, slots, j))
        update((1,), *new_keys(knh_ref, slots + fresh, j))
        return carry

    lax.fori_loop(cp + 1, 4, high_step, 0)
    runs = half // RUN

    def place(i):
        return (runs - 1 - i // RUN) * RUN + i % RUN

    update((1,), *new_keys(knh_ref, slots + fresh, cp), (None, place(key_id) <= place(row_id)))
    o_ref[...] = (acc_ref[...] / l_ref[...]).T.astype(jnp.bfloat16)


def attention(cache_len, queries, cache_kv, low_kv, high_kv, head0, heads):
    rows = queries.shape[0]

    def column(array, index):
        return pl.BlockSpec((array.shape[0], HEAD_DIM), lambda g: (0, index))

    arrays = (cache_kv, low_kv, high_kv)
    return pl.pallas_call(
        attn_kernel,
        grid=(heads,),
        out_shape=jax.ShapeDtypeStruct((rows, heads * HEAD_DIM), jnp.bfloat16),
        in_specs=[pl.BlockSpec(memory_space=pltpu.SMEM), pl.BlockSpec((rows, HEAD_DIM), lambda g: (0, g + head0))]
        + [column(a, i) for a in arrays for i in range(2)],
        out_specs=pl.BlockSpec((rows, HEAD_DIM), lambda g: (0, g)),
        scratch_shapes=[pltpu.VMEM((HEAD_DIM, sum(a.shape[0] for a in arrays)), jnp.bfloat16)] + [pltpu.VMEM((1, rows), jnp.float32)] * 2 + [pltpu.VMEM((HEAD_DIM, rows), jnp.float32)],
        cost_estimate=pl.CostEstimate(flops=2 * 2 * rows * heads * HEAD_DIM * 4608, bytes_accessed=8 * 2**20, transcendentals=rows * heads * 4608),
        name='attend',
    )(cache_len, queries, *[a for a in arrays for _ in range(2)])


def solution(mesh):
    tp_size, cp_size, dp_size = mesh.shape['tp'], mesh.shape['cp'], mesh.shape['dp']
    token_spec = P(('dp', 'cp', 'tp'), None)
    column_spec = P(None, 'tp')
    row_spec = P('tp', None)

    def device_layer(hidden_loc, pos_loc, cache_len, cache_k, cache_v, norm1_gain, w_query, w_key, w_value, w_out, norm2_gain, w_gate, w_up, w_down):
        shard_rows, d_model = hidden_loc.shape
        heads_width = w_query.shape[1]
        dp, tp, cp = lax.axis_index('dp'), lax.axis_index('tp'), lax.axis_index('cp')
        normed = rms_norm(hidden_loc, norm1_gain)
        inv_freq = 1.0 / (ROPE_BASE ** (jnp.arange(HEAD_DIM // 2, dtype=jnp.float32) * (2.0 / HEAD_DIM)))

        def place(parts, me):
            size = len(parts)
            out = jnp.zeros((size,) + parts[0].shape, parts[0].dtype)
            for shift, part in enumerate(parts):
                out = lax.dynamic_update_index_in_dim(out, part, (me - shift) % size, 0)
            return out

        def shifted(part, axis_name, size, shift):
            return part if shift == 0 else lax.ppermute(part, axis_name, [(i, (i + shift) % size) for i in range(size)])

        def share(block):
            return place([shifted(block, 'cp', cp_size, shift) for shift in range(cp_size)], cp).reshape(-1, block.shape[-1])

        def exchange(block, split_axis):
            pieces = [lax.dynamic_index_in_dim(block, (tp + shift) % tp_size, split_axis, keepdims=False) for shift in range(tp_size)]
            return place([shifted(piece, 'tp', tp_size, shift) for shift, piece in enumerate(pieces)], tp)

        slots = cache_k.shape[0]
        cache_kv = jnp.stack([cache_k.reshape(slots, tp_size, HEAD_DIM), cache_v.reshape(slots, tp_size, HEAD_DIM)], axis=2)
        cache_kv = jnp.transpose(cache_kv.reshape(slots, tp_size, 2 * HEAD_DIM), (1, 0, 2))
        cache_kv = share(exchange(cache_kv, 0).reshape(tp_size * slots, 2 * HEAD_DIM))

        def project(index):
            rows_in = lax.all_gather(normed[index * RUN:(index + 1) * RUN], 'tp', axis=0, tiled=True)
            runs = cp * tp_size + jnp.arange(tp_size)
            if index == 1:
                runs = 2 * cp_size * tp_size - 1 - runs
            positions = cache_len[0] + (runs[:, None] * RUN + jnp.arange(RUN)[None, :]).reshape(-1)
            angles = positions.astype(jnp.float32)[:, None] * inv_freq[None, :]
            cos_table, sin_table = jnp.cos(angles), jnp.sin(angles)

            def rotated(weight):
                wide = jnp.dot(rows_in, weight, preferred_element_type=jnp.float32).reshape(rows_in.shape[0], -1, HEAD_DIM)
                return rotary(wide, cos_table, sin_table).reshape(rows_in.shape[0], -1)

            values = jnp.dot(rows_in, w_value, preferred_element_type=jnp.float32).astype(jnp.bfloat16)
            shared = share(jnp.concatenate([rotated(w_key), values], axis=1))
            return rows_in, rotated(w_query), shared

        rows_low, q_low, low_kv = project(0)
        rows_high, q_high, high_kv = project(1)

        core, row_y = cp % 2, cp // 2
        piece_rows = w_out.shape[0] // (dp_size * cp_size)
        half_rows = w_out.shape[0] // 2
        piece = lax.dynamic_slice_in_dim(w_out, core * half_rows + (dp * 2 + row_y) * piece_rows, piece_rows, 0)
        piece, cache_kv, low_kv, q_low, rows_high = lax.optimization_barrier((piece, cache_kv, low_kv, q_low, rows_high))
        groups = [[(d * tp_size + t) * cp_size + 2 * y + k for d in range(dp_size) for t in range(tp_size) for y in range(cp_size // 2)] for k in range(2)]
        w_out_mine = lax.all_gather(piece, ('dp', 'tp', 'cp'), axis_index_groups=groups, axis=0, tiled=True)

        queries = jnp.concatenate([q_low, q_high], axis=0)
        groups_of_heads = []
        for head0, heads in ((0, 4), (4, 3)):
            attended = attention(cache_len, queries, cache_kv, low_kv, high_kv, head0, heads)
            attended = exchange(attended.reshape(2, tp_size, RUN, heads * HEAD_DIM), 1)
            groups_of_heads.append(attended.reshape(tp_size, shard_rows, heads * HEAD_DIM))
        attended = jnp.concatenate(groups_of_heads, axis=2).reshape(tp_size, shard_rows, 2, dp_size, -1)
        attended = jnp.transpose(attended, (2, 1, 3, 0, 4)).reshape(2, shard_rows, -1)
        attended, w_out_mine = lax.optimization_barrier((attended, w_out_mine))
        w_out_other = lax.ppermute(w_out_mine, 'cp', [(i, i ^ 1) for i in range(cp_size)])
        attn_out = jnp.dot(lax.dynamic_index_in_dim(attended, core, 0, keepdims=False), w_out_mine, preferred_element_type=jnp.float32)
        attn_out = attn_out + jnp.dot(lax.dynamic_index_in_dim(attended, 1 - core, 0, keepdims=False), w_out_other, preferred_element_type=jnp.float32)
        residual_mid = (hidden_loc.astype(jnp.float32) + attn_out).astype(jnp.bfloat16)
        normed_mid = rms_norm(residual_mid, norm2_gain)

        outs = []
        for index in range(2):
            rows = slice(index * RUN, (index + 1) * RUN)
            group_mid = lax.all_gather(normed_mid[rows], 'tp', axis=0, tiled=True)
            gate_proj = jnp.dot(group_mid, w_gate, preferred_element_type=jnp.float32)
            up_proj = jnp.dot(group_mid, w_up, preferred_element_type=jnp.float32)
            hidden_mlp = (jax.nn.silu(gate_proj) * up_proj).astype(jnp.bfloat16)
            mlp_part = jnp.dot(hidden_mlp, w_down, preferred_element_type=jnp.float32)
            summed = lax.psum_scatter(mlp_part, 'tp', scatter_dimension=0, tiled=True)
            outs.append((residual_mid[rows].astype(jnp.float32) + summed).astype(jnp.bfloat16))
        return jnp.concatenate(outs, axis=0)

    return jax.shard_map(device_layer, mesh=mesh, in_specs=(token_spec, P(('dp', 'cp', 'tp')), P('dp'), token_spec, token_spec, P(), column_spec, column_spec, column_spec, row_spec, P(), column_spec, column_spec, row_spec), out_specs=token_spec, check_vma=False)
```

profile of v0, /device:TPU:0, one launch (start us, length us, event | category | flops | bytes accessed | tf_op | source)
XLA Modules:
  0.0 558.6 jit_solution(12339894572689174930)
XLA Ops:
  12.0 3.1 collective-permute-start
  15.2 2.7 collective-permute-start.1
  22.6 4.9 collective-permute-done.1
  35.5 6.2 %collective-permute-done.3 = bf16[1024,256]{1,0:T(8,128)(2,1)S(1)} collective-permute-done((bf16[1024,256]{1,0:T(8,128)(2,1)S(1)}, bf16[1024,256]{1,0:T(8,128)(2,1)S(1)}, u32[]{:S(2)}, u32[]{:S(2)}) %collective-permute-start.3) | collective-permute-done | bytes 524320 | tf_op jit(solution)/shard_map/ppermute | solution.py:152
  44.2 9.0 %collective-permute-done.5 = bf16[1024,256]{1,0:T(8,128)(2,1)S(1)} collective-permute-done((bf16[1024,256]{1,0:T(8,128)(2,1)S(1)}, bf16[1024,256]{1,0:T(8,128)(2,1)S(1)}, u32[]{:S(2)}, u32[]{:S(2)}) %collective-permute-start.5) | collective-permute-done | bytes 524320 | tf_op jit(solution)/shard_map/ppermute | solution.py:152
  54.1 4.6 all-gather.8.cloned.1.call-done
  60.9 39.6 %all-gather.6.cloned.1.call-done = bf16[256,3584]{1,0:T(8,128)(2,1)} async-done(((bf16[64,3584]{1,0:T(8,128)(2,1)}), bf16[256,3584]{1,0:T(8,128)(2,1)}) %all-gather.6.cloned.1.call-update) | async-done | bytes 1835024 | tf_op jit(solution)/shard_map/all_gather | solution.py:167
  108.6 5.4 fusion.58
  126.7 5.4 fusion.59
  137.3 21.1 %attend.2 = bf16[512,512]{1,0:T(8,128)(2,1)} custom-call(s32[1]{0:T(128)} %copy.100.clen_ref, bf16[512,896]{1,0:T(8,128)(2,1)} %pad_maximum_fusion.q_ref, bf16[4096,256]{1,0:T(8,128)(2,1)} %bitcast.15.kc_ref.vc_ref, bf16[4096,256]{1,0:T(8,128)(2,1)} %bitcast.15.kc_ref.vc_ref, bf16[1024,256]{1,0:T(8,128)(2,1)} %bitcast.160, bf16[1024,256]{1,0:T(8,128)(2,1)} %bitcast.161, ...), custom_call_target="tpu_custom_call" | custom-call | flops 4831838208 | bytes 8388608 | tf_op jit(solution)/shard_map/attend/pallas_call | solution.py:118
  163.8 16.6 %attend.3 = bf16[512,384]{1,0:T(8,128)(2,1)} custom-call(s32[1]{0:T(128)} %copy.100.clen_ref, bf16[512,896]{1,0:T(8,128)(2,1)} %pad_maximum_fusion.q_ref, bf16[4096,256]{1,0:T(8,128)(2,1)} %bitcast.15.kc_ref.vc_ref, bf16[4096,256]{1,0:T(8,128)(2,1)} %bitcast.15.kc_ref.vc_ref, bf16[1024,256]{1,0:T(8,128)(2,1)} %bitcast.162, bf16[1024,256]{1,0:T(8,128)(2,1)} %bitcast.163, ...), custom_call_target="tpu_custom_call" | custom-call | flops 3623878656 | bytes 8388608 | tf_op jit(solution)/shard_map/attend/pallas_call | solution.py:118
  185.0 5.9 %collective-permute-done.15 = bf16[2,64,384]{2,1,0:T(8,128)(2,1)S(1)} collective-permute-done((bf16[2,64,384]{2,1,0:T(8,128)(2,1)S(1)}, bf16[2,64,384]{2,1,0:T(8,128)(2,1)S(1)}, u32[]{:S(2)}, u32[]{:S(2)}) %collective-permute-start.15) | collective-permute-done | bytes 98336 | tf_op jit(solution)/shard_map/ppermute | solution.py:152
  192.1 9.1 %collective-permute-done.16 = bf16[2,64,384]{2,1,0:T(8,128)(2,1)S(1)} collective-permute-done((bf16[2,64,384]{2,1,0:T(8,128)(2,1)S(1)}, bf16[2,64,384]{2,1,0:T(8,128)(2,1)S(1)}, u32[]{:S(2)}, u32[]{:S(2)}) %collective-permute-start.16) | collective-permute-done | bytes 98336 | tf_op jit(solution)/shard_map/ppermute | solution.py:152
  203.2 89.7 %all-gather.10.cloned.1.call-done = bf16[1792,3584]{1,0:T(8,128)(2,1)} async-done(((bf16[112,3584]{1,0:T(8,128)(2,1)}), bf16[1792,3584]{1,0:T(8,128)(2,1)}) %all-gather.10.cloned.1.call-update) | async-done | bytes 12845072 | tf_op jit(solution)/shard_map/all_gather | solution.py:192
  292.9 6.6 %fusion.25 = f32[128,3584]{1,0:T(8,128)S(1)} fusion(bf16[1792,3584]{1,0:T(8,128)(2,1)} %all-gather.10.cloned.1.call-done, bf16[2,128,1792]{1,2,0:T(8,128)(2,1)S(1)} %bitcast.141, s32[]{:T(128)S(6)} %select_n.205), kind=kOutput, calls=%fused_computation.48 | convolution fusion | flops 1644167168 | bytes 15138820 | tf_op jit(solution)/shard_map/dot_general | solution.py:204
  299.5 12.9 %collective-permute-done.18 = bf16[1792,3584]{1,0:T(8,128)(2,1)} collective-permute-done((bf16[1792,3584]{1,0:T(8,128)(2,1)}, bf16[1792,3584]{1,0:T(8,128)(2,1)}, u32[]{:S(2)}, u32[]{:S(2)}) %collective-permute-start.18) | collective-permute-done | bytes 12845088 | tf_op jit(solution)/shard_map/ppermute | solution.py:203
  312.3 6.8 %fusion.18 = (f32[128]{0:T(128)S(1)}, bf16[128,3584]{1,0:T(8,128)(2,1)S(1)}) fusion(f32[128,3584]{1,0:T(8,128)S(1)} %fusion.25, bf16[1792,3584]{1,0:T(8,128)(2,1)} %collective-permute-done.18, bf16[2,128,1792]{1,2,0:T(8,128)(2,1)S(1)} %bitcast.142, s32[]{:T(128)S(6)} %select_n.206, bf16[128,3584]{1,0:T(8,128)(2,1)S(1)} %copy-done.2), kind=kOutput, calls=%fused_computation.25 | convolution fusion | flops 1647378304 | bytes 16974340 | tf_op jit(solution)/shard_map/dot_general | solution.py:205
  321.1 39.0 %all-gather.14.cloned.1.call-done = bf16[256,3584]{1,0:T(8,128)(2,1)} async-done(((bf16[64,3584]{1,0:T(8,128)(2,1)}), bf16[256,3584]{1,0:T(8,128)(2,1)}) %all-gather.14.cloned.1.call-update) | async-done | bytes 1835024 | tf_op jit(solution)/shard_map/all_gather | solution.py:212
  360.1 18.0 %fusion.61 = f32[256,4736]{1,0:T(8,128)} fusion(bf16[256,3584]{1,0:T(8,128)(2,1)} %all-gather.14.cloned.1.call-done, bf16[3584,4736]{1,0:T(8,128)(2,1)} %param.24), kind=kOutput, calls=%fused_computation.136 | convolution fusion | flops 8690597888 | bytes 40632320 | tf_op jit(solution)/shard_map/dot_general | solution.py:213
  378.0 31.9 %fusion.2 = f32[256,3584]{1,0:T(8,128)} fusion(bf16[4736,3584]{1,0:T(8,128)(2,1)} %param.26, bf16[256,3584]{1,0:T(8,128)(2,1)} %all-gather.14.cloned.1.call-done, bf16[3584,4736]{1,0:T(8,128)(2,1)} %param.25, f32[256,4736]{1,0:T(8,128)} %fusion.61), kind=kOutput, calls=%fused_computation.4 | convolution fusion | flops 17388470272 | bytes 78249984 | tf_op jit(solution)/shard_map/dot_general | solution.py:216
  410.3 18.0 %fusion.60 = f32[256,4736]{1,0:T(8,128)} fusion(bf16[256,3584]{1,0:T(8,128)(2,1)} %all-gather.12.cloned.1.call-done, bf16[3584,4736]{1,0:T(8,128)(2,1)} %param.24), kind=kOutput, calls=%fused_computation.135 | convolution fusion | flops 8690597888 | bytes 40632320 | tf_op jit(solution)/shard_map/dot_general | solution.py:213
  428.2 31.9 %fusion.3 = f32[256,3584]{1,0:T(8,128)} fusion(bf16[4736,3584]{1,0:T(8,128)(2,1)} %param.26, bf16[256,3584]{1,0:T(8,128)(2,1)} %all-gather.12.cloned.1.call-done, bf16[3584,4736]{1,0:T(8,128)(2,1)} %param.25, f32[256,4736]{1,0:T(8,128)} %fusion.60), kind=kOutput, calls=%fused_computation.5 | convolution fusion | flops 17388470272 | bytes 78249984 | tf_op jit(solution)/shard_map/dot_general | solution.py:216
  460.2 17.6 %reduce-scatter.5.cloned.1.call-done = f32[64,3584]{1,0:T(8,128)} async-done(((f32[256,3584]{1,0:T(8,128)}), f32[64,3584]{1,0:T(8,128)}) %reduce-scatter.5.cloned.1.call-update) | async-done | bytes 917520 | tf_op jit(solution)/shard_map/reduce_scatter | solution.py:217
  477.7 71.0 %reduce-scatter.3.cloned.1.call-done = f32[64,3584]{1,0:T(8,128)} async-done(((f32[256,3584]{1,0:T(8,128)}), f32[64,3584]{1,0:T(8,128)}) %reduce-scatter.3.cloned.1.call-update) | async-done | bytes 917520 | tf_op jit(solution)/shard_map/reduce_scatter | solution.py:217
  (165 shorter events, 66.3 us)
Async XLA Ops:
  6.5 52.1 %all-gather.8.cloned.1.call-start = ((), (), s32[]{:S(2)}) async-start(), calls=%async_computation.3 | async-start | bytes 2293760 | tf_op jit(solution)/shard_map/all_gather | solution.py:167
  11.3 89.2 %all-gather.6.cloned.1.call-start = ((), (), s32[]{:S(2)}) async-start(), calls=%async_computation.2 | async-start | bytes 2293760 | tf_op jit(solution)/shard_map/all_gather | solution.py:167
  12.0 10.6 %collective-permute-start = (bf16[256,256]{1,0:T(8,128)(2,1)S(1)}, bf16[256,256]{1,0:T(8,128)(2,1)S(1)}, u32[]{:S(2)}, u32[]{:S(2)}) collective-permute-start(bf16[256,256]{1,0:T(8,128)(2,1)S(1)} %bitcast.170), channel_id=1, source_target_pairs={{0,4},{4,8},{8,12},{12,0},{1,5},{5,9},{9,13},{13,1},{2,6},{6,10},{... | collective-permute-start | bytes 393224 | tf_op jit(solution)/shard_map/ppermute | solution.py:152
  15.2 12.3 %collective-permute-start.1 = (bf16[256,256]{1,0:T(8,128)(2,1)S(1)}, bf16[256,256]{1,0:T(8,128)(2,1)S(1)}, u32[]{:S(2)}, u32[]{:S(2)}) collective-permute-start(bf16[256,256]{1,0:T(8,128)(2,1)S(1)} %bitcast.169), channel_id=1, source_target_pairs={{0,8},{4,12},{8,0},{12,4},{1,9},{5,13},{9,1},{13,5},{2,10},{6,14},... | collective-permute-start | bytes 393224 | tf_op jit(solution)/shard_map/ppermute | solution.py:152
  18.0 10.3 %collective-permute-start.2 = (bf16[256,256]{1,0:T(8,128)(2,1)S(1)}, bf16[256,256]{1,0:T(8,128)(2,1)S(1)}, u32[]{:S(2)}, u32[]{:S(2)}) collective-permute-start(bf16[256,256]{1,0:T(8,128)(2,1)S(1)} %bitcast.168), channel_id=1, source_target_pairs={{0,12},{4,0},{8,4},{12,8},{1,13},{5,1},{9,5},{13,9},{2,14},{6,2},{... | collective-permute-start | bytes 393224 | tf_op jit(solution)/shard_map/ppermute | solution.py:152
  19.4 273.4 %all-gather.10.cloned.1.call-start = ((), (), s32[]{:S(2)}) async-start(), calls=%async_computation.4 | async-start | bytes 13647872 | tf_op jit(solution)/shard_map/all_gather | solution.py:192
  28.2 13.4 %collective-permute-start.3 = (bf16[1024,256]{1,0:T(8,128)(2,1)S(1)}, bf16[1024,256]{1,0:T(8,128)(2,1)S(1)}, u32[]{:S(2)}, u32[]{:S(2)}) collective-permute-start(bf16[1024,256]{1,0:T(8,128)(2,1)S(1)} %bitcast.145), channel_id=1, source_target_pairs={{0,1},{1,2},{2,3},{3,0},{4,5},{5,6},{6,7},{7,4},{8,9},{9,10},{10,1... | collective-permute-start | bytes 1572872 | tf_op jit(solution)/shard_map/ppermute | solution.py:152
  28.6 14.8 %collective-permute-start.4 = (bf16[1024,256]{1,0:T(8,128)(2,1)S(1)}, bf16[1024,256]{1,0:T(8,128)(2,1)S(1)}, u32[]{:S(2)}, u32[]{:S(2)}) collective-permute-start(bf16[1024,256]{1,0:T(8,128)(2,1)S(1)} %bitcast.146), channel_id=1, source_target_pairs={{0,2},{1,3},{2,0},{3,1},{4,6},{5,7},{6,4},{7,5},{8,10},{9,11},{10,... | collective-permute-start | bytes 1572872 | tf_op jit(solution)/shard_map/ppermute | solution.py:152
  31.8 21.5 %collective-permute-start.5 = (bf16[1024,256]{1,0:T(8,128)(2,1)S(1)}, bf16[1024,256]{1,0:T(8,128)(2,1)S(1)}, u32[]{:S(2)}, u32[]{:S(2)}) collective-permute-start(bf16[1024,256]{1,0:T(8,128)(2,1)S(1)} %bitcast.147), channel_id=1, source_target_pairs={{0,3},{1,0},{2,1},{3,2},{4,7},{5,4},{6,5},{7,6},{8,11},{9,8},{10,9... | collective-permute-start | bytes 1572872 | tf_op jit(solution)/shard_map/ppermute | solution.py:152
  105.6 9.5 %collective-permute-start.6 = (bf16[256,256]{0,1:T(8,128)(2,1)}, bf16[256,256]{0,1:T(8,128)(2,1)S(1)}, u32[]{:S(2)}, u32[]{:S(2)}) collective-permute-start(bf16[256,256]{0,1:T(8,128)(2,1)} %get-tuple-element.43), channel_id=1, source_target_pairs={{0,1},{1,2},{2,3},{3,0},{4,5},{5,6},{6,7},{7,4},{8,9},{9,10},{10,1... | collective-permute-start | bytes 393224 | tf_op jit(solution)/shard_map/ppermute | solution.py:152
  105.6 11.2 %collective-permute-start.7 = (bf16[256,256]{0,1:T(8,128)(2,1)}, bf16[256,256]{0,1:T(8,128)(2,1)S(1)}, u32[]{:S(2)}, u32[]{:S(2)}) collective-permute-start(bf16[256,256]{0,1:T(8,128)(2,1)} %get-tuple-element.43), channel_id=1, source_target_pairs={{0,2},{1,3},{2,0},{3,1},{4,6},{5,7},{6,4},{7,5},{8,10},{9,11},{10,... | collective-permute-start | bytes 393224 | tf_op jit(solution)/shard_map/ppermute | solution.py:152
  107.0 11.4 %collective-permute-start.8 = (bf16[256,256]{0,1:T(8,128)(2,1)}, bf16[256,256]{0,1:T(8,128)(2,1)}, u32[]{:S(2)}, u32[]{:S(2)}) collective-permute-start(bf16[256,256]{0,1:T(8,128)(2,1)} %get-tuple-element.43), channel_id=1, source_target_pairs={{0,3},{1,0},{2,1},{3,2},{4,7},{5,4},{6,5},{7,6},{8,11},{9,8},{10,9... | collective-permute-start | bytes 393224 | tf_op jit(solution)/shard_map/ppermute | solution.py:152
  123.0 237.1 %all-gather.14.cloned.1.call-start = ((), (), s32[]{:S(2)}) async-start(), calls=%async_computation.7 | async-start | bytes 2293760 | tf_op jit(solution)/shard_map/all_gather | solution.py:212
  125.1 9.7 %collective-permute-start.11 = (bf16[256,256]{0,1:T(8,128)(2,1)}, bf16[256,256]{0,1:T(8,128)(2,1)}, u32[]{:S(2)}, u32[]{:S(2)}) collective-permute-start(bf16[256,256]{0,1:T(8,128)(2,1)} %get-tuple-element.41), channel_id=1, source_target_pairs={{0,3},{1,0},{2,1},{3,2},{4,7},{5,4},{6,5},{7,6},{8,11},{9,8},{10,9... | collective-permute-start | bytes 393224 | tf_op jit(solution)/shard_map/ppermute | solution.py:152
  159.4 42.8 %collective-permute-start.12 = (bf16[2,64,512]{2,1,0:T(8,128)(2,1)S(1)}, bf16[2,64,512]{2,1,0:T(8,128)(2,1)S(1)}, u32[]{:S(2)}, u32[]{:S(2)}) collective-permute-start(bf16[2,64,512]{2,1,0:T(8,128)(2,1)S(1)} %get-tuple-element.29), channel_id=1, source_target_pairs={{0,4},{4,8},{8,12},{12,0},{1,5},{5,9},{9,13},{13,1},{2,6},{6,10},{... | collective-permute-start | bytes 393224 | tf_op jit(solution)/shard_map/ppermute | solution.py:152
  160.3 42.0 %collective-permute-start.13 = (bf16[2,64,512]{2,1,0:T(8,128)(2,1)S(1)}, bf16[2,64,512]{2,1,0:T(8,128)(2,1)S(1)}, u32[]{:S(2)}, u32[]{:S(2)}) collective-permute-start(bf16[2,64,512]{2,1,0:T(8,128)(2,1)S(1)} %get-tuple-element.28), channel_id=1, source_target_pairs={{0,8},{4,12},{8,0},{12,4},{1,9},{5,13},{9,1},{13,5},{2,10},{6,14},... | collective-permute-start | bytes 393224 | tf_op jit(solution)/shard_map/ppermute | solution.py:152
  161.6 40.8 %collective-permute-start.14 = (bf16[2,64,512]{2,1,0:T(8,128)(2,1)S(1)}, bf16[2,64,512]{2,1,0:T(8,128)(2,1)S(1)}, u32[]{:S(2)}, u32[]{:S(2)}) collective-permute-start(bf16[2,64,512]{2,1,0:T(8,128)(2,1)S(1)} %get-tuple-element.27), channel_id=1, source_target_pairs={{0,12},{4,0},{8,4},{12,8},{1,13},{5,1},{9,5},{13,9},{2,14},{6,2},{... | collective-permute-start | bytes 393224 | tf_op jit(solution)/shard_map/ppermute | solution.py:152
  181.4 9.5 %collective-permute-start.15 = (bf16[2,64,384]{2,1,0:T(8,128)(2,1)S(1)}, bf16[2,64,384]{2,1,0:T(8,128)(2,1)S(1)}, u32[]{:S(2)}, u32[]{:S(2)}) collective-permute-start(bf16[2,64,384]{2,1,0:T(8,128)(2,1)S(1)} %get-tuple-element.36), channel_id=1, source_target_pairs={{0,4},{4,8},{8,12},{12,0},{1,5},{5,9},{9,13},{13,1},{2,6},{6,10},{... | collective-permute-start | bytes 294920 | tf_op jit(solution)/shard_map/ppermute | solution.py:152
  181.6 19.6 %collective-permute-start.16 = (bf16[2,64,384]{2,1,0:T(8,128)(2,1)S(1)}, bf16[2,64,384]{2,1,0:T(8,128)(2,1)S(1)}, u32[]{:S(2)}, u32[]{:S(2)}) collective-permute-start(bf16[2,64,384]{2,1,0:T(8,128)(2,1)S(1)} %get-tuple-element.35), channel_id=1, source_target_pairs={{0,8},{4,12},{8,0},{12,4},{1,9},{5,13},{9,1},{13,5},{2,10},{6,14},... | collective-permute-start | bytes 294920 | tf_op jit(solution)/shard_map/ppermute | solution.py:152
  190.9 11.3 %collective-permute-start.17 = (bf16[2,64,384]{2,1,0:T(8,128)(2,1)S(1)}, bf16[2,64,384]{2,1,0:T(8,128)(2,1)S(1)}, u32[]{:S(2)}, u32[]{:S(2)}) collective-permute-start(bf16[2,64,384]{2,1,0:T(8,128)(2,1)S(1)} %get-tuple-element.34), channel_id=1, source_target_pairs={{0,12},{4,0},{8,4},{12,8},{1,13},{5,1},{9,5},{13,9},{2,14},{6,2},{... | collective-permute-start | bytes 294920 | tf_op jit(solution)/shard_map/ppermute | solution.py:152
  292.9 19.5 %collective-permute-start.18 = (bf16[1792,3584]{1,0:T(8,128)(2,1)}, bf16[1792,3584]{1,0:T(8,128)(2,1)}, u32[]{:S(2)}, u32[]{:S(2)}) collective-permute-start(bf16[1792,3584]{1,0:T(8,128)(2,1)} %all-gather.10.cloned.1.call-done), channel_id=1, source_target_pairs={{0,1},{1,0},{2,3},{3,2},{4,5},{5,4},{6,7},{7,6},{8,9},{9,8},{10,11... | collective-permute-start | bytes 38535176 | tf_op jit(solution)/shard_map/ppermute | solution.py:203
  320.4 89.8 %all-gather.12.cloned.1.call-start = ((), (), s32[]{:S(2)}) async-start(), calls=%async_computation.5 | async-start | bytes 2293760 | tf_op jit(solution)/shard_map/all_gather | solution.py:212
  321.0 156.7 %reduce-scatter.5.cloned.1.call-start = ((), (), s32[]{:S(2)}) async-start(), calls=%async_computation.8 | async-start | bytes 4587520 | tf_op jit(solution)/shard_map/reduce_scatter | solution.py:217
  409.9 138.8 %reduce-scatter.3.cloned.1.call-start = ((), (), s32[]{:S(2)}) async-start(), calls=%async_computation.6 | async-start | bytes 4587520 | tf_op jit(solution)/shard_map/reduce_scatter | solution.py:217
  (20 other events, 317.6 us)
Sparse Core Ops, SparseCore 0:
  11.5 47.1 all-gather.7
  60.2 40.2 all-gather.5
  123.1 169.6 all-gather.9
  320.5 39.5 all-gather.13
  361.5 40.0 all-gather.11
  410.1 67.6 reduce-scatter.4
  480.0 68.6 reduce-scatter.2
where the time goes:
time: 566 us; the launch traced here: 559 us
  waiting for transfers between devices  313 us (55%)
  matrix products  130 us (23%)
  Pallas kernels  37.7 us (7%)
  local copies, waits for them, and re-layouts  28.1 us (5%)
  starting transfers between devices  23.5 us (4%)
  between operations  15.4 us (3%)
  other arithmetic  11 us (2%)
    all_gather x1, waiting for transfers between devices, device_layer(): lax.all_gather(piece, ('dp', 'tp', 'cp'), axis_index_groups=groups, axis=...  89.7 us
    reduce_scatter x2, waiting for transfers between devices, device_layer(): summed = lax.psum_scatter(mlp_part, 'tp', scatter_dimension=0, tiled=True)  88.6 us
    dot_general x2, matrix products, device_layer(): mlp_part = jnp.dot(hidden_mlp, w_down, preferred_element_type=jnp.float32)  63.8 us
    all_gather x2, waiting for transfers between devices, project(): lax.all_gather(normed[index * RUN:(index + 1) * RUN], 'tp', axis=0, tiled...  44.2 us
    all_gather x2, waiting for transfers between devices, device_layer(): group_mid = lax.all_gather(normed_mid[rows], 'tp', axis=0, tiled=True)  39 us
    ppermute x18, waiting for transfers between devices, shifted(): lax.ppermute(part, axis_name, [(i, (i + shift) % size) for i in range(siz...  37.8 us
    pallas_call x2, Pallas kernels, attention(): pl.pallas_call(attn_kernel, grid=(heads,), out_shape=jax.ShapeDtypeStruct...  37.7 us
    dot_general x2, matrix products, device_layer(): gate_proj = jnp.dot(group_mid, w_gate, preferred_element_type=jnp.float32)  35.9 us
  transfers between devices with their start and end apart: 26, of which 15 were waited for; matrix products, arithmetic and copies ran while one was open for 25% of the time, Pallas kernels for 7%

commit v1 on v0

v1 whole, which is shorter than its diff:
```python
import functools
import math
import jax
import jax.numpy as jnp
from jax import lax
from jax.experimental import pallas as pl
from jax.experimental.pallas import tpu as pltpu
from jax.sharding import PartitionSpec as P

HEAD_DIM = 128
ROPE_BASE = 500000.0
NORM_EPS = 1e-5
RUN = 64
KV_BLOCK = 512
LOG2E = 1.4426950408889634


def rms_norm(hidden, norm_gain):
    values = hidden.astype(jnp.float32)
    inv_rms = lax.rsqrt(jnp.mean(values * values, axis=-1, keepdims=True) + NORM_EPS)
    return (values * inv_rms * norm_gain.astype(jnp.float32)).astype(jnp.bfloat16)


def rotary(projected, cos_table, sin_table):
    half_dim = HEAD_DIM // 2
    cos_table = cos_table[:, None, :]
    sin_table = sin_table[:, None, :]
    first_half = projected[..., :half_dim]
    second_half = projected[..., half_dim:]
    rotated = jnp.concatenate([first_half * cos_table - second_half * sin_table, second_half * cos_table + first_half * sin_table], axis=-1)
    return rotated.astype(jnp.bfloat16)


def attn_kernel(is_low, clen_ref, q_ref, kc_ref, vc_ref, knl_ref, vnl_ref, knh_ref, vnh_ref, o_ref, vt_ref, m_ref, l_ref, acc_ref):
    cp = lax.axis_index('cp')
    scale = LOG2E / math.sqrt(HEAD_DIM)
    half = q_ref.shape[0]
    slots = kc_ref.shape[0]
    fresh = knl_ref.shape[0]
    cache_len = clen_ref[0]

    @pl.when(pl.program_id(0) == 0)
    def _():
        for ref, base in ((vc_ref, 0), (vnl_ref, slots), (vnh_ref, slots + fresh))[:2 if is_low else 3]:
            for j in range(ref.shape[0] // 512):
                block = ref[j * 512:(j + 1) * 512, :].astype(jnp.float32)
                vt_ref[:, base + j * 512:base + (j + 1) * 512] = block.T.astype(jnp.bfloat16)

    m_ref[...] = jnp.full_like(m_ref, -1e30)
    l_ref[...] = jnp.zeros_like(l_ref)
    acc_ref[...] = jnp.zeros_like(acc_ref)

    def update(blocks):
        scores = []
        for keys, _, mask in blocks:
            raw = lax.dot_general(keys, q_ref[...], (((1,), (1,)), ((), ())), preferred_element_type=jnp.float32)
            scores.append(raw if mask is None else jnp.where(mask, raw, -jnp.inf))
        for (_, vt_cols, _), score in zip(blocks, scores):
            m_old = m_ref[...]
            m_new = jnp.maximum(m_old, jnp.max(score, axis=0, keepdims=True))
            probs = jnp.exp2((score - m_new) * scale)
            alpha = jnp.exp2((m_old - m_new) * scale)
            l_ref[...] = alpha * l_ref[...] + jnp.sum(probs, axis=0, keepdims=True)
            acc_ref[...] = alpha * acc_ref[...] + jnp.dot(vt_ref[:, vt_cols], probs.astype(jnp.bfloat16), preferred_element_type=jnp.float32)
            m_ref[...] = m_new

    def cache_block(start):
        rows = pl.ds(pl.multiple_of(start, KV_BLOCK), KV_BLOCK)
        visible = start + lax.broadcasted_iota(jnp.int32, (KV_BLOCK, half), 0) < cache_len
        return rows, visible

    full_pairs = cache_len // (2 * KV_BLOCK)

    def cache_step(j, carry):
        first, second = (cache_block(j * 2 * KV_BLOCK + i * KV_BLOCK)[0] for i in range(2))
        update([(kc_ref[first, :], first, None), (kc_ref[second, :], second, None)])
        return carry

    lax.fori_loop(0, full_pairs, cache_step, 0)

    def tail_step(j, carry):
        rows, visible = cache_block(j * KV_BLOCK)
        update([(kc_ref[rows, :], rows, visible)])
        return carry

    lax.fori_loop(2 * full_pairs, (cache_len + KV_BLOCK - 1) // KV_BLOCK, tail_step, 0)

    def new_keys(ref, base, j, mask=None):
        start = pl.multiple_of(j * half, half)
        return ref[pl.ds(start, half), :], pl.ds(pl.multiple_of(base + start, half), half), mask

    def low_step(j, carry):
        update([new_keys(knl_ref, slots, j)])
        return carry

    key_id = lax.broadcasted_iota(jnp.int32, (half, half), 0)
    row_id = lax.broadcasted_iota(jnp.int32, (half, half), 1)
    if is_low:
        lax.fori_loop(0, cp, low_step, 0)
        update([new_keys(knl_ref, slots, cp, key_id <= row_id)])
    else:
        for j in range(0, 4, 2):
            update([new_keys(knl_ref, slots, j), new_keys(knl_ref, slots, j + 1)])

        def high_step(j, carry):
            update([new_keys(knh_ref, slots + fresh, j)])
            return carry

        lax.fori_loop(cp + 1, 4, high_step, 0)
        runs = half // RUN

        def place(i):
            return (runs - 1 - i // RUN) * RUN + i % RUN

        update([new_keys(knh_ref, slots + fresh, cp, place(key_id) <= place(row_id))])
    o_ref[...] = (acc_ref[...] / l_ref[...]).T.astype(jnp.bfloat16)


def attention(cache_len, queries, cache_kv, low_kv, high_kv, is_low):
    rows, width = queries.shape
    heads = width // HEAD_DIM

    def column(array, index):
        return pl.BlockSpec((array.shape[0], HEAD_DIM), lambda g: (0, index))

    arrays = (cache_kv, low_kv, high_kv)
    return pl.pallas_call(
        functools.partial(attn_kernel, is_low),
        grid=(heads,),
        out_shape=jax.ShapeDtypeStruct((rows, width), jnp.bfloat16),
        in_specs=[pl.BlockSpec(memory_space=pltpu.SMEM), pl.BlockSpec((rows, HEAD_DIM), lambda g: (0, g))]
        + [column(a, i) for a in arrays for i in range(2)],
        out_specs=pl.BlockSpec((rows, HEAD_DIM), lambda g: (0, g)),
        scratch_shapes=[pltpu.VMEM((HEAD_DIM, sum(a.shape[0] for a in arrays)), jnp.bfloat16)] + [pltpu.VMEM((1, rows), jnp.float32)] * 2 + [pltpu.VMEM((HEAD_DIM, rows), jnp.float32)],
        cost_estimate=pl.CostEstimate(flops=2 * 2 * rows * width * 4608, bytes_accessed=8 * 2**20, transcendentals=rows * heads * 4608),
        name='attend',
    )(cache_len, queries, *[a for a in arrays for _ in range(2)])


def solution(mesh):
    tp_size, cp_size, dp_size = mesh.shape['tp'], mesh.shape['cp'], mesh.shape['dp']
    token_spec = P(('dp', 'cp', 'tp'), None)
    column_spec = P(None, 'tp')
    row_spec = P('tp', None)

    def device_layer(hidden_loc, pos_loc, cache_len, cache_k, cache_v, norm1_gain, w_query, w_key, w_value, w_out, norm2_gain, w_gate, w_up, w_down):
        _, d_model = hidden_loc.shape
        dp, tp, cp = lax.axis_index('dp'), lax.axis_index('tp'), lax.axis_index('cp')
        inv_freq = 1.0 / (ROPE_BASE ** (jnp.arange(HEAD_DIM // 2, dtype=jnp.float32) * (2.0 / HEAD_DIM)))

        def place(parts, me):
            size = len(parts)
            out = jnp.zeros((size,) + parts[0].shape, parts[0].dtype)
            for shift, part in enumerate(parts):
                out = lax.dynamic_update_index_in_dim(out, part, (me - shift) % size, 0)
            return out

        def shifted(part, axis_name, size, shift):
            return part if shift == 0 else lax.ppermute(part, axis_name, [(i, (i + shift) % size) for i in range(size)])

        def share(block):
            return place([shifted(block, 'cp', cp_size, shift) for shift in range(cp_size)], cp).reshape(-1, block.shape[-1])

        def exchange(block, split_axis):
            pieces = [lax.dynamic_index_in_dim(block, (tp + shift) % tp_size, split_axis, keepdims=False) for shift in range(tp_size)]
            return place([shifted(piece, 'tp', tp_size, shift) for shift, piece in enumerate(pieces)], tp)

        slots = cache_k.shape[0]
        cache_kv = jnp.stack([cache_k.reshape(slots, tp_size, HEAD_DIM), cache_v.reshape(slots, tp_size, HEAD_DIM)], axis=2)
        cache_kv = jnp.transpose(cache_kv.reshape(slots, tp_size, 2 * HEAD_DIM), (1, 0, 2))
        cache_kv = share(exchange(cache_kv, 0).reshape(tp_size * slots, 2 * HEAD_DIM))

        core, row_y = cp % 2, cp // 2
        column_width = d_model // tp_size
        piece_rows = w_out.shape[0] // (dp_size * cp_size)
        piece = lax.dynamic_slice_in_dim(w_out, (core * 4 + row_y * 2 + dp) * piece_rows, piece_rows, 0)
        columns = exchange(piece.reshape(piece_rows, tp_size, column_width), 1)
        for axis_name, size, flip, me in (('dp', dp_size, 1, dp), ('cp', cp_size, 2, row_y), ('cp', cp_size, 1, core)):
            columns = place([columns, lax.ppermute(columns, axis_name, [(i, i ^ flip) for i in range(size)])], me)
        columns = jnp.transpose(columns.reshape(dp_size * cp_size, tp_size, piece_rows, column_width), (1, 0, 2, 3))
        w_out_columns = columns.reshape(-1, column_width)

        gathered = [lax.all_gather(hidden_loc[i * RUN:(i + 1) * RUN], 'tp', axis=0, tiled=True) for i in range(2)]

        def project(index, rows_in):
            rows_in = rms_norm(rows_in, norm1_gain)
            runs = cp * tp_size + jnp.arange(tp_size)
            if index == 1:
                runs = 2 * cp_size * tp_size - 1 - runs
            positions = cache_len[0] + (runs[:, None] * RUN + jnp.arange(RUN)[None, :]).reshape(-1)
            angles = positions.astype(jnp.float32)[:, None] * inv_freq[None, :]
            cos_table, sin_table = jnp.cos(angles), jnp.sin(angles)

            def rotated(weight):
                wide = jnp.dot(rows_in, weight, preferred_element_type=jnp.float32).reshape(rows_in.shape[0], -1, HEAD_DIM)
                return rotary(wide, cos_table, sin_table).reshape(rows_in.shape[0], -1)

            values = jnp.dot(rows_in, w_value, preferred_element_type=jnp.float32).astype(jnp.bfloat16)
            return rotated(w_query), jnp.concatenate([rotated(w_key), values], axis=1)

        gathered[0], cache_kv, w_out_columns = lax.optimization_barrier((gathered[0], cache_kv, w_out_columns))
        q_low, low_kv = project(0, gathered[0])
        low_kv = share(low_kv)
        gathered[1], q_low, low_kv = lax.optimization_barrier((gathered[1], q_low, low_kv))
        q_high, high_kv = project(1, gathered[1])
        high_kv = share(high_kv)

        attended = [attention(cache_len, q_low, cache_kv, low_kv, high_kv, True)]
        q_high, attended[0] = lax.optimization_barrier((q_high, attended[0]))
        attended.append(attention(cache_len, q_high, cache_kv, low_kv, high_kv, False))
        column0 = tp * column_width
        outs = []
        for index in range(2):
            heads_all = lax.all_gather(attended[index], 'tp', axis=1, tiled=True)
            residual = lax.dynamic_slice_in_dim(gathered[index], column0, column_width, 1).astype(jnp.float32)
            mid = (residual + jnp.dot(heads_all, w_out_columns, preferred_element_type=jnp.float32)).astype(jnp.bfloat16)
            mid = lax.all_gather(mid, 'tp', axis=1, tiled=True)
            group_mid = rms_norm(mid, norm2_gain)
            gate_proj = jnp.dot(group_mid, w_gate, preferred_element_type=jnp.float32)
            up_proj = jnp.dot(group_mid, w_up, preferred_element_type=jnp.float32)
            hidden_mlp = (jax.nn.silu(gate_proj) * up_proj).astype(jnp.bfloat16)
            mlp_part = jnp.dot(hidden_mlp, w_down, preferred_element_type=jnp.float32)
            summed = lax.psum_scatter(mlp_part, 'tp', scatter_dimension=0, tiled=True)
            mine = lax.dynamic_slice_in_dim(mid, tp * RUN, RUN, 0)
            outs.append((mine.astype(jnp.float32) + summed).astype(jnp.bfloat16))
        return jnp.concatenate(outs, axis=0)

    return jax.shard_map(device_layer, mesh=mesh, in_specs=(token_spec, P(('dp', 'cp', 'tp')), P('dp'), token_spec, token_spec, P(), column_spec, column_spec, column_spec, row_spec, P(), column_spec, column_spec, row_spec), out_specs=token_spec, check_vma=False)
```

time: 566 us -> 598 us (1.057)
  local copies, waits for them, and re-layouts: 28.1 us -> 47.1 us
  other arithmetic: 11 us -> 17.7 us
    ppermute x1 -> x3, waiting for transfers between devices: 12.9 us -> 46.1 us  [device_layer(): lax.ppermute(columns, axis_name, [(i, i ^ flip) for i in range(size)])]
    all_gather x5 -> x6, waiting for transfers between devices: 173 us -> 142 us  [the longest x2 107 us: device_layer(): heads_all = lax.all_gather(attended[index], 'tp', axis=1, tiled=True)]
    dynamic_update_slice x24 -> x26, local copies, waits for them, and re-layouts: 8.29 us -> 21.1 us  [place(): out = lax.dynamic_update_index_in_dim(out, part, (me - shift) % size, 0)]
    reduce_sum x1 -> x4, other arithmetic: 1.45 us -> 7.9 us  [rms_norm(): jnp.mean(values * values, axis=-1, keepdims=True) + NORM_EPS]
    ppermute x18 -> x15, waiting for transfers between devices: 37.8 us -> 36.2 us  [shifted(): lax.ppermute(part, axis_name, [(i, (i + shift) % size) for i in range(siz...]
    ppermute x18 -> x15, starting transfers between devices: 23 us -> 22.8 us  [shifted(): lax.ppermute(part, axis_name, [(i, (i + shift) % size) for i in range(siz...]
  transfers between devices with their start and end apart: 26 -> 26, of which waited for: 15 -> 14; matrix products, arithmetic and copies ran while one was open for 25% -> 29% of each run, Pallas kernels for 7% -> 0%
where the time goes in v1:
time: 598 us; the launch traced here: 589 us
  waiting for transfers between devices  309 us (52%)
  matrix products  131 us (22%)
  local copies, waits for them, and re-layouts  47.1 us (8%)
  Pallas kernels  43 us (7%)
  starting transfers between devices  26.6 us (4%)
  other arithmetic  17.7 us (3%)
  between operations  15.1 us (3%)
    all_gather x2, waiting for transfers between devices, device_layer(): heads_all = lax.all_gather(attended[index], 'tp', axis=1, tiled=True)  107 us
    reduce_scatter x2, waiting for transfers between devices, device_layer(): summed = lax.psum_scatter(mlp_part, 'tp', scatter_dimension=0, tiled=True)  84.3 us
    dot_general x2, matrix products, device_layer(): mlp_part = jnp.dot(hidden_mlp, w_down, preferred_element_type=jnp.float32)  64 us
    ppermute x3, waiting for transfers between devices, device_layer(): lax.ppermute(columns, axis_name, [(i, i ^ flip) for i in range(size)])  46.1 us
    pallas_call x2, Pallas kernels, attention(): pl.pallas_call(functools.partial(attn_kernel, is_low), grid=(heads,), out...  43 us
    dot_general x2, matrix products, device_layer(): gate_proj = jnp.dot(group_mid, w_gate, preferred_element_type=jnp.float32)  36.8 us
    ppermute x15, waiting for transfers between devices, shifted(): lax.ppermute(part, axis_name, [(i, (i + shift) % size) for i in range(siz...  36.2 us
    all_gather x2, waiting for transfers between devices, device_layer(): mid = lax.all_gather(mid, 'tp', axis=1, tiled=True)  35.2 us
  transfers between devices with their start and end apart: 26, of which 14 were waited for; matrix products, arithmetic and copies ran while one was open for 29% of the time, Pallas kernels for 0%

profile of v1, /device:TPU:0, one launch (start us, length us, event | category | flops | bytes accessed | tf_op | source)
XLA Modules:
  0.0 589.5 jit_solution(18014794612325517494)
XLA Ops:
  22.7 6.8 %collective-permute-done.7 = bf16[112,896]{1,0:T(8,128)(2,1)} collective-permute-done((bf16[112,896]{1,0:T(8,128)(2,1)}, bf16[112,896]{1,0:T(8,128)(2,1)}, u32[]{:S(2)}, u32[]{:S(2)}) %collective-permute-start.7) | collective-permute-done | bytes 200736 | tf_op jit(solution)/shard_map/ppermute | solution.py:159
  33.4 17.0 %collective-permute-done.9 = bf16[4,112,896]{2,1,0:T(8,128)(2,1)} collective-permute-done((bf16[4,112,896]{2,1,0:T(8,128)(2,1)S(1)}, bf16[4,112,896]{2,1,0:T(8,128)(2,1)}, u32[]{:S(2)}, u32[]{:S(2)}) %collective-permute-start.9) | collective-permute-done | bytes 802848 | tf_op jit(solution)/shard_map/ppermute | solution.py:179
  58.8 29.1 %collective-permute-done.10 = bf16[2,4,112,896]{3,2,0,1:T(8,128)(2,1)} collective-permute-done((bf16[2,4,112,896]{3,2,0,1:T(8,128)(2,1)S(1)}, bf16[2,4,112,896]{3,2,0,1:T(8,128)(2,1)}, u32[]{:S(2)}, u32[]{:S(2)}) %collective-permute-start.10) | collective-permute-done | bytes 1605664 | tf_op jit(solution)/shard_map/ppermute | solution.py:179
  90.8 3.9 collective-permute-start
  99.2 5.4 collective-permute-done.1
  109.4 8.6 %collective-permute-done.3 = bf16[1024,256]{1,0:T(8,128)(2,1)S(1)} collective-permute-done((bf16[1024,256]{1,0:T(8,128)(2,1)S(1)}, bf16[1024,256]{1,0:T(8,128)(2,1)S(1)}, u32[]{:S(2)}, u32[]{:S(2)}) %collective-permute-start.3) | collective-permute-done | bytes 524320 | tf_op jit(solution)/shard_map/ppermute | solution.py:159
  119.9 9.3 %collective-permute-done.5 = bf16[1024,256]{1,0:T(8,128)(2,1)S(1)} collective-permute-done((bf16[1024,256]{1,0:T(8,128)(2,1)S(1)}, bf16[1024,256]{1,0:T(8,128)(2,1)S(1)}, u32[]{:S(2)}, u32[]{:S(2)}) %collective-permute-start.5) | collective-permute-done | bytes 524320 | tf_op jit(solution)/shard_map/ppermute | solution.py:159
  132.6 3.9 bitcast_dynamic-update-slice_fusion
  136.5 3.9 bitcast_dynamic-update-slice_fusion.1
  150.0 5.5 fusion.69
  166.4 7.1 %fusion.65 = f32[256,896]{0,1:T(8,128)} fusion(bf16[3584,896]{1,0:T(8,128)(2,1)} %param.19, bf16[256,3584]{1,0:T(8,128)(2,1)} %all-gather.9.cloned.1.call-done, f32[256]{0:T(256)S(1)} %add_rsqrt_fusion.2, f32[3584]{0:T(1024)S(1)} %convert_element_type.108), kind=kOutput, calls=%fused_computation.140 | convolution fusion | flops 1647837184 | bytes 9190400 | tf_op jit(solution)/shard_map/dot_general | solution.py:195
  190.3 14.1 %attend.2 = bf16[256,896]{1,0:T(8,128)(2,1)} custom-call(s32[1]{0:T(128)} %copy.97.clen_ref, bf16[256,896]{1,0:T(8,128)(2,1)} %copy.56.q_ref, bf16[4096,256]{1,0:T(8,128)(2,1)} %bitcast.110, bf16[4096,256]{1,0:T(8,128)(2,1)} %bitcast.111, bf16[1024,256]{1,0:T(8,128)(2,1)} %bitcast.129, bf16[1024,256]{1,0:T(8,128)(2,1)} %bitcast.130, ...), custom_call_target="tpu_custom_call" | custom-call | flops 4227858432 | bytes 8388608 | tf_op jit(solution)/shard_map/attend/pallas_call | solution.py:127
  205.4 28.9 %attend.3 = bf16[256,896]{1,0:T(8,128)(2,1)} custom-call(s32[1]{0:T(128)} %copy.97.clen_ref, bf16[256,896]{1,0:T(8,128)(2,1)} %copy.57.q_ref, bf16[4096,256]{1,0:T(8,128)(2,1)} %bitcast.112, bf16[4096,256]{1,0:T(8,128)(2,1)} %bitcast.113, bf16[1024,256]{1,0:T(8,128)(2,1)} %bitcast.131, bf16[1024,256]{1,0:T(8,128)(2,1)} %bitcast.132, ...), custom_call_target="tpu_custom_call" | custom-call | flops 4227858432 | bytes 8388608 | tf_op jit(solution)/shard_map/attend/pallas_call | solution.py:127
  234.9 71.2 %all-gather.15.cloned.1.call-done = bf16[256,3584]{1,0:T(8,128)(2,1)} async-done(((bf16[256,896]{1,0:T(8,128)(2,1)}), bf16[256,3584]{1,0:T(8,128)(2,1)}) %all-gather.15.cloned.1.call-update) | async-done | bytes 1835024 | tf_op jit(solution)/shard_map/all_gather | solution.py:214
  306.2 6.3 %fusion.29 = bf16[256,896]{1,0:T(8,128)(2,1)} fusion(bf16[256,3584]{1,0:T(8,128)(2,1)} %all-gather.15.cloned.1.call-done, bf16[3584,896]{1,0:T(8,128)(2,1)} %bitcast.29, bf16[256,3584]{1,0:T(8,128)(2,1)} %all-gather.9.cloned.1.call-done, s32[]{:T(128)S(6)} %select_n.237), kind=kOutput, calls=%fused_computation.45 | convolution fusion | flops 1644855296 | bytes 9175044 | tf_op jit(solution)/shard_map/dot_general | solution.py:216
  312.5 35.3 %all-gather.11.cloned.1.call-done = bf16[256,3584]{1,0:T(8,128)(2,1)} async-done(((bf16[256,896]{1,0:T(8,128)(2,1)}), bf16[256,3584]{1,0:T(8,128)(2,1)}) %all-gather.11.cloned.1.call-update) | async-done | bytes 1835024 | tf_op jit(solution)/shard_map/all_gather | solution.py:214
  347.8 6.2 %fusion.28 = bf16[256,896]{1,0:T(8,128)(2,1)} fusion(bf16[256,3584]{1,0:T(8,128)(2,1)} %all-gather.11.cloned.1.call-done, bf16[3584,896]{1,0:T(8,128)(2,1)} %bitcast.29, bf16[256,3584]{1,0:T(8,128)(2,1)S(1)} %copy-done.4, s32[]{:T(128)S(6)} %select_n.237), kind=kOutput, calls=%fused_computation.44 | convolution fusion | flops 1644855296 | bytes 9175044 | tf_op jit(solution)/shard_map/dot_general | solution.py:216
  354.3 35.2 %all-gather.17.cloned.1.call-done = bf16[256,3584]{1,0:T(8,128)(2,1)} async-done(((bf16[256,896]{1,0:T(8,128)(2,1)}), bf16[256,3584]{1,0:T(8,128)(2,1)}) %all-gather.17.cloned.1.call-update) | async-done | bytes 1835024 | tf_op jit(solution)/shard_map/all_gather | solution.py:217
  391.5 18.3 %fusion.32 = f32[256,4736]{1,0:T(8,128)} fusion(bf16[3584,4736]{1,0:T(8,128)(2,1)} %param.24, bf16[256,3584]{1,0:T(8,128)(2,1)} %all-gather.17.cloned.1.call-done, f32[256]{0:T(256)S(1)} %add_rsqrt_fusion, f32[3584]{0:T(1024)S(1)} %convert_element_type.123), kind=kOutput, calls=%fused_computation.60 | convolution fusion | flops 8694267904 | bytes 40647680 | tf_op jit(solution)/shard_map/dot_general | solution.py:219
  409.7 31.7 %fusion.2 = f32[256,3584]{1,0:T(8,128)} fusion(bf16[4736,3584]{1,0:T(8,128)(2,1)} %param.26, bf16[3584,4736]{1,0:T(8,128)(2,1)} %param.25, f32[256,4736]{1,0:T(8,128)} %fusion.32, bf16[256,3584]{1,0:T(8,128)(2,1)S(1)} %copy-done.2, f32[256]{0:T(256)S(1)} %add_rsqrt_fusion, f32[3584]{0:T(1024)S(1)} %convert_element_type.123), kind=kOutput, calls=%fused_computation.4 | convolution fusion | flops 17392140288 | bytes 78265344 | tf_op jit(solution)/shard_map/dot_general | solution.py:222
  443.7 18.5 %fusion.36 = f32[256,4736]{1,0:T(8,128)} fusion(bf16[3584,4736]{1,0:T(8,128)(2,1)} %param.24, bf16[256,3584]{1,0:T(8,128)(2,1)} %all-gather.13.cloned.1.call-done, f32[3584]{0:T(1024)S(1)} %convert_element_type.123, f32[256]{0:T(256)S(1)} %add_rsqrt_fusion.1), kind=kOutput, calls=%fused_computation.61 | convolution fusion | flops 8694267904 | bytes 40647680 | tf_op jit(solution)/shard_map/dot_general | solution.py:219
  462.2 32.3 %fusion.3 = f32[256,3584]{1,0:T(8,128)} fusion(bf16[4736,3584]{1,0:T(8,128)(2,1)} %param.26, bf16[3584,4736]{1,0:T(8,128)(2,1)} %param.25, f32[256,4736]{1,0:T(8,128)} %fusion.36, bf16[256,3584]{1,0:T(8,128)(2,1)} %all-gather.13.cloned.1.call-done, f32[3584]{0:T(1024)S(1)} %convert_element_type.123, f32[256]{0:T(256)S(1)} %add_rsqrt_fusion.1), kind=kOutput, calls=%fused_computation.5 | convolution fusion | flops 17392140288 | bytes 78265344 | tf_op jit(solution)/shard_map/dot_general | solution.py:222
  494.5 14.4 %reduce-scatter.5.cloned.1.call-done = f32[64,3584]{1,0:T(8,128)} async-done(((f32[256,3584]{1,0:T(8,128)}), f32[64,3584]{1,0:T(8,128)}) %reduce-scatter.5.cloned.1.call-update) | async-done | bytes 917520 | tf_op jit(solution)/shard_map/reduce_scatter | solution.py:223
  510.2 69.9 %reduce-scatter.3.cloned.1.call-done = f32[64,3584]{1,0:T(8,128)} async-done(((f32[256,3584]{1,0:T(8,128)}), f32[64,3584]{1,0:T(8,128)}) %reduce-scatter.3.cloned.1.call-update) | async-done | bytes 917520 | tf_op jit(solution)/shard_map/reduce_scatter | solution.py:223
  (175 shorter events, 91.8 us)
Async XLA Ops:
  6.5 133.8 %all-gather.7.cloned.1.call-start = ((), (), s32[]{:S(2)}) async-start(), calls=%async_computation.2 | async-start | bytes 2293760 | tf_op jit(solution)/shard_map/all_gather | solution.py:183
  10.4 11.3 %collective-permute-start.6 = (bf16[112,896]{1,0:T(8,128)(2,1)}, bf16[112,896]{1,0:T(8,128)(2,1)}, u32[]{:S(2)}, u32[]{:S(2)}) collective-permute-start(bf16[112,896]{1,0:T(8,128)(2,1)} %bitcast.106), channel_id=1, source_target_pairs={{0,4},{4,8},{8,12},{12,0},{1,5},{5,9},{9,13},{13,1},{2,6},{6,10},{... | collective-permute-start | bytes 602120 | tf_op jit(solution)/shard_map/ppermute | solution.py:159
  14.2 15.3 %collective-permute-start.7 = (bf16[112,896]{1,0:T(8,128)(2,1)}, bf16[112,896]{1,0:T(8,128)(2,1)}, u32[]{:S(2)}, u32[]{:S(2)}) collective-permute-start(bf16[112,896]{1,0:T(8,128)(2,1)} %bitcast.105), channel_id=1, source_target_pairs={{0,8},{4,12},{8,0},{12,4},{1,9},{5,13},{9,1},{13,5},{2,10},{6,14},... | collective-permute-start | bytes 602120 | tf_op jit(solution)/shard_map/ppermute | solution.py:159
  16.8 13.7 %collective-permute-start.8 = (bf16[112,896]{1,0:T(8,128)(2,1)S(1)}, bf16[112,896]{1,0:T(8,128)(2,1)S(1)}, u32[]{:S(2)}, u32[]{:S(2)}) collective-permute-start(bf16[112,896]{1,0:T(8,128)(2,1)S(1)} %bitcast.133), channel_id=1, source_target_pairs={{0,12},{4,0},{8,4},{12,8},{1,13},{5,1},{9,5},{13,9},{2,14},{6,2},{... | collective-permute-start | bytes 602120 | tf_op jit(solution)/shard_map/ppermute | solution.py:159
  30.5 19.9 %collective-permute-start.9 = (bf16[4,112,896]{2,1,0:T(8,128)(2,1)S(1)}, bf16[4,112,896]{2,1,0:T(8,128)(2,1)}, u32[]{:S(2)}, u32[]{:S(2)}) collective-permute-start(bf16[4,112,896]{2,1,0:T(8,128)(2,1)S(1)} %bitcast_dynamic-update-slice_fusion.11), channel_id=1, source_target_pairs={{0,16},{16,0},{1,17},{17,1},{2,18},{18,2},{3,19},{19,3},{4,20},{20... | collective-permute-start | bytes 2408456 | tf_op jit(solution)/shard_map/ppermute | solution.py:179
  33.1 131.4 %all-gather.9.cloned.1.call-start = ((), (), s32[]{:S(2)}) async-start(), calls=%async_computation.3 | async-start | bytes 2293760 | tf_op jit(solution)/shard_map/all_gather | solution.py:183
  51.6 36.2 %collective-permute-start.10 = (bf16[2,4,112,896]{3,2,0,1:T(8,128)(2,1)S(1)}, bf16[2,4,112,896]{3,2,0,1:T(8,128)(2,1)}, u32[]{:S(2)}, u32[]{:S(2)}) collective-permute-start(bf16[2,4,112,896]{3,2,0,1:T(8,128)(2,1)S(1)} %bitcast_dynamic-update-slice_fusion.4), channel_id=1, source_target_pairs={{0,2},{1,3},{2,0},{3,1},{4,6},{5,7},{6,4},{7,5},{8,10},{9,11},{10,... | collective-permute-start | bytes 4816904 | tf_op jit(solution)/shard_map/ppermute | solution.py:179
  90.6 45.9 %collective-permute-start.11 = (bf16[2,2,4,112,896]{4,3,1,0,2:T(8,128)(2,1)}, bf16[2,2,4,112,896]{4,3,1,0,2:T(8,128)(2,1)}, u32[]{:S(2)}, u32[]{:S(2)}) collective-permute-start(bf16[2,2,4,112,896]{4,3,1,0,2:T(8,128)(2,1)} %bitcast_dynamic-update-slice_fusion.3), channel_id=1, source_target_pairs={{0,1},{1,0},{2,3},{3,2},{4,5},{5,4},{6,7},{7,6},{8,9},{9,8},{10,11... | collective-permute-start | bytes 9633800 | tf_op jit(solution)/shard_map/ppermute | solution.py:179
  94.8 9.8 %collective-permute-start.1 = (bf16[256,256]{1,0:T(8,128)(2,1)S(1)}, bf16[256,256]{1,0:T(8,128)(2,1)S(1)}, u32[]{:S(2)}, u32[]{:S(2)}) collective-permute-start(bf16[256,256]{1,0:T(8,128)(2,1)S(1)} %bitcast.135), channel_id=1, source_target_pairs={{0,8},{4,12},{8,0},{12,4},{1,9},{5,13},{9,1},{13,5},{2,10},{6,14},... | collective-permute-start | bytes 393224 | tf_op jit(solution)/shard_map/ppermute | solution.py:159
  95.6 9.0 %collective-permute-start.2 = (bf16[256,256]{1,0:T(8,128)(2,1)S(1)}, bf16[256,256]{1,0:T(8,128)(2,1)S(1)}, u32[]{:S(2)}, u32[]{:S(2)}) collective-permute-start(bf16[256,256]{1,0:T(8,128)(2,1)S(1)} %bitcast.134), channel_id=1, source_target_pairs={{0,12},{4,0},{8,4},{12,8},{1,13},{5,1},{9,5},{13,9},{2,14},{6,2},{... | collective-permute-start | bytes 393224 | tf_op jit(solution)/shard_map/ppermute | solution.py:159
  97.4 208.7 %all-gather.15.cloned.1.call-start = ((), (), s32[]{:S(2)}) async-start(), calls=%async_computation.7 | async-start | bytes 2293760 | tf_op jit(solution)/shard_map/all_gather | solution.py:214
  104.7 13.3 %collective-permute-start.3 = (bf16[1024,256]{1,0:T(8,128)(2,1)S(1)}, bf16[1024,256]{1,0:T(8,128)(2,1)S(1)}, u32[]{:S(2)}, u32[]{:S(2)}) collective-permute-start(bf16[1024,256]{1,0:T(8,128)(2,1)S(1)} %bitcast.115), channel_id=1, source_target_pairs={{0,1},{1,2},{2,3},{3,0},{4,5},{5,6},{6,7},{7,4},{8,9},{9,10},{10,1... | collective-permute-start | bytes 1572872 | tf_op jit(solution)/shard_map/ppermute | solution.py:159
  105.0 14.9 %collective-permute-start.4 = (bf16[1024,256]{1,0:T(8,128)(2,1)S(1)}, bf16[1024,256]{1,0:T(8,128)(2,1)S(1)}, u32[]{:S(2)}, u32[]{:S(2)}) collective-permute-start(bf16[1024,256]{1,0:T(8,128)(2,1)S(1)} %bitcast.116), channel_id=1, source_target_pairs={{0,2},{1,3},{2,0},{3,1},{4,6},{5,7},{6,4},{7,5},{8,10},{9,11},{10,... | collective-permute-start | bytes 1572872 | tf_op jit(solution)/shard_map/ppermute | solution.py:159
  107.8 21.4 %collective-permute-start.5 = (bf16[1024,256]{1,0:T(8,128)(2,1)S(1)}, bf16[1024,256]{1,0:T(8,128)(2,1)S(1)}, u32[]{:S(2)}, u32[]{:S(2)}) collective-permute-start(bf16[1024,256]{1,0:T(8,128)(2,1)S(1)} %bitcast.117), channel_id=1, source_target_pairs={{0,3},{1,0},{2,1},{3,2},{4,7},{5,4},{6,5},{7,6},{8,11},{9,8},{10,9... | collective-permute-start | bytes 1572872 | tf_op jit(solution)/shard_map/ppermute | solution.py:159
  146.9 9.6 %collective-permute-start.12 = (bf16[256,256]{0,1:T(8,128)(2,1)}, bf16[256,256]{0,1:T(8,128)(2,1)S(1)}, u32[]{:S(2)}, u32[]{:S(2)}) collective-permute-start(bf16[256,256]{0,1:T(8,128)(2,1)} %get-tuple-element.41), channel_id=1, source_target_pairs={{0,1},{1,2},{2,3},{3,0},{4,5},{5,6},{6,7},{7,4},{8,9},{9,10},{10,1... | collective-permute-start | bytes 393224 | tf_op jit(solution)/shard_map/ppermute | solution.py:159
  148.1 10.1 %collective-permute-start.13 = (bf16[256,256]{0,1:T(8,128)(2,1)}, bf16[256,256]{0,1:T(8,128)(2,1)S(1)}, u32[]{:S(2)}, u32[]{:S(2)}) collective-permute-start(bf16[256,256]{0,1:T(8,128)(2,1)} %get-tuple-element.41), channel_id=1, source_target_pairs={{0,2},{1,3},{2,0},{3,1},{4,6},{5,7},{6,4},{7,5},{8,10},{9,11},{10,... | collective-permute-start | bytes 393224 | tf_op jit(solution)/shard_map/ppermute | solution.py:159
  149.6 10.3 %collective-permute-start.14 = (bf16[256,256]{0,1:T(8,128)(2,1)}, bf16[256,256]{0,1:T(8,128)(2,1)}, u32[]{:S(2)}, u32[]{:S(2)}) collective-permute-start(bf16[256,256]{0,1:T(8,128)(2,1)} %get-tuple-element.41), channel_id=1, source_target_pairs={{0,3},{1,0},{2,1},{3,2},{4,7},{5,4},{6,5},{7,6},{8,11},{9,8},{10,9... | collective-permute-start | bytes 393224 | tf_op jit(solution)/shard_map/ppermute | solution.py:159
  177.1 9.2 %collective-permute-start.16 = (bf16[256,256]{0,1:T(8,128)(2,1)}, bf16[256,256]{0,1:T(8,128)(2,1)}, u32[]{:S(2)}, u32[]{:S(2)}) collective-permute-start(bf16[256,256]{0,1:T(8,128)(2,1)} %get-tuple-element.39), channel_id=1, source_target_pairs={{0,2},{1,3},{2,0},{3,1},{4,6},{5,7},{6,4},{7,5},{8,10},{9,11},{10,... | collective-permute-start | bytes 393224 | tf_op jit(solution)/shard_map/ppermute | solution.py:159
  177.9 9.4 %collective-permute-start.17 = (bf16[256,256]{0,1:T(8,128)(2,1)}, bf16[256,256]{0,1:T(8,128)(2,1)}, u32[]{:S(2)}, u32[]{:S(2)}) collective-permute-start(bf16[256,256]{0,1:T(8,128)(2,1)} %get-tuple-element.39), channel_id=1, source_target_pairs={{0,3},{1,0},{2,1},{3,2},{4,7},{5,4},{6,5},{7,6},{8,11},{9,8},{10,9... | collective-permute-start | bytes 393224 | tf_op jit(solution)/shard_map/ppermute | solution.py:159
  234.3 113.5 %all-gather.11.cloned.1.call-start = ((), (), s32[]{:S(2)}) async-start(), calls=%async_computation.4 | async-start | bytes 2293760 | tf_op jit(solution)/shard_map/all_gather | solution.py:214
  234.9 154.6 %all-gather.17.cloned.1.call-start = ((), (), s32[]{:S(2)}) async-start(), calls=%async_computation.8 | async-start | bytes 2293760 | tf_op jit(solution)/shard_map/all_gather | solution.py:217
  312.5 129.2 %all-gather.13.cloned.1.call-start = ((), (), s32[]{:S(2)}) async-start(), calls=%async_computation.5 | async-start | bytes 2293760 | tf_op jit(solution)/shard_map/all_gather | solution.py:217
  354.1 154.8 %reduce-scatter.5.cloned.1.call-start = ((), (), s32[]{:S(2)}) async-start(), calls=%async_computation.9 | async-start | bytes 4587520 | tf_op jit(solution)/shard_map/reduce_scatter | solution.py:223
  441.4 138.6 %reduce-scatter.3.cloned.1.call-start = ((), (), s32[]{:S(2)}) async-start(), calls=%async_computation.6 | async-start | bytes 4587520 | tf_op jit(solution)/shard_map/reduce_scatter | solution.py:223
  (21 other events, 511.1 us)
Sparse Core Ops, SparseCore 0:
  33.2 43.8 all-gather.6
  97.5 40.9 all-gather.8
  234.4 71.6 all-gather.14
  307.6 40.1 all-gather.10
  349.3 40.1 all-gather.16
  391.0 40.1 all-gather.12
  441.6 67.2 reduce-scatter.4
  511.2 68.8 reduce-scatter.2

commit v2 on v1

--- a/solution.py
+++ b/solution.py
@@ -116,9 +116,9 @@
     o_ref[...] = (acc_ref[...] / l_ref[...]).T.astype(jnp.bfloat16)
 
 
-def attention(cache_len, queries, cache_kv, low_kv, high_kv, is_low):
-    rows, width = queries.shape
-    heads = width // HEAD_DIM
+def attention(cache_len, queries, cache_kv, low_kv, high_kv, is_low, head0, heads):
+    rows = queries.shape[0]
+    width = heads * HEAD_DIM
 
     def column(array, index):
         return pl.BlockSpec((array.shape[0], HEAD_DIM), lambda g: (0, index))
@@ -128,7 +128,7 @@
         functools.partial(attn_kernel, is_low),
         grid=(heads,),
         out_shape=jax.ShapeDtypeStruct((rows, width), jnp.bfloat16),
-        in_specs=[pl.BlockSpec(memory_space=pltpu.SMEM), pl.BlockSpec((rows, HEAD_DIM), lambda g: (0, g))]
+        in_specs=[pl.BlockSpec(memory_space=pltpu.SMEM), pl.BlockSpec((rows, HEAD_DIM), lambda g: (0, g + head0))]
         + [column(a, i) for a in arrays for i in range(2)],
         out_specs=pl.BlockSpec((rows, HEAD_DIM), lambda g: (0, g)),
         scratch_shapes=[pltpu.VMEM((HEAD_DIM, sum(a.shape[0] for a in arrays)), jnp.bfloat16)] + [pltpu.VMEM((1, rows), jnp.float32)] * 2 + [pltpu.VMEM((HEAD_DIM, rows), jnp.float32)],
@@ -143,7 +143,7 @@
     column_spec = P(None, 'tp')
     row_spec = P('tp', None)
 
-    def device_layer(hidden_loc, pos_loc, cache_len, cache_k, cache_v, norm1_gain, w_query, w_key, w_value, w_out, norm2_gain, w_gate, w_up, w_down):
+    def layer(hidden_loc, pos_loc, cache_len, cache_k, cache_v, norm1_gain, w_query, w_key, w_value, w_out, norm2_gain, w_gate, w_up, w_down):
         _, d_model = hidden_loc.shape
         dp, tp, cp = lax.axis_index('dp'), lax.axis_index('tp'), lax.axis_index('cp')
         inv_freq = 1.0 / (ROPE_BASE ** (jnp.arange(HEAD_DIM // 2, dtype=jnp.float32) * (2.0 / HEAD_DIM)))
@@ -165,22 +165,25 @@
             pieces = [lax.dynamic_index_in_dim(block, (tp + shift) % tp_size, split_axis, keepdims=False) for shift in range(tp_size)]
             return place([shifted(piece, 'tp', tp_size, shift) for shift, piece in enumerate(pieces)], tp)
 
+        gathered = []
+        for i in range(2):
+            gathered.append(lax.all_gather(hidden_loc[i * RUN:(i + 1) * RUN], 'tp', axis=0, tiled=True))
+
         slots = cache_k.shape[0]
         cache_kv = jnp.stack([cache_k.reshape(slots, tp_size, HEAD_DIM), cache_v.reshape(slots, tp_size, HEAD_DIM)], axis=2)
         cache_kv = jnp.transpose(cache_kv.reshape(slots, tp_size, 2 * HEAD_DIM), (1, 0, 2))
-        cache_kv = share(exchange(cache_kv, 0).reshape(tp_size * slots, 2 * HEAD_DIM))
-
-        core, row_y = cp % 2, cp // 2
-        column_width = d_model // tp_size
-        piece_rows = w_out.shape[0] // (dp_size * cp_size)
-        piece = lax.dynamic_slice_in_dim(w_out, (core * 4 + row_y * 2 + dp) * piece_rows, piece_rows, 0)
-        columns = exchange(piece.reshape(piece_rows, tp_size, column_width), 1)
-        for axis_name, size, flip, me in (('dp', dp_size, 1, dp), ('cp', cp_size, 2, row_y), ('cp', cp_size, 1, core)):
-            columns = place([columns, lax.ppermute(columns, axis_name, [(i, i ^ flip) for i in range(size)])], me)
-        columns = jnp.transpose(columns.reshape(dp_size * cp_size, tp_size, piece_rows, column_width), (1, 0, 2, 3))
-        w_out_columns = columns.reshape(-1, column_width)
-
-        gathered = [lax.all_gather(hidden_loc[i * RUN:(i + 1) * RUN], 'tp', axis=0, tiled=True) for i in range(2)]
+        cache_kv = exchange(cache_kv, 0).reshape(tp_size * slots, 2 * HEAD_DIM)
+        cache_kv = share(cache_kv)
+
+        column_width = d_model // cp_size
+
+        def flipped(part, flip, axis_name='cp', size=cp_size):
+            return part if flip == 0 else lax.ppermute(part, axis_name, [(i, i ^ flip) for i in range(size)])
+
+        def columns_of(array, flip):
+            return lax.dynamic_slice_in_dim(array, (cp ^ flip) * column_width, column_width, 1)
+
+        residual_columns = [flipped(columns_of(hidden_loc, flip), flip) for flip in range(cp_size)]
 
         def project(index, rows_in):
             rows_in = rms_norm(rows_in, norm1_gain)
@@ -198,31 +201,61 @@
             values = jnp.dot(rows_in, w_value, preferred_element_type=jnp.float32).astype(jnp.bfloat16)
             return rotated(w_query), jnp.concatenate([rotated(w_key), values], axis=1)
 
-        gathered[0], cache_kv, w_out_columns = lax.optimization_barrier((gathered[0], cache_kv, w_out_columns))
+        gathered[0], cache_kv = lax.optimization_barrier((gathered[0], cache_kv))
         q_low, low_kv = project(0, gathered[0])
         low_kv = share(low_kv)
-        gathered[1], q_low, low_kv = lax.optimization_barrier((gathered[1], q_low, low_kv))
+        gathered[1], q_low, low_kv, residual_columns = lax.optimization_barrier((gathered[1], q_low, low_kv, residual_columns))
         q_high, high_kv = project(1, gathered[1])
         high_kv = share(high_kv)
 
-        attended = [attention(cache_len, q_low, cache_kv, low_kv, high_kv, True)]
-        q_high, attended[0] = lax.optimization_barrier((q_high, attended[0]))
-        attended.append(attention(cache_len, q_high, cache_kv, low_kv, high_kv, False))
-        column0 = tp * column_width
+        w_out_local = columns_of(w_out, 0)
+        half_rows = w_out.shape[0] // dp_size
+        w_half = lax.dynamic_slice_in_dim(w_out_local, dp * half_rows, half_rows, 0)
+        w_half, high_kv, q_high = lax.optimization_barrier((w_half, high_kv, q_high))
+        w_halves = [shifted(w_half, 'tp', tp_size, shift) for shift in range(1, tp_size)]
+        low_out = attention(cache_len, q_low, cache_kv, low_kv, high_kv, True, 0, 7)
+
+        def to_owner(out):
+            blocks = out.reshape(tp_size, RUN, out.shape[1])
+            return [shifted(lax.dynamic_index_in_dim(blocks, (tp + shift) % tp_size, 0, keepdims=False), 'tp', tp_size, shift) for shift in range(tp_size)]
+
+        low_parts = to_owner(low_out)
+        q_high, low_out, w_halves = lax.optimization_barrier((q_high, low_out, w_halves))
+        w_others = [flipped(w, 1, 'dp', dp_size) for w in w_halves]
+        high_a = attention(cache_len, q_high, cache_kv, low_kv, high_kv, False, 0, 4)
+        high_parts_a = to_owner(high_a)
+
+        def spread(parts):
+            block = jnp.stack(parts)
+            across = flipped(block, 2)
+            return [block, flipped(block, 1), across, flipped(across, 1)]
+
+        low_parts, q_high = lax.optimization_barrier((low_parts, q_high))
+        low_rows = spread(low_parts)
+        high_b = attention(cache_len, q_high, cache_kv, low_kv, high_kv, False, 4, 3)
+        high_parts_b = to_owner(high_b)
+        high_parts = [jnp.concatenate(pair, axis=1) for pair in zip(high_parts_a, high_parts_b)]
+        high_rows = spread(high_parts)
+        w_all = [w_out_local] + [jnp.where(dp == 0, jnp.concatenate([w, o], axis=0), jnp.concatenate([o, w], axis=0)) for w, o in zip(w_halves, w_others)]
+
         outs = []
-        for index in range(2):
-            heads_all = lax.all_gather(attended[index], 'tp', axis=1, tiled=True)
-            residual = lax.dynamic_slice_in_dim(gathered[index], column0, column_width, 1).astype(jnp.float32)
-            mid = (residual + jnp.dot(heads_all, w_out_columns, preferred_element_type=jnp.float32)).astype(jnp.bfloat16)
-            mid = lax.all_gather(mid, 'tp', axis=1, tiled=True)
-            group_mid = rms_norm(mid, norm2_gain)
+        for index, spread_rows in enumerate((low_rows, high_rows)):
+            rows = slice(index * RUN, (index + 1) * RUN)
+            rows_in = jnp.concatenate(spread_rows, axis=1)
+            attn_out = sum(jnp.dot(rows_in[shift], w_all[shift], preferred_element_type=jnp.float32) for shift in range(tp_size))
+            mid_columns = (jnp.concatenate([r[rows] for r in residual_columns], axis=0).astype(jnp.float32) + attn_out).astype(jnp.bfloat16)
+            mid = jnp.zeros((RUN, cp_size, column_width), jnp.bfloat16)
+            for flip in range(cp_size):
+                part = flipped(mid_columns[flip * RUN:(flip + 1) * RUN], flip)
+                mid = lax.dynamic_update_slice_in_dim(mid, part[:, None, :], cp ^ flip, 1)
+            mid = mid.reshape(RUN, d_model)
+            group_mid = lax.all_gather(rms_norm(mid, norm2_gain), 'tp', axis=0, tiled=True)
             gate_proj = jnp.dot(group_mid, w_gate, preferred_element_type=jnp.float32)
             up_proj = jnp.dot(group_mid, w_up, preferred_element_type=jnp.float32)
             hidden_mlp = (jax.nn.silu(gate_proj) * up_proj).astype(jnp.bfloat16)
             mlp_part = jnp.dot(hidden_mlp, w_down, preferred_element_type=jnp.float32)
             summed = lax.psum_scatter(mlp_part, 'tp', scatter_dimension=0, tiled=True)
-            mine = lax.dynamic_slice_in_dim(mid, tp * RUN, RUN, 0)
-            outs.append((mine.astype(jnp.float32) + summed).astype(jnp.bfloat16))
+            outs.append((mid.astype(jnp.float32) + summed).astype(jnp.bfloat16))
         return jnp.concatenate(outs, axis=0)
 
-    return jax.shard_map(device_layer, mesh=mesh, in_specs=(token_spec, P(('dp', 'cp', 'tp')), P('dp'), token_spec, token_spec, P(), column_spec, column_spec, column_spec, row_spec, P(), column_spec, column_spec, row_spec), out_specs=token_spec, check_vma=False)
+    return jax.shard_map(layer, mesh=mesh, in_specs=(token_spec, P(('dp', 'cp', 'tp')), P('dp'), token_spec, token_spec, P(), column_spec, column_spec, column_spec, row_spec, P(), column_spec, column_spec, row_spec), out_specs=token_spec, check_vma=False)

time: 598 us -> 578 us (0.967)
  starting transfers between devices: 26.6 us -> 61 us
  waiting for transfers between devices: 309 us -> 276 us
  local copies, waits for them, and re-layouts: 47.1 us -> 24.5 us
    all_gather x6 -> x4, waiting for transfers between devices: 142 us -> 62.8 us  [the longest x2 40.8 us: layer(): lax.all_gather(rms_norm(mid, norm2_gain), 'tp', axis=0, tiled=True)]
    ppermute x15 -> x24, waiting for transfers between devices: 36.2 us -> 80.1 us  [shifted(): lax.ppermute(part, axis_name, [(i, (i + shift) % size) for i in range(siz...]
    ppermute x3 -> x18, starting transfers between devices: 3.15 us -> 27 us  [flipped(): lax.ppermute(part, axis_name, [(i, i ^ flip) for i in range(size)])]
    dynamic_update_slice x26 -> x16, local copies, waits for them, and re-layouts: 21.1 us -> 1.38 us  [place(): out = lax.dynamic_update_index_in_dim(out, part, (me - shift) % size, 0)]
    ppermute x15 -> x24, starting transfers between devices: 22.8 us -> 33.2 us  [shifted(): lax.ppermute(part, axis_name, [(i, (i + shift) % size) for i in range(siz...]
    pallas_call x2 -> x3, Pallas kernels: 43 us -> 45.9 us  [attention(): pl.pallas_call(functools.partial(attn_kernel, is_low), grid=(heads,), out...]
    dot_general x6 -> x12, matrix products: 113 us -> 115 us  [the longest x2 64.2 us: layer(): mlp_part = jnp.dot(hidden_mlp, w_down, preferred_element_type=jnp.float32)]
    ppermute x3 -> x18, waiting for transfers between devices: 46.1 us -> 45.7 us  [flipped(): lax.ppermute(part, axis_name, [(i, i ^ flip) for i in range(size)])]
  transfers between devices with their start and end apart: 26 -> 48, of which waited for: 14 -> 23; matrix products, arithmetic and copies ran while one was open for 29% -> 28% of each run, Pallas kernels for 0% -> 8%
where the time goes in v2:
time: 578 us; the launch traced here: 569 us
  waiting for transfers between devices  276 us (48%)
  matrix products  133 us (23%)
  starting transfers between devices  61 us (11%)
  Pallas kernels  45.9 us (8%)
  local copies, waits for them, and re-layouts  24.5 us (4%)
  between operations  15.6 us (3%)
  other arithmetic  12.9 us (2%)
    reduce_scatter x2, waiting for transfers between devices, layer(): summed = lax.psum_scatter(mlp_part, 'tp', scatter_dimension=0, tiled=True)  86.4 us
    ppermute x24, waiting for transfers between devices, shifted(): lax.ppermute(part, axis_name, [(i, (i + shift) % size) for i in range(siz...  80.1 us
    dot_general x2, matrix products, layer(): mlp_part = jnp.dot(hidden_mlp, w_down, preferred_element_type=jnp.float32)  64.2 us
    pallas_call x3, Pallas kernels, attention(): pl.pallas_call(functools.partial(attn_kernel, is_low), grid=(heads,), out...  45.9 us
    ppermute x18, waiting for transfers between devices, flipped(): lax.ppermute(part, axis_name, [(i, i ^ flip) for i in range(size)])  45.7 us
    all_gather x2, waiting for transfers between devices, layer(): lax.all_gather(rms_norm(mid, norm2_gain), 'tp', axis=0, tiled=True)  40.8 us
    dot_general x2, matrix products, layer(): gate_proj = jnp.dot(group_mid, w_gate, preferred_element_type=jnp.float32)  36.3 us
    ppermute x24, starting transfers between devices, shifted(): lax.ppermute(part, axis_name, [(i, (i + shift) % size) for i in range(siz...  33.2 us
  transfers between devices with their start and end apart: 48, of which 23 were waited for; matrix products, arithmetic and copies ran while one was open for 28% of the time, Pallas kernels for 8%

profile of v2, /device:TPU:0, one launch (start us, length us, event | category | flops | bytes accessed | tf_op | source)
XLA Modules:
  0.0 568.8 jit_solution(9472028044965889753)
XLA Ops:
  22.4 8.1 %collective-permute-done.1 = bf16[256,256]{1,0:T(8,128)(2,1)S(1)} collective-permute-done((bf16[256,256]{1,0:T(8,128)(2,1)S(1)}, bf16[256,256]{1,0:T(8,128)(2,1)S(1)}, u32[]{:S(2)}, u32[]{:S(2)}) %collective-permute-start.1) | collective-permute-done | bytes 131104 | tf_op jit(solution)/shard_map/ppermute | solution.py:159
  37.7 3.7 collective-permute-done.3
  42.5 5.8 %collective-permute-done.4 = bf16[1024,256]{1,0:T(8,128)(2,1)S(1)} collective-permute-done((bf16[1024,256]{1,0:T(8,128)(2,1)S(1)}, bf16[1024,256]{1,0:T(8,128)(2,1)S(1)}, u32[]{:S(2)}, u32[]{:S(2)}) %collective-permute-start.4) | collective-permute-done | bytes 524320 | tf_op jit(solution)/shard_map/ppermute | solution.py:159
  48.3 6.7 %collective-permute-done.5 = bf16[1024,256]{1,0:T(8,128)(2,1)S(1)} collective-permute-done((bf16[1024,256]{1,0:T(8,128)(2,1)S(1)}, bf16[1024,256]{1,0:T(8,128)(2,1)S(1)}, u32[]{:S(2)}, u32[]{:S(2)}) %collective-permute-start.5) | collective-permute-done | bytes 524320 | tf_op jit(solution)/shard_map/ppermute | solution.py:159
  67.4 6.2 %fusion.105 = f32[256,896]{0,1:T(8,128)S(1)} fusion(bf16[3584,896]{1,0:T(8,128)(2,1)} %param.19, bf16[256,3584]{1,0:T(8,128)(2,1)} %all-gather.7.cloned.1.call-done, f32[3584]{0:T(1024)S(1)} %convert_element_type.115, f32[256]{0:T(256)S(1)} %add_rsqrt_fusion.1), kind=kOutput, calls=%fused_computation.186 | convolution fusion | flops 1647837184 | bytes 9190400 | tf_op jit(solution)/shard_map/dot_general | solution.py:198
  75.2 6.7 %collective-permute-done.11 = bf16[128,896]{1,0:T(8,128)(2,1)S(1)} collective-permute-done((bf16[128,896]{1,0:T(8,128)(2,1)S(1)}, bf16[128,896]{1,0:T(8,128)(2,1)S(1)}, u32[]{:S(2)}, u32[]{:S(2)}) %collective-permute-start.11) | collective-permute-done | bytes 229408 | tf_op jit(solution)/shard_map/ppermute | solution.py:181
  81.9 18.8 %all-gather.5.cloned.1.call-done = bf16[256,3584]{1,0:T(8,128)(2,1)} async-done(((bf16[64,3584]{1,0:T(8,128)(2,1)}), bf16[256,3584]{1,0:T(8,128)(2,1)}) %all-gather.5.cloned.1.call-update) | async-done | bytes 1835024 | tf_op jit(solution)/shard_map/all_gather | solution.py:170
  109.6 5.6 fusion.99
  122.2 14.1 %attend.3 = bf16[256,896]{1,0:T(8,128)(2,1)} custom-call(s32[1]{0:T(128)} %copy.102.clen_ref, bf16[256,896]{1,0:T(8,128)(2,1)} %copy.63.q_ref, bf16[4096,256]{1,0:T(8,128)(2,1)} %bitcast.159, bf16[4096,256]{1,0:T(8,128)(2,1)} %bitcast.160, bf16[1024,256]{1,0:T(8,128)(2,1)} %bitcast.176, bf16[1024,256]{1,0:T(8,128)(2,1)} %bitcast.177, ...), custom_call_target="tpu_custom_call" | custom-call | flops 4227858432 | bytes 8388608 | tf_op jit(solution)/shard_map/attend/pallas_call | solution.py:127
  143.0 31.2 %collective-permute-done.19 = bf16[448,896]{1,0:T(8,128)(2,1)} collective-permute-done((bf16[448,896]{1,0:T(8,128)(2,1)S(1)}, bf16[448,896]{1,0:T(8,128)(2,1)}, u32[]{:S(2)}, u32[]{:S(2)}) %collective-permute-start.19) | collective-permute-done | bytes 802848 | tf_op jit(solution)/shard_map/ppermute | solution.py:159
  176.5 20.4 %collective-permute-done.16 = bf16[64,896]{1,0:T(8,128)(2,1)S(1)} collective-permute-done((bf16[64,896]{1,0:T(8,128)(2,1)S(1)}, bf16[64,896]{1,0:T(8,128)(2,1)S(1)}, u32[]{:S(2)}, u32[]{:S(2)}) %collective-permute-start.16) | collective-permute-done | bytes 114720 | tf_op jit(solution)/shard_map/ppermute | solution.py:159
  199.3 14.1 %attend.5 = bf16[256,384]{1,0:T(8,128)(2,1)} custom-call(s32[1]{0:T(128)} %copy.102.clen_ref, bf16[256,896]{1,0:T(8,128)(2,1)} %copy.69.q_ref, bf16[4096,256]{1,0:T(8,128)(2,1)} %bitcast.161, bf16[4096,256]{1,0:T(8,128)(2,1)} %bitcast.162, bf16[1024,256]{1,0:T(8,128)(2,1)} %bitcast.178, bf16[1024,256]{1,0:T(8,128)(2,1)} %bitcast.179, ...), custom_call_target="tpu_custom_call" | custom-call | flops 1811939328 | bytes 8388608 | tf_op jit(solution)/shard_map/attend/pallas_call | solution.py:127
  216.9 17.8 %attend.4 = bf16[256,512]{1,0:T(8,128)(2,1)} custom-call(s32[1]{0:T(128)} %copy.102.clen_ref, bf16[256,896]{1,0:T(8,128)(2,1)} %copy.68.q_ref, bf16[4096,256]{1,0:T(8,128)(2,1)} %bitcast.163, bf16[4096,256]{1,0:T(8,128)(2,1)} %bitcast.164, bf16[1024,256]{1,0:T(8,128)(2,1)} %bitcast.180, bf16[1024,256]{1,0:T(8,128)(2,1)} %bitcast.181, ...), custom_call_target="tpu_custom_call" | custom-call | flops 2415919104 | bytes 8388608 | tf_op jit(solution)/shard_map/attend/pallas_call | solution.py:127
  244.0 15.6 %collective-permute-start.26 = (bf16[448,896]{1,0:T(8,128)(2,1)}, bf16[448,896]{1,0:T(8,128)(2,1)S(1)}, u32[]{:S(2)}, u32[]{:S(2)}) collective-permute-start(bf16[448,896]{1,0:T(8,128)(2,1)} %collective-permute-done.20), channel_id=1, source_target_pairs={{0,16},{16,0},{1,17},{17,1},{2,18},{18,2},{3,19},{19,3},{4,20},{20... | collective-permute-start | bytes 2408456 | tf_op jit(solution)/shard_map/ppermute | solution.py:181
  269.2 9.3 %collective-permute-done.26 = bf16[448,896]{1,0:T(8,128)(2,1)S(1)} collective-permute-done((bf16[448,896]{1,0:T(8,128)(2,1)}, bf16[448,896]{1,0:T(8,128)(2,1)S(1)}, u32[]{:S(2)}, u32[]{:S(2)}) %collective-permute-start.26) | collective-permute-done | bytes 802848 | tf_op jit(solution)/shard_map/ppermute | solution.py:181
  280.7 15.1 %collective-permute-done.25 = bf16[448,896]{1,0:T(8,128)(2,1)S(1)} collective-permute-done((bf16[448,896]{1,0:T(8,128)(2,1)}, bf16[448,896]{1,0:T(8,128)(2,1)S(1)}, u32[]{:S(2)}, u32[]{:S(2)}) %collective-permute-start.25) | collective-permute-done | bytes 802848 | tf_op jit(solution)/shard_map/ppermute | solution.py:181
  298.0 9.6 %collective-permute-done.24 = bf16[448,896]{1,0:T(8,128)(2,1)S(1)} collective-permute-done((bf16[448,896]{1,0:T(8,128)(2,1)}, bf16[448,896]{1,0:T(8,128)(2,1)S(1)}, u32[]{:S(2)}, u32[]{:S(2)}) %collective-permute-start.24) | collective-permute-done | bytes 802848 | tf_op jit(solution)/shard_map/ppermute | solution.py:181
  330.2 40.8 %all-gather.11.cloned.1.call-done = bf16[256,3584]{1,0:T(8,128)(2,1)} async-done(((bf16[64,3584]{1,0:T(8,128)(2,1)}), bf16[256,3584]{1,0:T(8,128)(2,1)}) %all-gather.11.cloned.1.call-update) | async-done | bytes 1835024 | tf_op jit(solution)/shard_map/all_gather | solution.py:252
  371.0 17.9 %fusion.115 = f32[256,4736]{1,0:T(8,128)} fusion(bf16[256,3584]{1,0:T(8,128)(2,1)} %all-gather.11.cloned.1.call-done, bf16[3584,4736]{1,0:T(8,128)(2,1)} %param.24), kind=kOutput, calls=%fused_computation.195 | convolution fusion | flops 8690597888 | bytes 40632320 | tf_op jit(solution)/shard_map/dot_general | solution.py:253
  388.9 32.0 %fusion.2 = f32[256,3584]{1,0:T(8,128)} fusion(bf16[4736,3584]{1,0:T(8,128)(2,1)} %param.26, bf16[256,3584]{1,0:T(8,128)(2,1)} %all-gather.11.cloned.1.call-done, bf16[3584,4736]{1,0:T(8,128)(2,1)} %param.25, f32[256,4736]{1,0:T(8,128)} %fusion.115), kind=kOutput, calls=%fused_computation.4 | convolution fusion | flops 17388470272 | bytes 78249984 | tf_op jit(solution)/shard_map/dot_general | solution.py:256
  421.2 18.4 %fusion.114 = f32[256,4736]{1,0:T(8,128)} fusion(bf16[256,3584]{1,0:T(8,128)(2,1)} %all-gather.9.cloned.1.call-done, bf16[3584,4736]{1,0:T(8,128)(2,1)} %param.24), kind=kOutput, calls=%fused_computation.194 | convolution fusion | flops 8690597888 | bytes 40632320 | tf_op jit(solution)/shard_map/dot_general | solution.py:253
  439.6 32.1 %fusion.3 = f32[256,3584]{1,0:T(8,128)} fusion(bf16[4736,3584]{1,0:T(8,128)(2,1)} %param.26, bf16[256,3584]{1,0:T(8,128)(2,1)} %all-gather.9.cloned.1.call-done, bf16[3584,4736]{1,0:T(8,128)(2,1)} %param.25, f32[256,4736]{1,0:T(8,128)} %fusion.114), kind=kOutput, calls=%fused_computation.5 | convolution fusion | flops 17388470272 | bytes 78249984 | tf_op jit(solution)/shard_map/dot_general | solution.py:256
  471.8 16.7 %reduce-scatter.5.cloned.1.call-done = f32[64,3584]{1,0:T(8,128)} async-done(((f32[256,3584]{1,0:T(8,128)}), f32[64,3584]{1,0:T(8,128)}) %reduce-scatter.5.cloned.1.call-update) | async-done | bytes 917520 | tf_op jit(solution)/shard_map/reduce_scatter | solution.py:257
  489.7 69.7 %reduce-scatter.3.cloned.1.call-done = f32[64,3584]{1,0:T(8,128)} async-done(((f32[256,3584]{1,0:T(8,128)}), f32[64,3584]{1,0:T(8,128)}) %reduce-scatter.3.cloned.1.call-update) | async-done | bytes 917520 | tf_op jit(solution)/shard_map/reduce_scatter | solution.py:257
  (258 shorter events, 117.0 us)
Async XLA Ops:
  6.5 51.7 %all-gather.7.cloned.1.call-start = ((), (), s32[]{:S(2)}) async-start(), calls=%async_computation.3 | async-start | bytes 2293760 | tf_op jit(solution)/shard_map/all_gather | solution.py:170
  8.8 91.8 %all-gather.5.cloned.1.call-start = ((), (), s32[]{:S(2)}) async-start(), calls=%async_computation.2 | async-start | bytes 2293760 | tf_op jit(solution)/shard_map/all_gather | solution.py:170
  19.8 55.4 %collective-permute-start.9 = (bf16[128,896]{1,0:T(8,128)(2,1)}, bf16[128,896]{1,0:T(8,128)(2,1)}, u32[]{:S(2)}, u32[]{:S(2)}) collective-permute-start(bf16[128,896]{1,0:T(8,128)(2,1)} %get-tuple-element.52), channel_id=1, source_target_pairs={{0,1},{1,0},{2,3},{3,2},{4,5},{5,4},{6,7},{7,6},{8,9},{9,8},{10,11... | collective-permute-start | bytes 688136 | tf_op jit(solution)/shard_map/ppermute | solution.py:181
  19.8 55.5 %collective-permute-start.10 = (bf16[128,896]{1,0:T(8,128)(2,1)}, bf16[128,896]{1,0:T(8,128)(2,1)}, u32[]{:S(2)}, u32[]{:S(2)}) collective-permute-start(bf16[128,896]{1,0:T(8,128)(2,1)} %get-tuple-element.54), channel_id=1, source_target_pairs={{0,2},{1,3},{2,0},{3,1},{4,6},{5,7},{6,4},{7,5},{8,10},{9,11},{10,... | collective-permute-start | bytes 688136 | tf_op jit(solution)/shard_map/ppermute | solution.py:181
  21.3 349.6 %all-gather.11.cloned.1.call-start = ((), (), s32[]{:S(2)}) async-start(), calls=%async_computation.6 | async-start | bytes 2293760 | tf_op jit(solution)/shard_map/all_gather | solution.py:252
  36.1 18.9 %collective-permute-start.5 = (bf16[1024,256]{1,0:T(8,128)(2,1)S(1)}, bf16[1024,256]{1,0:T(8,128)(2,1)S(1)}, u32[]{:S(2)}, u32[]{:S(2)}) collective-permute-start(bf16[1024,256]{1,0:T(8,128)(2,1)S(1)} %bitcast.189), channel_id=1, source_target_pairs={{0,3},{1,0},{2,1},{3,2},{4,7},{5,4},{6,5},{7,6},{8,11},{9,8},{10,9... | collective-permute-start | bytes 1572872 | tf_op jit(solution)/shard_map/ppermute | solution.py:159
  116.9 22.8 %collective-permute-start.18 = (bf16[448,896]{1,0:T(8,128)(2,1)S(1)}, bf16[448,896]{1,0:T(8,128)(2,1)}, u32[]{:S(2)}, u32[]{:S(2)}) collective-permute-start(bf16[448,896]{1,0:T(8,128)(2,1)S(1)} %copy-done.9), channel_id=1, source_target_pairs={{0,4},{4,8},{8,12},{12,0},{1,5},{5,9},{9,13},{13,1},{2,6},{6,10},{... | collective-permute-start | bytes 2408456 | tf_op jit(solution)/shard_map/ppermute | solution.py:159
  117.4 56.9 %collective-permute-start.19 = (bf16[448,896]{1,0:T(8,128)(2,1)S(1)}, bf16[448,896]{1,0:T(8,128)(2,1)}, u32[]{:S(2)}, u32[]{:S(2)}) collective-permute-start(bf16[448,896]{1,0:T(8,128)(2,1)S(1)} %copy-done.9), channel_id=1, source_target_pairs={{0,8},{4,12},{8,0},{12,4},{1,9},{5,13},{9,1},{13,5},{2,10},{6,14},... | collective-permute-start | bytes 2408456 | tf_op jit(solution)/shard_map/ppermute | solution.py:159
  118.8 55.4 %collective-permute-start.20 = (bf16[448,896]{1,0:T(8,128)(2,1)S(1)}, bf16[448,896]{1,0:T(8,128)(2,1)}, u32[]{:S(2)}, u32[]{:S(2)}) collective-permute-start(bf16[448,896]{1,0:T(8,128)(2,1)S(1)} %copy-done.9), channel_id=1, source_target_pairs={{0,12},{4,0},{8,4},{12,8},{1,13},{5,1},{9,5},{13,9},{2,14},{6,2},{... | collective-permute-start | bytes 2408456 | tf_op jit(solution)/shard_map/ppermute | solution.py:159
  137.3 39.2 %collective-permute-start.15 = (bf16[64,896]{1,0:T(8,128)(2,1)S(1)}, bf16[64,896]{1,0:T(8,128)(2,1)S(1)}, u32[]{:S(2)}, u32[]{:S(2)}) collective-permute-start(bf16[64,896]{1,0:T(8,128)(2,1)S(1)} %get-tuple-element.69), channel_id=1, source_target_pairs={{0,4},{4,8},{8,12},{12,0},{1,5},{5,9},{9,13},{13,1},{2,6},{6,10},{... | collective-permute-start | bytes 344072 | tf_op jit(solution)/shard_map/ppermute | solution.py:159
  137.6 59.3 %collective-permute-start.16 = (bf16[64,896]{1,0:T(8,128)(2,1)S(1)}, bf16[64,896]{1,0:T(8,128)(2,1)S(1)}, u32[]{:S(2)}, u32[]{:S(2)}) collective-permute-start(bf16[64,896]{1,0:T(8,128)(2,1)S(1)} %get-tuple-element.68), channel_id=1, source_target_pairs={{0,8},{4,12},{8,0},{12,4},{1,9},{5,13},{9,1},{13,5},{2,10},{6,14},... | collective-permute-start | bytes 344072 | tf_op jit(solution)/shard_map/ppermute | solution.py:159
  139.7 57.1 %collective-permute-start.17 = (bf16[64,896]{1,0:T(8,128)(2,1)S(1)}, bf16[64,896]{1,0:T(8,128)(2,1)S(1)}, u32[]{:S(2)}, u32[]{:S(2)}) collective-permute-start(bf16[64,896]{1,0:T(8,128)(2,1)S(1)} %get-tuple-element.67), channel_id=1, source_target_pairs={{0,12},{4,0},{8,4},{12,8},{1,13},{5,1},{9,5},{13,9},{2,14},{6,2},{... | collective-permute-start | bytes 344072 | tf_op jit(solution)/shard_map/ppermute | solution.py:159
  196.9 62.8 %collective-permute-start.22 = (bf16[4,64,896]{2,1,0:T(8,128)(2,1)S(1)}, bf16[4,64,896]{2,1,0:T(8,128)(2,1)S(1)}, u32[]{:S(2)}, u32[]{:S(2)}) collective-permute-start(bf16[4,64,896]{2,1,0:T(8,128)(2,1)S(1)} %pad_maximum_fusion.6), channel_id=1, source_target_pairs={{0,2},{1,3},{2,0},{3,1},{4,6},{5,7},{6,4},{7,5},{8,10},{9,11},{10,... | collective-permute-start | bytes 1376264 | tf_op jit(solution)/shard_map/ppermute | solution.py:181
  198.3 66.2 %collective-permute-start.21 = (bf16[4,64,896]{2,1,0:T(8,128)(2,1)S(1)}, bf16[4,64,896]{2,1,0:T(8,128)(2,1)S(1)}, u32[]{:S(2)}, u32[]{:S(2)}) collective-permute-start(bf16[4,64,896]{2,1,0:T(8,128)(2,1)S(1)} %pad_maximum_fusion.6), channel_id=1, source_target_pairs={{0,1},{1,0},{2,3},{3,2},{4,5},{5,4},{6,7},{7,6},{8,9},{9,8},{10,11... | collective-permute-start | bytes 1376264 | tf_op jit(solution)/shard_map/ppermute | solution.py:181
  214.2 22.5 %collective-permute-start.35 = (bf16[64,384]{1,0:T(8,128)(2,1)S(1)}, bf16[64,384]{1,0:T(8,128)(2,1)S(1)}, u32[]{:S(2)}, u32[]{:S(2)}) collective-permute-start(bf16[64,384]{1,0:T(8,128)(2,1)S(1)} %get-tuple-element.84), channel_id=1, source_target_pairs={{0,12},{4,0},{8,4},{12,8},{1,13},{5,1},{9,5},{13,9},{2,14},{6,2},{... | collective-permute-start | bytes 147464 | tf_op jit(solution)/shard_map/ppermute | solution.py:159
  240.1 19.5 %collective-permute-start.31 = (bf16[64,384]{1,0:T(8,128)(2,1)S(1)}, bf16[64,384]{1,0:T(8,128)(2,1)S(1)}, u32[]{:S(2)}, u32[]{:S(2)}) collective-permute-start(bf16[64,384]{1,0:T(8,128)(2,1)S(1)} %get-tuple-element.86), channel_id=1, source_target_pairs={{0,4},{4,8},{8,12},{12,0},{1,5},{5,9},{9,13},{13,1},{2,6},{6,10},{... | collective-permute-start | bytes 147464 | tf_op jit(solution)/shard_map/ppermute | solution.py:159
  244.0 34.6 %collective-permute-start.26 = (bf16[448,896]{1,0:T(8,128)(2,1)}, bf16[448,896]{1,0:T(8,128)(2,1)S(1)}, u32[]{:S(2)}, u32[]{:S(2)}) collective-permute-start(bf16[448,896]{1,0:T(8,128)(2,1)} %collective-permute-done.20), channel_id=1, source_target_pairs={{0,16},{16,0},{1,17},{17,1},{2,18},{18,2},{3,19},{19,3},{4,20},{20... | collective-permute-start | bytes 2408456 | tf_op jit(solution)/shard_map/ppermute | solution.py:181
  260.9 34.9 %collective-permute-start.25 = (bf16[448,896]{1,0:T(8,128)(2,1)}, bf16[448,896]{1,0:T(8,128)(2,1)S(1)}, u32[]{:S(2)}, u32[]{:S(2)}) collective-permute-start(bf16[448,896]{1,0:T(8,128)(2,1)} %collective-permute-done.19), channel_id=1, source_target_pairs={{0,16},{16,0},{1,17},{17,1},{2,18},{18,2},{3,19},{19,3},{4,20},{20... | collective-permute-start | bytes 2408456 | tf_op jit(solution)/shard_map/ppermute | solution.py:181
  264.5 43.1 %collective-permute-start.24 = (bf16[448,896]{1,0:T(8,128)(2,1)}, bf16[448,896]{1,0:T(8,128)(2,1)S(1)}, u32[]{:S(2)}, u32[]{:S(2)}) collective-permute-start(bf16[448,896]{1,0:T(8,128)(2,1)} %collective-permute-done.18), channel_id=1, source_target_pairs={{0,16},{16,0},{1,17},{17,1},{2,18},{18,2},{3,19},{19,3},{4,20},{20... | collective-permute-start | bytes 2408456 | tf_op jit(solution)/shard_map/ppermute | solution.py:181
  268.3 44.3 %collective-permute-start.36 = (bf16[4,64,896]{2,1,0:T(8,128)(2,1)S(1)}, bf16[4,64,896]{2,1,0:T(8,128)(2,1)S(1)}, u32[]{:S(2)}, u32[]{:S(2)}) collective-permute-start(bf16[4,64,896]{2,1,0:T(8,128)(2,1)S(1)} %pad_maximum_fusion.7), channel_id=1, source_target_pairs={{0,1},{1,0},{2,3},{3,2},{4,5},{5,4},{6,7},{7,6},{8,9},{9,8},{10,11... | collective-permute-start | bytes 1376264 | tf_op jit(solution)/shard_map/ppermute | solution.py:181
  268.3 44.3 %collective-permute-start.38 = (bf16[4,64,896]{2,1,0:T(8,128)(2,1)S(1)}, bf16[4,64,896]{2,1,0:T(8,128)(2,1)S(1)}, u32[]{:S(2)}, u32[]{:S(2)}) collective-permute-start(bf16[4,64,896]{2,1,0:T(8,128)(2,1)S(1)} %collective-permute-done.37), channel_id=1, source_target_pairs={{0,1},{1,0},{2,3},{3,2},{4,5},{5,4},{6,7},{7,6},{8,9},{9,8},{10,11... | collective-permute-start | bytes 1376264 | tf_op jit(solution)/shard_map/ppermute | solution.py:181
  329.2 92.0 %all-gather.9.cloned.1.call-start = ((), (), s32[]{:S(2)}) async-start(), calls=%async_computation.4 | async-start | bytes 2293760 | tf_op jit(solution)/shard_map/all_gather | solution.py:252
  329.7 158.7 %reduce-scatter.5.cloned.1.call-start = ((), (), s32[]{:S(2)}) async-start(), calls=%async_computation.7 | async-start | bytes 4587520 | tf_op jit(solution)/shard_map/reduce_scatter | solution.py:257
  420.9 138.5 %reduce-scatter.3.cloned.1.call-start = ((), (), s32[]{:S(2)}) async-start(), calls=%async_computation.5 | async-start | bytes 4587520 | tf_op jit(solution)/shard_map/reduce_scatter | solution.py:257
  (51 other events, 624.1 us)
Sparse Core Ops, SparseCore 0:
  9.0 49.2 all-gather.6
  59.8 40.8 all-gather.4
  329.3 41.6 all-gather.10
  372.4 40.1 all-gather.8
  421.1 67.3 reduce-scatter.4
  490.6 68.8 reduce-scatter.2

commit v3 on v2

--- a/solution.py
+++ b/solution.py
@@ -165,9 +165,14 @@
             pieces = [lax.dynamic_index_in_dim(block, (tp + shift) % tp_size, split_axis, keepdims=False) for shift in range(tp_size)]
             return place([shifted(piece, 'tp', tp_size, shift) for shift, piece in enumerate(pieces)], tp)
 
-        gathered = []
-        for i in range(2):
-            gathered.append(lax.all_gather(hidden_loc[i * RUN:(i + 1) * RUN], 'tp', axis=0, tiled=True))
+        def gather_rows(block, after=None):
+            parts = [shifted(block, 'tp', tp_size, shift) for shift in range(tp_size)]
+            if after is not None:
+                parts = lax.optimization_barrier((parts, after))[0]
+            return place(parts, tp).reshape(-1, d_model)
+
+        gathered = [lax.all_gather(hidden_loc[:RUN], 'tp', axis=0, tiled=True)]
+        gathered.append(gather_rows(hidden_loc[RUN:]))
 
         slots = cache_k.shape[0]
         cache_kv = jnp.stack([cache_k.reshape(slots, tp_size, HEAD_DIM), cache_v.reshape(slots, tp_size, HEAD_DIM)], axis=2)
@@ -211,7 +216,6 @@
         w_out_local = columns_of(w_out, 0)
         half_rows = w_out.shape[0] // dp_size
         w_half = lax.dynamic_slice_in_dim(w_out_local, dp * half_rows, half_rows, 0)
-        w_half, high_kv, q_high = lax.optimization_barrier((w_half, high_kv, q_high))
         w_halves = [shifted(w_half, 'tp', tp_size, shift) for shift in range(1, tp_size)]
         low_out = attention(cache_len, q_low, cache_kv, low_kv, high_kv, True, 0, 7)
 
@@ -220,7 +224,7 @@
             return [shifted(lax.dynamic_index_in_dim(blocks, (tp + shift) % tp_size, 0, keepdims=False), 'tp', tp_size, shift) for shift in range(tp_size)]
 
         low_parts = to_owner(low_out)
-        q_high, low_out, w_halves = lax.optimization_barrier((q_high, low_out, w_halves))
+        q_high, low_out = lax.optimization_barrier((q_high, low_out))
         w_others = [flipped(w, 1, 'dp', dp_size) for w in w_halves]
         high_a = attention(cache_len, q_high, cache_kv, low_kv, high_kv, False, 0, 4)
         high_parts_a = to_owner(high_a)
@@ -239,6 +243,7 @@
         w_all = [w_out_local] + [jnp.where(dp == 0, jnp.concatenate([w, o], axis=0), jnp.concatenate([o, w], axis=0)) for w, o in zip(w_halves, w_others)]
 
         outs = []
+        group_mid = None
         for index, spread_rows in enumerate((low_rows, high_rows)):
             rows = slice(index * RUN, (index + 1) * RUN)
             rows_in = jnp.concatenate(spread_rows, axis=1)
@@ -249,13 +254,15 @@
                 part = flipped(mid_columns[flip * RUN:(flip + 1) * RUN], flip)
                 mid = lax.dynamic_update_slice_in_dim(mid, part[:, None, :], cp ^ flip, 1)
             mid = mid.reshape(RUN, d_model)
-            group_mid = lax.all_gather(rms_norm(mid, norm2_gain), 'tp', axis=0, tiled=True)
-            gate_proj = jnp.dot(group_mid, w_gate, preferred_element_type=jnp.float32)
-            up_proj = jnp.dot(group_mid, w_up, preferred_element_type=jnp.float32)
-            hidden_mlp = (jax.nn.silu(gate_proj) * up_proj).astype(jnp.bfloat16)
-            mlp_part = jnp.dot(hidden_mlp, w_down, preferred_element_type=jnp.float32)
-            summed = lax.psum_scatter(mlp_part, 'tp', scatter_dimension=0, tiled=True)
-            outs.append((mid.astype(jnp.float32) + summed).astype(jnp.bfloat16))
+            normed_mid = rms_norm(mid, norm2_gain)
+            for start, count in (((0, RUN // 2), (RUN // 2, RUN // 2)), ((0, RUN),))[index]:
+                group_mid = gather_rows(normed_mid[start:start + count], group_mid)
+                gate_proj = jnp.dot(group_mid, w_gate, preferred_element_type=jnp.float32)
+                up_proj = jnp.dot(group_mid, w_up, preferred_element_type=jnp.float32)
+                hidden_mlp = (jax.nn.silu(gate_proj) * up_proj).astype(jnp.bfloat16)
+                mlp_part = jnp.dot(hidden_mlp, w_down, preferred_element_type=jnp.float32)
+                summed = lax.psum_scatter(mlp_part, 'tp', scatter_dimension=0, tiled=True)
+                outs.append((mid[start:start + count].astype(jnp.float32) + summed).astype(jnp.bfloat16))
         return jnp.concatenate(outs, axis=0)
 
     return jax.shard_map(layer, mesh=mesh, in_specs=(token_spec, P(('dp', 'cp', 'tp')), P('dp'), token_spec, token_spec, P(), column_spec, column_spec, column_spec, row_spec, P(), column_spec, column_spec, row_spec), out_specs=token_spec, check_vma=False)

time: 578 us -> 651 us (1.13)
  starting transfers between devices: 61 us -> 102 us
  matrix products: 133 us -> 167 us
  waiting for transfers between devices: 276 us -> 260 us
  local copies, waits for them, and re-layouts: 24.5 us -> 39.9 us
    ppermute x24 -> x36, waiting for transfers between devices: 80.1 us -> 144 us  [shifted(): lax.ppermute(part, axis_name, [(i, (i + shift) % size) for i in range(siz...]
    all_gather x4 -> x1, waiting for transfers between devices: 62.8 us -> 0.02 us  [layer(): gathered = [lax.all_gather(hidden_loc[:RUN], 'tp', axis=0, tiled=True)]]
    ppermute x24 -> x36, starting transfers between devices: 33.2 us -> 61 us  [shifted(): lax.ppermute(part, axis_name, [(i, (i + shift) % size) for i in range(siz...]
    dot_general x2 -> x3, matrix products: 64.2 us -> 84.9 us  [layer(): mlp_part = jnp.dot(hidden_mlp, w_down, preferred_element_type=jnp.float32)]
    reduce_scatter x2 -> x3, waiting for transfers between devices: 86.4 us -> 67 us  [layer(): summed = lax.psum_scatter(mlp_part, 'tp', scatter_dimension=0, tiled=True)]
    ppermute x18, starting transfers between devices: 27 us -> 40.2 us  [flipped(): lax.ppermute(part, axis_name, [(i, i ^ flip) for i in range(size)])]
    dot_general x2 -> x3, matrix products: 36.3 us -> 47.6 us  [layer(): gate_proj = jnp.dot(group_mid, w_gate, preferred_element_type=jnp.float32)]
    dynamic_update_slice x16 -> x32, local copies, waits for them, and re-layouts: 1.38 us -> 11 us  [place(): out = lax.dynamic_update_index_in_dim(out, part, (me - shift) % size, 0)]
  transfers between devices with their start and end apart: 48 -> 58, of which waited for: 23 -> 20; matrix products, arithmetic and copies ran while one was open for 28% -> 33% of each run, Pallas kernels for 8% -> 7%
where the time goes in v3:
time: 651 us; the launch traced here: 645 us
  waiting for transfers between devices  260 us (40%)
  matrix products  167 us (26%)
  starting transfers between devices  102 us (16%)
  Pallas kernels  45.9 us (7%)
  local copies, waits for them, and re-layouts  39.9 us (6%)
  other arithmetic  15.6 us (2%)
  between operations  15.6 us (2%)
    ppermute x36, waiting for transfers between devices, shifted(): lax.ppermute(part, axis_name, [(i, (i + shift) % size) for i in range(siz...  144 us
    dot_general x3, matrix products, layer(): mlp_part = jnp.dot(hidden_mlp, w_down, preferred_element_type=jnp.float32)  84.9 us
    reduce_scatter x3, waiting for transfers between devices, layer(): summed = lax.psum_scatter(mlp_part, 'tp', scatter_dimension=0, tiled=True)  67 us
    ppermute x36, starting transfers between devices, shifted(): lax.ppermute(part, axis_name, [(i, (i + shift) % size) for i in range(siz...  61 us
    ppermute x18, waiting for transfers between devices, flipped(): lax.ppermute(part, axis_name, [(i, i ^ flip) for i in range(size)])  48.6 us
    dot_general x3, matrix products, layer(): gate_proj = jnp.dot(group_mid, w_gate, preferred_element_type=jnp.float32)  47.6 us
    pallas_call x3, Pallas kernels, attention(): pl.pallas_call(functools.partial(attn_kernel, is_low), grid=(heads,), out...  45.9 us
    ppermute x18, starting transfers between devices, flipped(): lax.ppermute(part, axis_name, [(i, i ^ flip) for i in range(size)])  40.2 us
  transfers between devices with their start and end apart: 58, of which 20 were waited for; matrix products, arithmetic and copies ran while one was open for 33% of the time, Pallas kernels for 7%

profile of v3, /device:TPU:0, one launch (start us, length us, event | category | flops | bytes accessed | tf_op | source)
XLA Modules:
  0.0 644.9 jit_solution(10947737301561392895)
XLA Ops:
  26.6 41.8 %collective-permute-done.3 = bf16[256,256]{1,0:T(8,128)(2,1)S(1)} collective-permute-done((bf16[256,256]{1,0:T(8,128)(2,1)S(1)}, bf16[256,256]{1,0:T(8,128)(2,1)S(1)}, u32[]{:S(2)}, u32[]{:S(2)}) %collective-permute-start.3) | collective-permute-done | bytes 131104 | tf_op jit(solution)/shard_map/ppermute | solution.py:159
  68.5 23.7 %collective-permute-done.4 = bf16[256,256]{1,0:T(8,128)(2,1)S(1)} collective-permute-done((bf16[256,256]{1,0:T(8,128)(2,1)S(1)}, bf16[256,256]{1,0:T(8,128)(2,1)S(1)}, u32[]{:S(2)}, u32[]{:S(2)}) %collective-permute-start.4) | collective-permute-done | bytes 131104 | tf_op jit(solution)/shard_map/ppermute | solution.py:159
  116.2 7.7 %collective-permute-done.8 = bf16[1024,256]{1,0:T(8,128)(2,1)S(1)} collective-permute-done((bf16[1024,256]{1,0:T(8,128)(2,1)S(1)}, bf16[1024,256]{1,0:T(8,128)(2,1)S(1)}, u32[]{:S(2)}, u32[]{:S(2)}) %collective-permute-start.8) | collective-permute-done | bytes 524320 | tf_op jit(solution)/shard_map/ppermute | solution.py:159
  133.5 5.6 fusion.108
  164.9 6.1 fusion.102
  176.3 14.1 %attend.3 = bf16[256,896]{1,0:T(8,128)(2,1)} custom-call(s32[1]{0:T(128)} %copy.120.clen_ref, bf16[256,896]{1,0:T(8,128)(2,1)} %copy.62.q_ref, bf16[4096,256]{1,0:T(8,128)(2,1)} %bitcast.204, bf16[4096,256]{1,0:T(8,128)(2,1)} %bitcast.205, bf16[1024,256]{1,0:T(8,128)(2,1)} %bitcast.219, bf16[1024,256]{1,0:T(8,128)(2,1)} %bitcast.220, ...), custom_call_target="tpu_custom_call" | custom-call | flops 4227858432 | bytes 8388608 | tf_op jit(solution)/shard_map/attend/pallas_call | solution.py:127
  196.7 17.7 %attend.4 = bf16[256,512]{1,0:T(8,128)(2,1)} custom-call(s32[1]{0:T(128)} %copy.120.clen_ref, bf16[256,896]{1,0:T(8,128)(2,1)} %copy.68.q_ref, bf16[4096,256]{1,0:T(8,128)(2,1)} %bitcast.206, bf16[4096,256]{1,0:T(8,128)(2,1)} %bitcast.207, bf16[1024,256]{1,0:T(8,128)(2,1)} %bitcast.221, bf16[1024,256]{1,0:T(8,128)(2,1)} %bitcast.222, ...), custom_call_target="tpu_custom_call" | custom-call | flops 2415919104 | bytes 8388608 | tf_op jit(solution)/shard_map/attend/pallas_call | solution.py:127
  220.3 14.1 %attend.5 = bf16[256,384]{1,0:T(8,128)(2,1)} custom-call(s32[1]{0:T(128)} %copy.120.clen_ref, bf16[256,896]{1,0:T(8,128)(2,1)} %copy.69.q_ref, bf16[4096,256]{1,0:T(8,128)(2,1)} %bitcast.208, bf16[4096,256]{1,0:T(8,128)(2,1)} %bitcast.209, bf16[1024,256]{1,0:T(8,128)(2,1)} %bitcast.223, bf16[1024,256]{1,0:T(8,128)(2,1)} %bitcast.224, ...), custom_call_target="tpu_custom_call" | custom-call | flops 1811939328 | bytes 8388608 | tf_op jit(solution)/shard_map/attend/pallas_call | solution.py:127
  249.4 27.6 %collective-permute-start.29 = (bf16[448,896]{1,0:T(8,128)(2,1)}, bf16[448,896]{1,0:T(8,128)(2,1)S(1)}, u32[]{:S(2)}, u32[]{:S(2)}) collective-permute-start(bf16[448,896]{1,0:T(8,128)(2,1)} %collective-permute-done.28), channel_id=1, source_target_pairs={{0,16},{16,0},{1,17},{17,1},{2,18},{18,2},{3,19},{19,3},{4,20},{20... | collective-permute-start | bytes 2408456 | tf_op jit(solution)/shard_map/ppermute | solution.py:186
  280.6 9.4 %collective-permute-done.46 = bf16[4,64,896]{2,1,0:T(8,128)(2,1)S(1)} collective-permute-done((bf16[4,64,896]{2,1,0:T(8,128)(2,1)S(1)}, bf16[4,64,896]{2,1,0:T(8,128)(2,1)S(1)}, u32[]{:S(2)}, u32[]{:S(2)}) %collective-permute-start.46) | collective-permute-done | bytes 458784 | tf_op jit(solution)/shard_map/ppermute | solution.py:186
  298.0 15.1 %collective-permute-done.27 = bf16[448,896]{1,0:T(8,128)(2,1)S(1)} collective-permute-done((bf16[448,896]{1,0:T(8,128)(2,1)}, bf16[448,896]{1,0:T(8,128)(2,1)S(1)}, u32[]{:S(2)}, u32[]{:S(2)}) %collective-permute-start.27) | collective-permute-done | bytes 802848 | tf_op jit(solution)/shard_map/ppermute | solution.py:186
  315.4 10.5 %collective-permute-done.25 = bf16[448,896]{1,0:T(8,128)(2,1)S(1)} collective-permute-done((bf16[448,896]{1,0:T(8,128)(2,1)}, bf16[448,896]{1,0:T(8,128)(2,1)S(1)}, u32[]{:S(2)}, u32[]{:S(2)}) %collective-permute-start.25) | collective-permute-done | bytes 802848 | tf_op jit(solution)/shard_map/ppermute | solution.py:186
  353.6 33.6 %collective-permute-done.33 = bf16[32,3584]{1,0:T(8,128)(2,1)S(1)} collective-permute-done((bf16[32,3584]{1,0:T(8,128)(2,1)S(1)}, bf16[32,3584]{1,0:T(8,128)(2,1)S(1)}, u32[]{:S(2)}, u32[]{:S(2)}) %collective-permute-start.33) | collective-permute-done | bytes 229408 | tf_op jit(solution)/shard_map/ppermute | solution.py:159
  387.2 14.3 %collective-permute-start.34 = (bf16[32,3584]{1,0:T(8,128)(2,1)S(1)}, bf16[32,3584]{1,0:T(8,128)(2,1)S(1)}, u32[]{:S(2)}, u32[]{:S(2)}) collective-permute-start(bf16[32,3584]{1,0:T(8,128)(2,1)S(1)} %get-tuple-element.67), channel_id=1, source_target_pairs={{0,8},{4,12},{8,0},{12,4},{1,9},{5,13},{9,1},{13,5},{2,10},{6,14},... | collective-permute-start | bytes 688136 | tf_op jit(solution)/shard_map/ppermute | solution.py:159
  401.5 10.5 %collective-permute-done.34 = bf16[32,3584]{1,0:T(8,128)(2,1)S(1)} collective-permute-done((bf16[32,3584]{1,0:T(8,128)(2,1)S(1)}, bf16[32,3584]{1,0:T(8,128)(2,1)S(1)}, u32[]{:S(2)}, u32[]{:S(2)}) %collective-permute-start.34) | collective-permute-done | bytes 229408 | tf_op jit(solution)/shard_map/ppermute | solution.py:159
  412.4 6.9 %collective-permute-done.35 = bf16[32,3584]{1,0:T(8,128)(2,1)S(1)} collective-permute-done((bf16[32,3584]{1,0:T(8,128)(2,1)S(1)}, bf16[32,3584]{1,0:T(8,128)(2,1)S(1)}, u32[]{:S(2)}, u32[]{:S(2)}) %collective-permute-start.35) | collective-permute-done | bytes 229408 | tf_op jit(solution)/shard_map/ppermute | solution.py:159
  421.7 6.1 collective-permute-done.38
  428.0 14.6 %fusion.121 = f32[128,4736]{1,0:T(8,128)} fusion(bf16[128,3584]{1,0:T(8,128)(2,1)S(1)} %bitcast.229, bf16[3584,4736]{1,0:T(8,128)(2,1)} %param.24), kind=kOutput, calls=%fused_computation.220 | convolution fusion | flops 4345298944 | bytes 37289984 | tf_op jit(solution)/shard_map/dot_general | solution.py:260
  442.6 26.2 %fusion.14 = f32[128,3584]{1,0:T(8,128)} fusion(bf16[4736,3584]{1,0:T(8,128)(2,1)} %param.26, bf16[128,3584]{1,0:T(8,128)(2,1)S(1)} %bitcast.230, bf16[3584,4736]{1,0:T(8,128)(2,1)} %param.25, f32[128,4736]{1,0:T(8,128)} %fusion.121), kind=kOutput, calls=%fused_computation.20 | convolution fusion | flops 8694235136 | bytes 73072640 | tf_op jit(solution)/shard_map/dot_general | solution.py:263
  468.8 15.0 %fusion.120 = f32[128,4736]{1,0:T(8,128)} fusion(bf16[128,3584]{1,0:T(8,128)(2,1)S(1)} %bitcast.227, bf16[3584,4736]{1,0:T(8,128)(2,1)} %param.24), kind=kOutput, calls=%fused_computation.219 | convolution fusion | flops 4345298944 | bytes 37289984 | tf_op jit(solution)/shard_map/dot_general | solution.py:260
  483.8 26.6 %fusion.55 = f32[128,3584]{1,0:T(8,128)} fusion(bf16[4736,3584]{1,0:T(8,128)(2,1)} %param.26, f32[128,4736]{1,0:T(8,128)} %fusion.120, bf16[128,3584]{1,0:T(8,128)(2,1)S(1)} %bitcast.228, bf16[3584,4736]{1,0:T(8,128)(2,1)} %param.25), kind=kOutput, calls=%fused_computation.47 | convolution fusion | flops 8694235136 | bytes 73072640 | tf_op jit(solution)/shard_map/dot_general | solution.py:263
  516.3 18.0 %fusion.122 = f32[256,4736]{1,0:T(8,128)} fusion(bf16[256,3584]{1,0:T(8,128)(2,1)S(1)} %bitcast.242, bf16[3584,4736]{1,0:T(8,128)(2,1)} %param.24), kind=kOutput, calls=%fused_computation.221 | convolution fusion | flops 8690597888 | bytes 40632320 | tf_op jit(solution)/shard_map/dot_general | solution.py:260
  534.4 32.1 %fusion.2 = f32[256,3584]{1,0:T(8,128)} fusion(bf16[4736,3584]{1,0:T(8,128)(2,1)} %param.26, bf16[256,3584]{1,0:T(8,128)(2,1)} %bitcast.243, bf16[3584,4736]{1,0:T(8,128)(2,1)} %param.25, f32[256,4736]{1,0:T(8,128)} %fusion.122), kind=kOutput, calls=%fused_computation.4 | convolution fusion | flops 17388470272 | bytes 78249984 | tf_op jit(solution)/shard_map/dot_general | solution.py:263
  568.9 66.9 %reduce-scatter.8.cloned.1.call-done = f32[64,3584]{1,0:T(8,128)} async-done(((f32[256,3584]{1,0:T(8,128)}), f32[64,3584]{1,0:T(8,128)}) %reduce-scatter.8.cloned.1.call-update) | async-done | bytes 917520 | tf_op jit(solution)/shard_map/reduce_scatter | solution.py:264
  (319 shorter events, 165.1 us)
Async XLA Ops:
  6.5 117.5 %all-gather.2.cloned.1.call-start = ((), (), s32[]{:S(2)}) async-start(), calls=%async_computation.3 | async-start | bytes 2293760 | tf_op jit(solution)/shard_map/all_gather | solution.py:174
  8.8 90.7 %collective-permute-start = (bf16[64,3584]{1,0:T(8,128)(2,1)}, bf16[64,3584]{1,0:T(8,128)(2,1)}, u32[]{:S(2)}, u32[]{:S(2)}) collective-permute-start(bf16[64,3584]{1,0:T(8,128)(2,1)} %get-tuple-element.60), channel_id=1, source_target_pairs={{0,4},{4,8},{8,12},{12,0},{1,5},{5,9},{9,13},{13,1},{2,6},{6,10},{... | collective-permute-start | bytes 1376264 | tf_op jit(solution)/shard_map/ppermute | solution.py:159
  11.9 89.5 %collective-permute-start.1 = (bf16[64,3584]{1,0:T(8,128)(2,1)}, bf16[64,3584]{1,0:T(8,128)(2,1)}, u32[]{:S(2)}, u32[]{:S(2)}) collective-permute-start(bf16[64,3584]{1,0:T(8,128)(2,1)} %get-tuple-element.60), channel_id=1, source_target_pairs={{0,8},{4,12},{8,0},{12,4},{1,9},{5,13},{9,1},{13,5},{2,10},{6,14},... | collective-permute-start | bytes 1376264 | tf_op jit(solution)/shard_map/ppermute | solution.py:159
  14.5 90.2 %collective-permute-start.2 = (bf16[64,3584]{1,0:T(8,128)(2,1)}, bf16[64,3584]{1,0:T(8,128)(2,1)}, u32[]{:S(2)}, u32[]{:S(2)}) collective-permute-start(bf16[64,3584]{1,0:T(8,128)(2,1)} %get-tuple-element.60), channel_id=1, source_target_pairs={{0,12},{4,0},{8,4},{12,8},{1,13},{5,1},{9,5},{13,9},{2,14},{6,2},{... | collective-permute-start | bytes 1376264 | tf_op jit(solution)/shard_map/ppermute | solution.py:159
  15.8 550.8 %reduce-scatter.6.cloned.1.call-start = ((), (), s32[]{:S(2)}) async-start(), calls=%async_computation.5 | async-start | bytes 2293760 | tf_op jit(solution)/shard_map/reduce_scatter | solution.py:264
  16.5 51.9 %collective-permute-start.3 = (bf16[256,256]{1,0:T(8,128)(2,1)S(1)}, bf16[256,256]{1,0:T(8,128)(2,1)S(1)}, u32[]{:S(2)}, u32[]{:S(2)}) collective-permute-start(bf16[256,256]{1,0:T(8,128)(2,1)S(1)} %bitcast.262), channel_id=1, source_target_pairs={{0,4},{4,8},{8,12},{12,0},{1,5},{5,9},{9,13},{13,1},{2,6},{6,10},{... | collective-permute-start | bytes 393224 | tf_op jit(solution)/shard_map/ppermute | solution.py:159
  17.4 74.8 %collective-permute-start.4 = (bf16[256,256]{1,0:T(8,128)(2,1)S(1)}, bf16[256,256]{1,0:T(8,128)(2,1)S(1)}, u32[]{:S(2)}, u32[]{:S(2)}) collective-permute-start(bf16[256,256]{1,0:T(8,128)(2,1)S(1)} %bitcast.261), channel_id=1, source_target_pairs={{0,8},{4,12},{8,0},{12,4},{1,9},{5,13},{9,1},{13,5},{2,10},{6,14},... | collective-permute-start | bytes 393224 | tf_op jit(solution)/shard_map/ppermute | solution.py:159
  92.2 143.3 %collective-permute-start.28 = (bf16[448,896]{1,0:T(8,128)(2,1)}, bf16[448,896]{1,0:T(8,128)(2,1)}, u32[]{:S(2)}, u32[]{:S(2)}) collective-permute-start(bf16[448,896]{1,0:T(8,128)(2,1)} %dynamic_slice.74), channel_id=1, source_target_pairs={{0,12},{4,0},{8,4},{12,8},{1,13},{5,1},{9,5},{13,9},{2,14},{6,2},{... | collective-permute-start | bytes 2408456 | tf_op jit(solution)/shard_map/ppermute | solution.py:159
  96.5 180.5 %collective-permute-start.26 = (bf16[448,896]{1,0:T(8,128)(2,1)}, bf16[448,896]{1,0:T(8,128)(2,1)}, u32[]{:S(2)}, u32[]{:S(2)}) collective-permute-start(bf16[448,896]{1,0:T(8,128)(2,1)} %dynamic_slice.74), channel_id=1, source_target_pairs={{0,8},{4,12},{8,0},{12,4},{1,9},{5,13},{9,1},{13,5},{2,10},{6,14},... | collective-permute-start | bytes 2408456 | tf_op jit(solution)/shard_map/ppermute | solution.py:159
  215.5 63.0 %collective-permute-start.24 = (bf16[448,896]{1,0:T(8,128)(2,1)}, bf16[448,896]{1,0:T(8,128)(2,1)}, u32[]{:S(2)}, u32[]{:S(2)}) collective-permute-start(bf16[448,896]{1,0:T(8,128)(2,1)} %dynamic_slice.74), channel_id=1, source_target_pairs={{0,4},{4,8},{8,12},{12,0},{1,5},{5,9},{9,13},{13,1},{2,6},{6,10},{... | collective-permute-start | bytes 2408456 | tf_op jit(solution)/shard_map/ppermute | solution.py:159
  240.3 37.9 %collective-permute-start.22 = (bf16[4,64,896]{2,1,0:T(8,128)(2,1)S(1)}, bf16[4,64,896]{2,1,0:T(8,128)(2,1)S(1)}, u32[]{:S(2)}, u32[]{:S(2)}) collective-permute-start(bf16[4,64,896]{2,1,0:T(8,128)(2,1)S(1)} %pad_maximum_fusion.6), channel_id=1, source_target_pairs={{0,2},{1,3},{2,0},{3,1},{4,6},{5,7},{6,4},{7,5},{8,10},{9,11},{10,... | collective-permute-start | bytes 1376264 | tf_op jit(solution)/shard_map/ppermute | solution.py:186
  249.4 46.5 %collective-permute-start.29 = (bf16[448,896]{1,0:T(8,128)(2,1)}, bf16[448,896]{1,0:T(8,128)(2,1)S(1)}, u32[]{:S(2)}, u32[]{:S(2)}) collective-permute-start(bf16[448,896]{1,0:T(8,128)(2,1)} %collective-permute-done.28), channel_id=1, source_target_pairs={{0,16},{16,0},{1,17},{17,1},{2,18},{18,2},{3,19},{19,3},{4,20},{20... | collective-permute-start | bytes 2408456 | tf_op jit(solution)/shard_map/ppermute | solution.py:186
  278.4 34.7 %collective-permute-start.27 = (bf16[448,896]{1,0:T(8,128)(2,1)}, bf16[448,896]{1,0:T(8,128)(2,1)S(1)}, u32[]{:S(2)}, u32[]{:S(2)}) collective-permute-start(bf16[448,896]{1,0:T(8,128)(2,1)} %collective-permute-done.26), channel_id=1, source_target_pairs={{0,16},{16,0},{1,17},{17,1},{2,18},{18,2},{3,19},{19,3},{4,20},{20... | collective-permute-start | bytes 2408456 | tf_op jit(solution)/shard_map/ppermute | solution.py:186
  279.6 46.3 %collective-permute-start.25 = (bf16[448,896]{1,0:T(8,128)(2,1)}, bf16[448,896]{1,0:T(8,128)(2,1)S(1)}, u32[]{:S(2)}, u32[]{:S(2)}) collective-permute-start(bf16[448,896]{1,0:T(8,128)(2,1)} %collective-permute-done.24), channel_id=1, source_target_pairs={{0,16},{16,0},{1,17},{17,1},{2,18},{18,2},{3,19},{19,3},{4,20},{20... | collective-permute-start | bytes 2408456 | tf_op jit(solution)/shard_map/ppermute | solution.py:186
  290.1 40.8 %collective-permute-start.45 = (bf16[4,64,896]{2,1,0:T(8,128)(2,1)S(1)}, bf16[4,64,896]{2,1,0:T(8,128)(2,1)S(1)}, u32[]{:S(2)}, u32[]{:S(2)}) collective-permute-start(bf16[4,64,896]{2,1,0:T(8,128)(2,1)S(1)} %pad_maximum_fusion.7), channel_id=1, source_target_pairs={{0,1},{1,0},{2,3},{3,2},{4,5},{5,4},{6,7},{7,6},{8,9},{9,8},{10,11... | collective-permute-start | bytes 1376264 | tf_op jit(solution)/shard_map/ppermute | solution.py:186
  290.1 40.8 %collective-permute-start.47 = (bf16[4,64,896]{2,1,0:T(8,128)(2,1)S(1)}, bf16[4,64,896]{2,1,0:T(8,128)(2,1)S(1)}, u32[]{:S(2)}, u32[]{:S(2)}) collective-permute-start(bf16[4,64,896]{2,1,0:T(8,128)(2,1)S(1)} %collective-permute-done.46), channel_id=1, source_target_pairs={{0,1},{1,0},{2,3},{3,2},{4,5},{5,4},{6,7},{7,6},{8,9},{9,8},{10,11... | collective-permute-start | bytes 1376264 | tf_op jit(solution)/shard_map/ppermute | solution.py:186
  347.4 163.3 %collective-permute-start.51 = (bf16[64,3584]{1,0:T(8,128)(2,1)}, bf16[64,3584]{1,0:T(8,128)(2,1)}, u32[]{:S(2)}, u32[]{:S(2)}) collective-permute-start(bf16[64,3584]{1,0:T(8,128)(2,1)} %get-tuple-element.47), channel_id=1, source_target_pairs={{0,4},{4,8},{8,12},{12,0},{1,5},{5,9},{9,13},{13,1},{2,6},{6,10},{... | collective-permute-start | bytes 1376264 | tf_op jit(solution)/shard_map/ppermute | solution.py:159
  347.6 163.1 %collective-permute-start.52 = (bf16[64,3584]{1,0:T(8,128)(2,1)}, bf16[64,3584]{1,0:T(8,128)(2,1)}, u32[]{:S(2)}, u32[]{:S(2)}) collective-permute-start(bf16[64,3584]{1,0:T(8,128)(2,1)} %get-tuple-element.47), channel_id=1, source_target_pairs={{0,8},{4,12},{8,0},{12,4},{1,9},{5,13},{9,1},{13,5},{2,10},{6,14},... | collective-permute-start | bytes 1376264 | tf_op jit(solution)/shard_map/ppermute | solution.py:159
  349.0 72.4 %collective-permute-start.36 = (bf16[32,3584]{1,0:T(8,128)(2,1)S(1)}, bf16[32,3584]{1,0:T(8,128)(2,1)S(1)}, u32[]{:S(2)}, u32[]{:S(2)}) collective-permute-start(bf16[32,3584]{1,0:T(8,128)(2,1)S(1)} %get-tuple-element.42), channel_id=1, source_target_pairs={{0,4},{4,8},{8,12},{12,0},{1,5},{5,9},{9,13},{13,1},{2,6},{6,10},{... | collective-permute-start | bytes 688136 | tf_op jit(solution)/shard_map/ppermute | solution.py:159
  351.9 69.8 %collective-permute-start.37 = (bf16[32,3584]{1,0:T(8,128)(2,1)S(1)}, bf16[32,3584]{1,0:T(8,128)(2,1)S(1)}, u32[]{:S(2)}, u32[]{:S(2)}) collective-permute-start(bf16[32,3584]{1,0:T(8,128)(2,1)S(1)} %get-tuple-element.42), channel_id=1, source_target_pairs={{0,8},{4,12},{8,0},{12,4},{1,9},{5,13},{9,1},{13,5},{2,10},{6,14},... | collective-permute-start | bytes 688136 | tf_op jit(solution)/shard_map/ppermute | solution.py:159
  352.4 34.8 %collective-permute-start.33 = (bf16[32,3584]{1,0:T(8,128)(2,1)S(1)}, bf16[32,3584]{1,0:T(8,128)(2,1)S(1)}, u32[]{:S(2)}, u32[]{:S(2)}) collective-permute-start(bf16[32,3584]{1,0:T(8,128)(2,1)S(1)} %get-tuple-element.67), channel_id=1, source_target_pairs={{0,4},{4,8},{8,12},{12,0},{1,5},{5,9},{9,13},{13,1},{2,6},{6,10},{... | collective-permute-start | bytes 688136 | tf_op jit(solution)/shard_map/ppermute | solution.py:159
  421.4 89.3 %collective-permute-start.53 = (bf16[64,3584]{1,0:T(8,128)(2,1)}, bf16[64,3584]{1,0:T(8,128)(2,1)}, u32[]{:S(2)}, u32[]{:S(2)}) collective-permute-start(bf16[64,3584]{1,0:T(8,128)(2,1)} %get-tuple-element.47), channel_id=1, source_target_pairs={{0,12},{4,0},{8,4},{12,8},{1,13},{5,1},{9,5},{13,9},{2,14},{6,2},{... | collective-permute-start | bytes 1376264 | tf_op jit(solution)/shard_map/ppermute | solution.py:159
  468.8 99.0 %reduce-scatter.4.cloned.1.call-start = ((), (), s32[]{:S(2)}) async-start(), calls=%async_computation.4 | async-start | bytes 2293760 | tf_op jit(solution)/shard_map/reduce_scatter | solution.py:264
  510.4 125.4 %reduce-scatter.8.cloned.1.call-start = ((), (), s32[]{:S(2)}) async-start(), calls=%async_computation.6 | async-start | bytes 4587520 | tf_op jit(solution)/shard_map/reduce_scatter | solution.py:264
  (69 other events, 929.5 us)
Sparse Core Ops, SparseCore 0:
  16.0 67.5 all-gather.1
  468.9 40.3 reduce-scatter.5
  511.6 39.2 reduce-scatter.3
  566.6 69.2 reduce-scatter.7

commit v4 on v2

--- a/solution.py
+++ b/solution.py
@@ -12,6 +12,7 @@
 NORM_EPS = 1e-5
 RUN = 64
 KV_BLOCK = 512
+MLP_TILE = 512
 LOG2E = 1.4426950408889634
 
 
@@ -137,6 +138,47 @@
     )(cache_len, queries, *[a for a in arrays for _ in range(2)])
 
 
+def mlp_kernel(tail, rows_ref, gate_ref, up_ref, down_ref, out_ref):
+    step = pl.program_id(0)
+    last = pl.num_programs(0) - 1
+
+    @pl.when(step == 0)
+    def _():
+        out_ref[...] = jnp.zeros_like(out_ref)
+
+    def tile(width):
+        rows = rows_ref[...]
+        gate_proj = jnp.dot(rows, gate_ref[:, :width], preferred_element_type=jnp.float32)
+        up_proj = jnp.dot(rows, up_ref[:, :width], preferred_element_type=jnp.float32)
+        hidden_mlp = (jax.nn.silu(gate_proj) * up_proj).astype(jnp.bfloat16)
+        out_ref[...] += jnp.dot(hidden_mlp, down_ref[:width, :], preferred_element_type=jnp.float32)
+
+    @pl.when(step < last)
+    def _():
+        tile(gate_ref.shape[1])
+
+    @pl.when(step == last)
+    def _():
+        tile(tail)
+
+
+def gated_mlp(rows, w_gate, w_up, w_down):
+    count, d_model = rows.shape
+    width = w_gate.shape[1]
+    steps = (width + MLP_TILE - 1) // MLP_TILE
+    wide = pl.BlockSpec((d_model, MLP_TILE), lambda i: (0, i))
+    return pl.pallas_call(
+        functools.partial(mlp_kernel, width - (steps - 1) * MLP_TILE),
+        grid=(steps,),
+        out_shape=jax.ShapeDtypeStruct((count, d_model), jnp.float32),
+        in_specs=[pl.BlockSpec((count, d_model), lambda i: (0, 0)), wide, wide, pl.BlockSpec((MLP_TILE, d_model), lambda i: (i, 0))],
+        out_specs=pl.BlockSpec((count, d_model), lambda i: (0, 0)),
+        compiler_params=pltpu.CompilerParams(vmem_limit_bytes=56 * 2**20),
+        cost_estimate=pl.CostEstimate(flops=6 * count * d_model * width, bytes_accessed=6 * d_model * width, transcendentals=count * width),
+        name='gated_mlp',
+    )(rows, w_gate, w_up, w_down)
+
+
 def solution(mesh):
     tp_size, cp_size, dp_size = mesh.shape['tp'], mesh.shape['cp'], mesh.shape['dp']
     token_spec = P(('dp', 'cp', 'tp'), None)
@@ -211,7 +253,6 @@
         w_out_local = columns_of(w_out, 0)
         half_rows = w_out.shape[0] // dp_size
         w_half = lax.dynamic_slice_in_dim(w_out_local, dp * half_rows, half_rows, 0)
-        w_half, high_kv, q_high = lax.optimization_barrier((w_half, high_kv, q_high))
         w_halves = [shifted(w_half, 'tp', tp_size, shift) for shift in range(1, tp_size)]
         low_out = attention(cache_len, q_low, cache_kv, low_kv, high_kv, True, 0, 7)
 
@@ -220,7 +261,7 @@
             return [shifted(lax.dynamic_index_in_dim(blocks, (tp + shift) % tp_size, 0, keepdims=False), 'tp', tp_size, shift) for shift in range(tp_size)]
 
         low_parts = to_owner(low_out)
-        q_high, low_out, w_halves = lax.optimization_barrier((q_high, low_out, w_halves))
+        q_high, low_out = lax.optimization_barrier((q_high, low_out))
         w_others = [flipped(w, 1, 'dp', dp_size) for w in w_halves]
         high_a = attention(cache_len, q_high, cache_kv, low_kv, high_kv, False, 0, 4)
         high_parts_a = to_owner(high_a)
@@ -240,6 +281,8 @@
 
         outs = []
         for index, spread_rows in enumerate((low_rows, high_rows)):
+            if index == 1:
+                spread_rows = lax.optimization_barrier((spread_rows, normed_mid))[0]
             rows = slice(index * RUN, (index + 1) * RUN)
             rows_in = jnp.concatenate(spread_rows, axis=1)
             attn_out = sum(jnp.dot(rows_in[shift], w_all[shift], preferred_element_type=jnp.float32) for shift in range(tp_size))
@@ -249,11 +292,9 @@
                 part = flipped(mid_columns[flip * RUN:(flip + 1) * RUN], flip)
                 mid = lax.dynamic_update_slice_in_dim(mid, part[:, None, :], cp ^ flip, 1)
             mid = mid.reshape(RUN, d_model)
-            group_mid = lax.all_gather(rms_norm(mid, norm2_gain), 'tp', axis=0, tiled=True)
-            gate_proj = jnp.dot(group_mid, w_gate, preferred_element_type=jnp.float32)
-            up_proj = jnp.dot(group_mid, w_up, preferred_element_type=jnp.float32)
-            hidden_mlp = (jax.nn.silu(gate_proj) * up_proj).astype(jnp.bfloat16)
-            mlp_part = jnp.dot(hidden_mlp, w_down, preferred_element_type=jnp.float32)
+            normed_mid = rms_norm(mid, norm2_gain)
+            group_mid = lax.all_gather(normed_mid, 'tp', axis=0, tiled=True)
+            mlp_part = gated_mlp(group_mid, w_gate, w_up, w_down)
             summed = lax.psum_scatter(mlp_part, 'tp', scatter_dimension=0, tiled=True)
             outs.append((mid.astype(jnp.float32) + summed).astype(jnp.bfloat16))
         return jnp.concatenate(outs, axis=0)

time: 578 us -> 583 us (level)
  matrix products: 133 us -> 35 us
  Pallas kernels: 45.9 us -> 129 us
  waiting for transfers between devices: 276 us -> 251 us
  local copies, waits for them, and re-layouts: 24.5 us -> 48.2 us
  starting transfers between devices: 61 us -> 78.7 us
    dot_general x4 -> x0, matrix products: 101 us -> none  [the longest x2 64.2 us: layer(): mlp_part = jnp.dot(hidden_mlp, w_down, preferred_element_type=jnp.float32)]
    pallas_call x0 -> x2, Pallas kernels: none -> 83 us  [gated_mlp(): pl.pallas_call(functools.partial(mlp_kernel, width - (steps - 1) * MLP_TI...]
    all_gather x2, waiting for transfers between devices: 40.8 us -> 12.6 us  [layer(): group_mid = lax.all_gather(normed_mid, 'tp', axis=0, tiled=True)]
    ppermute x24, waiting for transfers between devices: 80.1 us -> 106 us  [shifted(): lax.ppermute(part, axis_name, [(i, (i + shift) % size) for i in range(siz...]
    all_gather x2, waiting for transfers between devices: 22 us -> 0.02 us  [layer(): lax.all_gather(hidden_loc[i * RUN:(i + 1) * RUN], 'tp', axis=0, tiled=True)]
    dynamic_update_slice x9 -> x8, local copies, waits for them, and re-layouts: 3.47 us -> 23.8 us  [layer(): mid = lax.dynamic_update_slice_in_dim(mid, part[:, None, :], cp ^ flip, 1)]
    ppermute x18, starting transfers between devices: 27 us -> 40.9 us  [flipped(): lax.ppermute(part, axis_name, [(i, i ^ flip) for i in range(size)])]
    reduce_scatter x2, waiting for transfers between devices: 86.4 us -> 97.4 us  [layer(): summed = lax.psum_scatter(mlp_part, 'tp', scatter_dimension=0, tiled=True)]
  transfers between devices with their start and end apart: 48 -> 48, of which waited for: 23 -> 19; matrix products, arithmetic and copies ran while one was open for 28% -> 16% of each run, Pallas kernels for 8% -> 22%
where the time goes in v4:
time: 583 us; the launch traced here: 573 us
  waiting for transfers between devices  251 us (43%)
  Pallas kernels  129 us (22%)
  starting transfers between devices  78.7 us (13%)
  local copies, waits for them, and re-layouts  48.2 us (8%)
  matrix products  35 us (6%)
  between operations  16 us (3%)
  other arithmetic  15.2 us (3%)
    ppermute x24, waiting for transfers between devices, shifted(): lax.ppermute(part, axis_name, [(i, (i + shift) % size) for i in range(siz...  106 us
    reduce_scatter x2, waiting for transfers between devices, layer(): summed = lax.psum_scatter(mlp_part, 'tp', scatter_dimension=0, tiled=True)  97.4 us
    pallas_call x2, Pallas kernels, gated_mlp(): pl.pallas_call(functools.partial(mlp_kernel, width - (steps - 1) * MLP_TI...  83 us
    pallas_call x3, Pallas kernels, attention(): pl.pallas_call(functools.partial(attn_kernel, is_low), grid=(heads,), out...  45.9 us
    ppermute x18, starting transfers between devices, flipped(): lax.ppermute(part, axis_name, [(i, i ^ flip) for i in range(size)])  40.9 us
    ppermute x24, starting transfers between devices, shifted(): lax.ppermute(part, axis_name, [(i, (i + shift) % size) for i in range(siz...  37 us
    ppermute x18, waiting for transfers between devices, flipped(): lax.ppermute(part, axis_name, [(i, i ^ flip) for i in range(size)])  35.5 us
    dynamic_update_slice x8, local copies, waits for them, and re-layouts, layer(): mid = lax.dynamic_update_slice_in_dim(mid, part[:, None, :], cp ^ flip, 1)  23.8 us
  transfers between devices with their start and end apart: 48, of which 19 were waited for; matrix products, arithmetic and copies ran while one was open for 16% of the time, Pallas kernels for 22%

profile of v4, /device:TPU:0, one launch (start us, length us, event | category | flops | bytes accessed | tf_op | source)
XLA Modules:
  0.0 573.4 jit_solution(3753333208349449650)
XLA Ops:
  11.5 5.1 collective-permute-start.25
  24.5 60.1 %collective-permute-done = bf16[256,256]{1,0:T(8,128)(2,1)S(1)} collective-permute-done((bf16[256,256]{1,0:T(8,128)(2,1)S(1)}, bf16[256,256]{1,0:T(8,128)(2,1)S(1)}, u32[]{:S(2)}, u32[]{:S(2)}) %collective-permute-start) | collective-permute-done | bytes 131104 | tf_op jit(solution)/shard_map/ppermute | solution.py:201
  84.6 22.7 %collective-permute-done.1 = bf16[256,256]{1,0:T(8,128)(2,1)S(1)} collective-permute-done((bf16[256,256]{1,0:T(8,128)(2,1)S(1)}, bf16[256,256]{1,0:T(8,128)(2,1)S(1)}, u32[]{:S(2)}, u32[]{:S(2)}) %collective-permute-start.1) | collective-permute-done | bytes 131104 | tf_op jit(solution)/shard_map/ppermute | solution.py:201
  113.0 7.9 %collective-permute-done.3 = bf16[1024,256]{1,0:T(8,128)(2,1)} collective-permute-done((bf16[1024,256]{1,0:T(8,128)(2,1)S(1)}, bf16[1024,256]{1,0:T(8,128)(2,1)}, u32[]{:S(2)}, u32[]{:S(2)}) %collective-permute-start.3) | collective-permute-done | bytes 524320 | tf_op jit(solution)/shard_map/ppermute | solution.py:201
  123.6 8.3 %collective-permute-done.5 = bf16[1024,256]{1,0:T(8,128)(2,1)S(1)} collective-permute-done((bf16[1024,256]{1,0:T(8,128)(2,1)S(1)}, bf16[1024,256]{1,0:T(8,128)(2,1)S(1)}, u32[]{:S(2)}, u32[]{:S(2)}) %collective-permute-start.5) | collective-permute-done | bytes 524320 | tf_op jit(solution)/shard_map/ppermute | solution.py:201
  141.9 5.5 fusion.69
  153.0 4.9 collective-permute-done.10
  157.9 3.0 collective-permute-done.11
  169.0 5.6 fusion.63
  180.7 14.1 %attend.3 = bf16[256,896]{1,0:T(8,128)(2,1)} custom-call(s32[1]{0:T(128)} %copy.111.clen_ref, bf16[256,896]{1,0:T(8,128)(2,1)} %copy.68.q_ref, bf16[4096,256]{1,0:T(8,128)(2,1)} %bitcast.141, bf16[4096,256]{1,0:T(8,128)(2,1)} %bitcast.142, bf16[1024,256]{1,0:T(8,128)(2,1)} %bitcast.157, bf16[1024,256]{1,0:T(8,128)(2,1)} %bitcast.158, ...), custom_call_target="tpu_custom_call" | custom-call | flops 4227858432 | bytes 8388608 | tf_op jit(solution)/shard_map/attend/pallas_call | solution.py:128
  203.6 17.8 %attend.4 = bf16[256,512]{1,0:T(8,128)(2,1)} custom-call(s32[1]{0:T(128)} %copy.111.clen_ref, bf16[256,896]{1,0:T(8,128)(2,1)} %copy.74.q_ref, bf16[4096,256]{1,0:T(8,128)(2,1)} %bitcast.143, bf16[4096,256]{1,0:T(8,128)(2,1)} %bitcast.144, bf16[1024,256]{1,0:T(8,128)(2,1)} %bitcast.159, bf16[1024,256]{1,0:T(8,128)(2,1)} %bitcast.160, ...), custom_call_target="tpu_custom_call" | custom-call | flops 2415919104 | bytes 8388608 | tf_op jit(solution)/shard_map/attend/pallas_call | solution.py:128
  221.3 23.9 %collective-permute-start.26 = (bf16[448,896]{1,0:T(8,128)(2,1)}, bf16[448,896]{1,0:T(8,128)(2,1)}, u32[]{:S(2)}, u32[]{:S(2)}) collective-permute-start(bf16[448,896]{1,0:T(8,128)(2,1)} %collective-permute-done.25), channel_id=1, source_target_pairs={{0,16},{16,0},{1,17},{17,1},{2,18},{18,2},{3,19},{19,3},{4,20},{20... | collective-permute-start | bytes 2408456 | tf_op jit(solution)/shard_map/ppermute | solution.py:223
  250.2 14.1 %attend.5 = bf16[256,384]{1,0:T(8,128)(2,1)} custom-call(s32[1]{0:T(128)} %copy.111.clen_ref, bf16[256,896]{1,0:T(8,128)(2,1)} %copy.75.q_ref, bf16[4096,256]{1,0:T(8,128)(2,1)} %bitcast.145, bf16[4096,256]{1,0:T(8,128)(2,1)} %bitcast.146, bf16[1024,256]{1,0:T(8,128)(2,1)} %bitcast.161, bf16[1024,256]{1,0:T(8,128)(2,1)} %bitcast.162, ...), custom_call_target="tpu_custom_call" | custom-call | flops 1811939328 | bytes 8388608 | tf_op jit(solution)/shard_map/attend/pallas_call | solution.py:128
  279.0 6.2 %collective-permute-start.24 = (bf16[448,896]{1,0:T(8,128)(2,1)}, bf16[448,896]{1,0:T(8,128)(2,1)S(1)}, u32[]{:S(2)}, u32[]{:S(2)}) collective-permute-start(bf16[448,896]{1,0:T(8,128)(2,1)} %collective-permute-done.23), channel_id=1, source_target_pairs={{0,16},{16,0},{1,17},{17,1},{2,18},{18,2},{3,19},{19,3},{4,20},{20... | collective-permute-start | bytes 2408456 | tf_op jit(solution)/shard_map/ppermute | solution.py:223
  290.1 14.0 %collective-permute-done.24 = bf16[448,896]{1,0:T(8,128)(2,1)S(1)} collective-permute-done((bf16[448,896]{1,0:T(8,128)(2,1)}, bf16[448,896]{1,0:T(8,128)(2,1)S(1)}, u32[]{:S(2)}, u32[]{:S(2)}) %collective-permute-start.24) | collective-permute-done | bytes 802848 | tf_op jit(solution)/shard_map/ppermute | solution.py:223
  306.5 11.4 %collective-permute-done.22 = bf16[448,896]{1,0:T(8,128)(2,1)S(1)} collective-permute-done((bf16[448,896]{1,0:T(8,128)(2,1)}, bf16[448,896]{1,0:T(8,128)(2,1)S(1)}, u32[]{:S(2)}, u32[]{:S(2)}) %collective-permute-start.22) | collective-permute-done | bytes 802848 | tf_op jit(solution)/shard_map/ppermute | solution.py:223
  325.3 3.0 dynamic_update_slice.90
  330.3 3.0 dynamic_update_slice.91
  333.3 3.0 dynamic_update_slice.92
  369.0 12.6 %all-gather.9.cloned.1.call-done.rows_ref = bf16[256,3584]{1,0:T(8,128)(2,1)} async-done(((bf16[64,3584]{1,0:T(8,128)(2,1)}), bf16[256,3584]{1,0:T(8,128)(2,1)}) %all-gather.9.cloned.1.call-update) | async-done | bytes 1835024 | tf_op jit(solution)/shard_map/all_gather | solution.py:296
  381.6 41.4 %gated_mlp.2 = f32[256,3584]{1,0:T(8,128)} custom-call(bf16[256,3584]{1,0:T(8,128)(2,1)} %all-gather.9.cloned.1.call-done.rows_ref, bf16[3584,4736]{1,0:T(8,128)(2,1)} %gate_ref.3, bf16[3584,4736]{1,0:T(8,128)(2,1)} %up_ref.3, bf16[4736,3584]{1,0:T(8,128)(2,1)} %down_ref.3), custom_call_target="tpu_custom_call" | custom-call | flops 26071793664 | bytes 101842944 | tf_op jit(solution)/shard_map/gated_mlp/pallas_call | solution.py:170
  423.4 41.6 %gated_mlp.3 = f32[256,3584]{1,0:T(8,128)} custom-call(bf16[256,3584]{1,0:T(8,128)(2,1)} %all-gather.11.cloned.1.call-done.rows_ref, bf16[3584,4736]{1,0:T(8,128)(2,1)} %gate_ref.3, bf16[3584,4736]{1,0:T(8,128)(2,1)} %up_ref.3, bf16[4736,3584]{1,0:T(8,128)(2,1)} %down_ref.3), custom_call_target="tpu_custom_call" | custom-call | flops 26071793664 | bytes 101842944 | tf_op jit(solution)/shard_map/gated_mlp/pallas_call | solution.py:170
  465.0 27.8 %reduce-scatter.3.cloned.1.call-done = f32[64,3584]{1,0:T(8,128)} async-done(((f32[256,3584]{1,0:T(8,128)}), f32[64,3584]{1,0:T(8,128)}) %reduce-scatter.3.cloned.1.call-update) | async-done | bytes 917520 | tf_op jit(solution)/shard_map/reduce_scatter | solution.py:298
  494.1 69.7 %reduce-scatter.5.cloned.1.call-done = f32[64,3584]{1,0:T(8,128)} async-done(((f32[256,3584]{1,0:T(8,128)}), f32[64,3584]{1,0:T(8,128)}) %reduce-scatter.5.cloned.1.call-update) | async-done | bytes 917520 | tf_op jit(solution)/shard_map/reduce_scatter | solution.py:298
  (281 shorter events, 131.0 us)
Async XLA Ops:
  6.5 125.4 %all-gather.7.cloned.1.call-start = ((), (), s32[]{:S(2)}) async-start(), calls=%async_computation.3 | async-start | bytes 2293760 | tf_op jit(solution)/shard_map/all_gather | solution.py:212
  8.9 152.0 %all-gather.5.cloned.1.call-start = ((), (), s32[]{:S(2)}) async-start(), calls=%async_computation.2 | async-start | bytes 2293760 | tf_op jit(solution)/shard_map/all_gather | solution.py:212
  11.5 189.2 %collective-permute-start.25 = (bf16[448,896]{1,0:T(8,128)(2,1)}, bf16[448,896]{1,0:T(8,128)(2,1)}, u32[]{:S(2)}, u32[]{:S(2)}) collective-permute-start(bf16[448,896]{1,0:T(8,128)(2,1)} %dynamic_slice.74), channel_id=1, source_target_pairs={{0,12},{4,0},{8,4},{12,8},{1,13},{5,1},{9,5},{13,9},{2,14},{6,2},{... | collective-permute-start | bytes 2408456 | tf_op jit(solution)/shard_map/ppermute | solution.py:201
  16.6 248.6 %collective-permute-start.23 = (bf16[448,896]{1,0:T(8,128)(2,1)}, bf16[448,896]{1,0:T(8,128)(2,1)}, u32[]{:S(2)}, u32[]{:S(2)}) collective-permute-start(bf16[448,896]{1,0:T(8,128)(2,1)} %dynamic_slice.74), channel_id=1, source_target_pairs={{0,8},{4,12},{8,0},{12,4},{1,9},{5,13},{9,1},{13,5},{2,10},{6,14},... | collective-permute-start | bytes 2408456 | tf_op jit(solution)/shard_map/ppermute | solution.py:201
  17.1 67.5 %collective-permute-start = (bf16[256,256]{1,0:T(8,128)(2,1)S(1)}, bf16[256,256]{1,0:T(8,128)(2,1)S(1)}, u32[]{:S(2)}, u32[]{:S(2)}) collective-permute-start(bf16[256,256]{1,0:T(8,128)(2,1)S(1)} %bitcast.190), channel_id=1, source_target_pairs={{0,4},{4,8},{8,12},{12,0},{1,5},{5,9},{9,13},{13,1},{2,6},{6,10},{... | collective-permute-start | bytes 393224 | tf_op jit(solution)/shard_map/ppermute | solution.py:201
  18.3 89.0 %collective-permute-start.1 = (bf16[256,256]{1,0:T(8,128)(2,1)S(1)}, bf16[256,256]{1,0:T(8,128)(2,1)S(1)}, u32[]{:S(2)}, u32[]{:S(2)}) collective-permute-start(bf16[256,256]{1,0:T(8,128)(2,1)S(1)} %bitcast.189), channel_id=1, source_target_pairs={{0,8},{4,12},{8,0},{12,4},{1,9},{5,13},{9,1},{13,5},{2,10},{6,14},... | collective-permute-start | bytes 393224 | tf_op jit(solution)/shard_map/ppermute | solution.py:201
  20.4 86.9 %collective-permute-start.2 = (bf16[256,256]{1,0:T(8,128)(2,1)S(1)}, bf16[256,256]{1,0:T(8,128)(2,1)S(1)}, u32[]{:S(2)}, u32[]{:S(2)}) collective-permute-start(bf16[256,256]{1,0:T(8,128)(2,1)S(1)} %bitcast.188), channel_id=1, source_target_pairs={{0,12},{4,0},{8,4},{12,8},{1,13},{5,1},{9,5},{13,9},{2,14},{6,2},{... | collective-permute-start | bytes 393224 | tf_op jit(solution)/shard_map/ppermute | solution.py:201
  23.4 358.2 %all-gather.9.cloned.1.call-start = ((), (), s32[]{:S(2)}) async-start(), calls=%async_computation.4 | async-start | bytes 2293760 | tf_op jit(solution)/shard_map/all_gather | solution.py:296
  111.3 20.5 %collective-permute-start.5 = (bf16[1024,256]{1,0:T(8,128)(2,1)S(1)}, bf16[1024,256]{1,0:T(8,128)(2,1)S(1)}, u32[]{:S(2)}, u32[]{:S(2)}) collective-permute-start(bf16[1024,256]{1,0:T(8,128)(2,1)S(1)} %bitcast.170), channel_id=1, source_target_pairs={{0,3},{1,0},{2,1},{3,2},{4,7},{5,4},{6,5},{7,6},{8,11},{9,8},{10,9... | collective-permute-start | bytes 1572872 | tf_op jit(solution)/shard_map/ppermute | solution.py:201
  177.3 88.6 %collective-permute-start.21 = (bf16[448,896]{1,0:T(8,128)(2,1)}, bf16[448,896]{1,0:T(8,128)(2,1)}, u32[]{:S(2)}, u32[]{:S(2)}) collective-permute-start(bf16[448,896]{1,0:T(8,128)(2,1)} %dynamic_slice.74), channel_id=1, source_target_pairs={{0,4},{4,8},{8,12},{12,0},{1,5},{5,9},{9,13},{13,1},{2,6},{6,10},{... | collective-permute-start | bytes 2408456 | tf_op jit(solution)/shard_map/ppermute | solution.py:201
  195.9 25.5 %collective-permute-start.15 = (bf16[64,896]{1,0:T(8,128)(2,1)S(1)}, bf16[64,896]{1,0:T(8,128)(2,1)S(1)}, u32[]{:S(2)}, u32[]{:S(2)}) collective-permute-start(bf16[64,896]{1,0:T(8,128)(2,1)S(1)} %get-tuple-element.67), channel_id=1, source_target_pairs={{0,4},{4,8},{8,12},{12,0},{1,5},{5,9},{9,13},{13,1},{2,6},{6,10},{... | collective-permute-start | bytes 344072 | tf_op jit(solution)/shard_map/ppermute | solution.py:201
  196.8 48.4 %collective-permute-start.16 = (bf16[64,896]{1,0:T(8,128)(2,1)S(1)}, bf16[64,896]{1,0:T(8,128)(2,1)S(1)}, u32[]{:S(2)}, u32[]{:S(2)}) collective-permute-start(bf16[64,896]{1,0:T(8,128)(2,1)S(1)} %get-tuple-element.66), channel_id=1, source_target_pairs={{0,8},{4,12},{8,0},{12,4},{1,9},{5,13},{9,1},{13,5},{2,10},{6,14},... | collective-permute-start | bytes 344072 | tf_op jit(solution)/shard_map/ppermute | solution.py:201
  200.7 44.5 %collective-permute-start.17 = (bf16[64,896]{1,0:T(8,128)(2,1)S(1)}, bf16[64,896]{1,0:T(8,128)(2,1)S(1)}, u32[]{:S(2)}, u32[]{:S(2)}) collective-permute-start(bf16[64,896]{1,0:T(8,128)(2,1)S(1)} %get-tuple-element.65), channel_id=1, source_target_pairs={{0,12},{4,0},{8,4},{12,8},{1,13},{5,1},{9,5},{13,9},{2,14},{6,2},{... | collective-permute-start | bytes 344072 | tf_op jit(solution)/shard_map/ppermute | solution.py:201
  221.3 66.0 %collective-permute-start.26 = (bf16[448,896]{1,0:T(8,128)(2,1)}, bf16[448,896]{1,0:T(8,128)(2,1)}, u32[]{:S(2)}, u32[]{:S(2)}) collective-permute-start(bf16[448,896]{1,0:T(8,128)(2,1)} %collective-permute-done.25), channel_id=1, source_target_pairs={{0,16},{16,0},{1,17},{17,1},{2,18},{18,2},{3,19},{19,3},{4,20},{20... | collective-permute-start | bytes 2408456 | tf_op jit(solution)/shard_map/ppermute | solution.py:223
  245.3 25.2 %collective-permute-start.19 = (bf16[4,64,896]{2,1,0:T(8,128)(2,1)S(1)}, bf16[4,64,896]{2,1,0:T(8,128)(2,1)S(1)}, u32[]{:S(2)}, u32[]{:S(2)}) collective-permute-start(bf16[4,64,896]{2,1,0:T(8,128)(2,1)S(1)} %pad_maximum_fusion.5), channel_id=1, source_target_pairs={{0,2},{1,3},{2,0},{3,1},{4,6},{5,7},{6,4},{7,5},{8,10},{9,11},{10,... | collective-permute-start | bytes 1376264 | tf_op jit(solution)/shard_map/ppermute | solution.py:223
  249.2 19.6 %collective-permute-start.34 = (bf16[64,512]{1,0:T(8,128)(2,1)S(1)}, bf16[64,512]{1,0:T(8,128)(2,1)S(1)}, u32[]{:S(2)}, u32[]{:S(2)}) collective-permute-start(bf16[64,512]{1,0:T(8,128)(2,1)S(1)} %get-tuple-element.70), channel_id=1, source_target_pairs={{0,12},{4,0},{8,4},{12,8},{1,13},{5,1},{9,5},{13,9},{2,14},{6,2},{... | collective-permute-start | bytes 196616 | tf_op jit(solution)/shard_map/ppermute | solution.py:201
  268.8 17.9 %collective-permute-start.18 = (bf16[4,64,896]{2,1,0:T(8,128)(2,1)S(1)}, bf16[4,64,896]{2,1,0:T(8,128)(2,1)S(1)}, u32[]{:S(2)}, u32[]{:S(2)}) collective-permute-start(bf16[4,64,896]{2,1,0:T(8,128)(2,1)S(1)} %pad_maximum_fusion.5), channel_id=1, source_target_pairs={{0,1},{1,0},{2,3},{3,2},{4,5},{5,4},{6,7},{7,6},{8,9},{9,8},{10,11... | collective-permute-start | bytes 1376264 | tf_op jit(solution)/shard_map/ppermute | solution.py:223
  279.0 25.1 %collective-permute-start.24 = (bf16[448,896]{1,0:T(8,128)(2,1)}, bf16[448,896]{1,0:T(8,128)(2,1)S(1)}, u32[]{:S(2)}, u32[]{:S(2)}) collective-permute-start(bf16[448,896]{1,0:T(8,128)(2,1)} %collective-permute-done.23), channel_id=1, source_target_pairs={{0,16},{16,0},{1,17},{17,1},{2,18},{18,2},{3,19},{19,3},{4,20},{20... | collective-permute-start | bytes 2408456 | tf_op jit(solution)/shard_map/ppermute | solution.py:223
  285.2 32.7 %collective-permute-start.22 = (bf16[448,896]{1,0:T(8,128)(2,1)}, bf16[448,896]{1,0:T(8,128)(2,1)S(1)}, u32[]{:S(2)}, u32[]{:S(2)}) collective-permute-start(bf16[448,896]{1,0:T(8,128)(2,1)} %collective-permute-done.21), channel_id=1, source_target_pairs={{0,16},{16,0},{1,17},{17,1},{2,18},{18,2},{3,19},{19,3},{4,20},{20... | collective-permute-start | bytes 2408456 | tf_op jit(solution)/shard_map/ppermute | solution.py:223
  286.7 38.1 %collective-permute-start.37 = (bf16[4,64,896]{2,1,0:T(8,128)(2,1)S(1)}, bf16[4,64,896]{2,1,0:T(8,128)(2,1)S(1)}, u32[]{:S(2)}, u32[]{:S(2)}) collective-permute-start(bf16[4,64,896]{2,1,0:T(8,128)(2,1)S(1)} %pad_maximum_fusion.6), channel_id=1, source_target_pairs={{0,2},{1,3},{2,0},{3,1},{4,6},{5,7},{6,4},{7,5},{8,10},{9,11},{10,... | collective-permute-start | bytes 1376264 | tf_op jit(solution)/shard_map/ppermute | solution.py:223
  324.5 16.6 %collective-permute-start.36 = (bf16[4,64,896]{2,1,0:T(8,128)(2,1)S(1)}, bf16[4,64,896]{2,1,0:T(8,128)(2,1)S(1)}, u32[]{:S(2)}, u32[]{:S(2)}) collective-permute-start(bf16[4,64,896]{2,1,0:T(8,128)(2,1)S(1)} %pad_maximum_fusion.6), channel_id=1, source_target_pairs={{0,1},{1,0},{2,3},{3,2},{4,5},{5,4},{6,7},{7,6},{8,9},{9,8},{10,11... | collective-permute-start | bytes 1376264 | tf_op jit(solution)/shard_map/ppermute | solution.py:223
  340.8 82.5 %all-gather.11.cloned.1.call-start = ((), (), s32[]{:S(2)}) async-start(), calls=%async_computation.6 | async-start | bytes 2293760 | tf_op jit(solution)/shard_map/all_gather | solution.py:296
  369.0 123.8 %reduce-scatter.3.cloned.1.call-start = ((), (), s32[]{:S(2)}) async-start(), calls=%async_computation.5 | async-start | bytes 4587520 | tf_op jit(solution)/shard_map/reduce_scatter | solution.py:298
  423.0 140.8 %reduce-scatter.5.cloned.1.call-start = ((), (), s32[]{:S(2)}) async-start(), calls=%async_computation.7 | async-start | bytes 4587520 | tf_op jit(solution)/shard_map/reduce_scatter | solution.py:298
  (60 other events, 775.3 us)
Sparse Core Ops, SparseCore 0:
  9.0 80.4 all-gather.6
  91.1 55.1 all-gather.4
  341.0 40.5 all-gather.8
  383.0 40.1 all-gather.10
  425.4 67.3 reduce-scatter.2
  494.9 68.8 reduce-scatter.4

commit v5 on v4

--- a/solution.py
+++ b/solution.py
@@ -218,6 +218,7 @@
         cache_kv = share(cache_kv)
 
         column_width = d_model // cp_size
+        core, row_y = cp % 2, cp // 2
 
         def flipped(part, flip, axis_name='cp', size=cp_size):
             return part if flip == 0 else lax.ppermute(part, axis_name, [(i, i ^ flip) for i in range(size)])
@@ -287,11 +288,10 @@
             rows_in = jnp.concatenate(spread_rows, axis=1)
             attn_out = sum(jnp.dot(rows_in[shift], w_all[shift], preferred_element_type=jnp.float32) for shift in range(tp_size))
             mid_columns = (jnp.concatenate([r[rows] for r in residual_columns], axis=0).astype(jnp.float32) + attn_out).astype(jnp.bfloat16)
-            mid = jnp.zeros((RUN, cp_size, column_width), jnp.bfloat16)
-            for flip in range(cp_size):
-                part = flipped(mid_columns[flip * RUN:(flip + 1) * RUN], flip)
-                mid = lax.dynamic_update_slice_in_dim(mid, part[:, None, :], cp ^ flip, 1)
-            mid = mid.reshape(RUN, d_model)
+            parts = [flipped(mid_columns[flip * RUN:(flip + 1) * RUN], flip) for flip in range(cp_size)]
+            for bit, choice in ((1, core), (2, row_y)):
+                parts = [jnp.where(choice == 1, parts[i ^ bit], parts[i]) for i in range(cp_size)]
+            mid = jnp.concatenate(parts, axis=1)
             normed_mid = rms_norm(mid, norm2_gain)
             group_mid = lax.all_gather(normed_mid, 'tp', axis=0, tiled=True)
             mlp_part = gated_mlp(group_mid, w_gate, w_up, w_down)

time: 583 us -> 574 us (0.985)
  local copies, waits for them, and re-layouts: 48.2 us -> 23.9 us
  waiting for transfers between devices: 251 us -> 268 us
    dynamic_update_slice x8 -> x0, local copies, waits for them, and re-layouts: 23.8 us -> none  [layer(): mid = lax.dynamic_update_slice_in_dim(mid, part[:, None, :], cp ^ flip, 1)]
    all_gather x2, waiting for transfers between devices: 12.6 us -> 21.7 us  [layer(): group_mid = lax.all_gather(normed_mid, 'tp', axis=0, tiled=True)]
    ppermute x18, waiting for transfers between devices: 35.5 us -> 43.3 us  [flipped(): lax.ppermute(part, axis_name, [(i, i ^ flip) for i in range(size)])]
  transfers between devices with their start and end apart: 48 -> 48, of which waited for: 19 -> 20; matrix products, arithmetic and copies ran while one was open for 16% -> 12% of each run, Pallas kernels for 22% -> 23%
where the time goes in v5:
time: 574 us; the launch traced here: 564 us
  waiting for transfers between devices  268 us (47%)
  Pallas kernels  129 us (22%)
  starting transfers between devices  78.8 us (14%)
  matrix products  34.2 us (6%)
  local copies, waits for them, and re-layouts  23.9 us (4%)
  between operations  15.6 us (3%)
  other arithmetic  14.6 us (3%)
    ppermute x24, waiting for transfers between devices, shifted(): lax.ppermute(part, axis_name, [(i, (i + shift) % size) for i in range(siz...  106 us
    reduce_scatter x2, waiting for transfers between devices, layer(): summed = lax.psum_scatter(mlp_part, 'tp', scatter_dimension=0, tiled=True)  97.5 us
    pallas_call x2, Pallas kernels, gated_mlp(): pl.pallas_call(functools.partial(mlp_kernel, width - (steps - 1) * MLP_TI...  83 us
    pallas_call x3, Pallas kernels, attention(): pl.pallas_call(functools.partial(attn_kernel, is_low), grid=(heads,), out...  45.9 us
    ppermute x18, waiting for transfers between devices, flipped(): lax.ppermute(part, axis_name, [(i, i ^ flip) for i in range(size)])  43.3 us
    ppermute x18, starting transfers between devices, flipped(): lax.ppermute(part, axis_name, [(i, i ^ flip) for i in range(size)])  41.1 us
    ppermute x24, starting transfers between devices, shifted(): lax.ppermute(part, axis_name, [(i, (i + shift) % size) for i in range(siz...  37.3 us
    all_gather x2, waiting for transfers between devices, layer(): group_mid = lax.all_gather(normed_mid, 'tp', axis=0, tiled=True)  21.7 us
  transfers between devices with their start and end apart: 48, of which 20 were waited for; matrix products, arithmetic and copies ran while one was open for 12% of the time, Pallas kernels for 23%

profile of v5, /device:TPU:0, one launch (start us, length us, event | category | flops | bytes accessed | tf_op | source)
XLA Modules:
  0.0 564.4 jit_solution(7340712310024750897)
XLA Ops:
  11.5 5.1 collective-permute-start.25
  20.4 3.0 collective-permute-start.2
  24.5 60.1 %collective-permute-done = bf16[256,256]{1,0:T(8,128)(2,1)S(1)} collective-permute-done((bf16[256,256]{1,0:T(8,128)(2,1)S(1)}, bf16[256,256]{1,0:T(8,128)(2,1)S(1)}, u32[]{:S(2)}, u32[]{:S(2)}) %collective-permute-start) | collective-permute-done | bytes 131104 | tf_op jit(solution)/shard_map/ppermute | solution.py:201
  84.6 22.7 %collective-permute-done.1 = bf16[256,256]{1,0:T(8,128)(2,1)S(1)} collective-permute-done((bf16[256,256]{1,0:T(8,128)(2,1)S(1)}, bf16[256,256]{1,0:T(8,128)(2,1)S(1)}, u32[]{:S(2)}, u32[]{:S(2)}) %collective-permute-start.1) | collective-permute-done | bytes 131104 | tf_op jit(solution)/shard_map/ppermute | solution.py:201
  112.9 8.0 %collective-permute-done.3 = bf16[1024,256]{1,0:T(8,128)(2,1)} collective-permute-done((bf16[1024,256]{1,0:T(8,128)(2,1)S(1)}, bf16[1024,256]{1,0:T(8,128)(2,1)}, u32[]{:S(2)}, u32[]{:S(2)}) %collective-permute-start.3) | collective-permute-done | bytes 524320 | tf_op jit(solution)/shard_map/ppermute | solution.py:201
  123.6 8.3 %collective-permute-done.5 = bf16[1024,256]{1,0:T(8,128)(2,1)S(1)} collective-permute-done((bf16[1024,256]{1,0:T(8,128)(2,1)S(1)}, bf16[1024,256]{1,0:T(8,128)(2,1)S(1)}, u32[]{:S(2)}, u32[]{:S(2)}) %collective-permute-start.5) | collective-permute-done | bytes 524320 | tf_op jit(solution)/shard_map/ppermute | solution.py:201
  141.9 5.5 fusion.77
  153.0 4.9 collective-permute-done.10
  157.9 3.0 collective-permute-done.11
  169.2 5.6 fusion.71
  182.3 14.1 %attend.3 = bf16[256,896]{1,0:T(8,128)(2,1)} custom-call(s32[1]{0:T(128)} %copy.77.clen_ref, bf16[256,896]{1,0:T(8,128)(2,1)} %copy.52.q_ref, bf16[4096,256]{1,0:T(8,128)(2,1)} %bitcast.125, bf16[4096,256]{1,0:T(8,128)(2,1)} %bitcast.126, bf16[1024,256]{1,0:T(8,128)(2,1)} %bitcast.137, bf16[1024,256]{1,0:T(8,128)(2,1)} %bitcast.138, ...), custom_call_target="tpu_custom_call" | custom-call | flops 4227858432 | bytes 8388608 | tf_op jit(solution)/shard_map/attend/pallas_call | solution.py:128
  205.1 17.8 %attend.4 = bf16[256,512]{1,0:T(8,128)(2,1)} custom-call(s32[1]{0:T(128)} %copy.77.clen_ref, bf16[256,896]{1,0:T(8,128)(2,1)} %copy.54.q_ref, bf16[4096,256]{1,0:T(8,128)(2,1)} %bitcast.127, bf16[4096,256]{1,0:T(8,128)(2,1)} %bitcast.128, bf16[1024,256]{1,0:T(8,128)(2,1)} %bitcast.139, bf16[1024,256]{1,0:T(8,128)(2,1)} %bitcast.140, ...), custom_call_target="tpu_custom_call" | custom-call | flops 2415919104 | bytes 8388608 | tf_op jit(solution)/shard_map/attend/pallas_call | solution.py:128
  222.9 23.9 %collective-permute-start.26 = (bf16[448,896]{1,0:T(8,128)(2,1)}, bf16[448,896]{1,0:T(8,128)(2,1)S(1)}, u32[]{:S(2)}, u32[]{:S(2)}) collective-permute-start(bf16[448,896]{1,0:T(8,128)(2,1)} %collective-permute-done.25), channel_id=1, source_target_pairs={{0,16},{16,0},{1,17},{17,1},{2,18},{18,2},{3,19},{19,3},{4,20},{20... | collective-permute-start | bytes 2408456 | tf_op jit(solution)/shard_map/ppermute | solution.py:224
  246.8 2.9 collective-permute-start.19
  251.8 14.1 %attend.5 = bf16[256,384]{1,0:T(8,128)(2,1)} custom-call(s32[1]{0:T(128)} %copy.77.clen_ref, bf16[256,896]{1,0:T(8,128)(2,1)} %copy.55.q_ref, bf16[4096,256]{1,0:T(8,128)(2,1)} %bitcast.129, bf16[4096,256]{1,0:T(8,128)(2,1)} %bitcast.130, bf16[1024,256]{1,0:T(8,128)(2,1)} %bitcast.141, bf16[1024,256]{1,0:T(8,128)(2,1)} %bitcast.142, ...), custom_call_target="tpu_custom_call" | custom-call | flops 1811939328 | bytes 8388608 | tf_op jit(solution)/shard_map/attend/pallas_call | solution.py:128
  280.5 6.2 %collective-permute-start.24 = (bf16[448,896]{1,0:T(8,128)(2,1)}, bf16[448,896]{1,0:T(8,128)(2,1)S(1)}, u32[]{:S(2)}, u32[]{:S(2)}) collective-permute-start(bf16[448,896]{1,0:T(8,128)(2,1)} %collective-permute-done.23), channel_id=1, source_target_pairs={{0,16},{16,0},{1,17},{17,1},{2,18},{18,2},{3,19},{19,3},{4,20},{20... | collective-permute-start | bytes 2408456 | tf_op jit(solution)/shard_map/ppermute | solution.py:224
  291.3 14.4 %collective-permute-done.24 = bf16[448,896]{1,0:T(8,128)(2,1)S(1)} collective-permute-done((bf16[448,896]{1,0:T(8,128)(2,1)}, bf16[448,896]{1,0:T(8,128)(2,1)S(1)}, u32[]{:S(2)}, u32[]{:S(2)}) %collective-permute-start.24) | collective-permute-done | bytes 802848 | tf_op jit(solution)/shard_map/ppermute | solution.py:224
  308.1 11.3 %collective-permute-done.22 = bf16[448,896]{1,0:T(8,128)(2,1)S(1)} collective-permute-done((bf16[448,896]{1,0:T(8,128)(2,1)}, bf16[448,896]{1,0:T(8,128)(2,1)S(1)}, u32[]{:S(2)}, u32[]{:S(2)}) %collective-permute-start.22) | collective-permute-done | bytes 802848 | tf_op jit(solution)/shard_map/ppermute | solution.py:224
  346.9 3.0 collective-permute-done.40
  351.2 21.7 %all-gather.9.cloned.1.call-done.rows_ref = bf16[256,3584]{1,0:T(8,128)(2,1)} async-done(((bf16[64,3584]{1,0:T(8,128)(2,1)}), bf16[256,3584]{1,0:T(8,128)(2,1)}) %all-gather.9.cloned.1.call-update) | async-done | bytes 1835024 | tf_op jit(solution)/shard_map/all_gather | solution.py:296
  372.9 41.4 %gated_mlp.2 = f32[256,3584]{1,0:T(8,128)} custom-call(bf16[256,3584]{1,0:T(8,128)(2,1)} %all-gather.9.cloned.1.call-done.rows_ref, bf16[3584,4736]{1,0:T(8,128)(2,1)} %gate_ref.3, bf16[3584,4736]{1,0:T(8,128)(2,1)} %up_ref.3, bf16[4736,3584]{1,0:T(8,128)(2,1)} %down_ref.3), custom_call_target="tpu_custom_call" | custom-call | flops 26071793664 | bytes 101842944 | tf_op jit(solution)/shard_map/gated_mlp/pallas_call | solution.py:170
  414.6 41.6 %gated_mlp.3 = f32[256,3584]{1,0:T(8,128)} custom-call(bf16[256,3584]{1,0:T(8,128)(2,1)} %all-gather.11.cloned.1.call-done.rows_ref, bf16[3584,4736]{1,0:T(8,128)(2,1)} %gate_ref.3, bf16[3584,4736]{1,0:T(8,128)(2,1)} %up_ref.3, bf16[4736,3584]{1,0:T(8,128)(2,1)} %down_ref.3), custom_call_target="tpu_custom_call" | custom-call | flops 26071793664 | bytes 101842944 | tf_op jit(solution)/shard_map/gated_mlp/pallas_call | solution.py:170
  456.2 27.8 %reduce-scatter.3.cloned.1.call-done = f32[64,3584]{1,0:T(8,128)} async-done(((f32[256,3584]{1,0:T(8,128)}), f32[64,3584]{1,0:T(8,128)}) %reduce-scatter.3.cloned.1.call-update) | async-done | bytes 917520 | tf_op jit(solution)/shard_map/reduce_scatter | solution.py:298
  485.4 69.7 %reduce-scatter.5.cloned.1.call-done = f32[64,3584]{1,0:T(8,128)} async-done(((f32[256,3584]{1,0:T(8,128)}), f32[64,3584]{1,0:T(8,128)}) %reduce-scatter.5.cloned.1.call-update) | async-done | bytes 917520 | tf_op jit(solution)/shard_map/reduce_scatter | solution.py:298
  (265 shorter events, 112.9 us)
Async XLA Ops:
  6.5 125.4 %all-gather.7.cloned.1.call-start = ((), (), s32[]{:S(2)}) async-start(), calls=%async_computation.3 | async-start | bytes 2293760 | tf_op jit(solution)/shard_map/all_gather | solution.py:212
  8.9 152.0 %all-gather.5.cloned.1.call-start = ((), (), s32[]{:S(2)}) async-start(), calls=%async_computation.2 | async-start | bytes 2293760 | tf_op jit(solution)/shard_map/all_gather | solution.py:212
  11.5 190.8 %collective-permute-start.25 = (bf16[448,896]{1,0:T(8,128)(2,1)}, bf16[448,896]{1,0:T(8,128)(2,1)}, u32[]{:S(2)}, u32[]{:S(2)}) collective-permute-start(bf16[448,896]{1,0:T(8,128)(2,1)} %dynamic_slice.74), channel_id=1, source_target_pairs={{0,12},{4,0},{8,4},{12,8},{1,13},{5,1},{9,5},{13,9},{2,14},{6,2},{... | collective-permute-start | bytes 2408456 | tf_op jit(solution)/shard_map/ppermute | solution.py:201
  16.6 250.2 %collective-permute-start.23 = (bf16[448,896]{1,0:T(8,128)(2,1)}, bf16[448,896]{1,0:T(8,128)(2,1)}, u32[]{:S(2)}, u32[]{:S(2)}) collective-permute-start(bf16[448,896]{1,0:T(8,128)(2,1)} %dynamic_slice.74), channel_id=1, source_target_pairs={{0,8},{4,12},{8,0},{12,4},{1,9},{5,13},{9,1},{13,5},{2,10},{6,14},... | collective-permute-start | bytes 2408456 | tf_op jit(solution)/shard_map/ppermute | solution.py:201
  17.1 67.5 %collective-permute-start = (bf16[256,256]{1,0:T(8,128)(2,1)S(1)}, bf16[256,256]{1,0:T(8,128)(2,1)S(1)}, u32[]{:S(2)}, u32[]{:S(2)}) collective-permute-start(bf16[256,256]{1,0:T(8,128)(2,1)S(1)} %bitcast.168), channel_id=1, source_target_pairs={{0,4},{4,8},{8,12},{12,0},{1,5},{5,9},{9,13},{13,1},{2,6},{6,10},{... | collective-permute-start | bytes 393224 | tf_op jit(solution)/shard_map/ppermute | solution.py:201
  18.3 89.0 %collective-permute-start.1 = (bf16[256,256]{1,0:T(8,128)(2,1)S(1)}, bf16[256,256]{1,0:T(8,128)(2,1)S(1)}, u32[]{:S(2)}, u32[]{:S(2)}) collective-permute-start(bf16[256,256]{1,0:T(8,128)(2,1)S(1)} %bitcast.167), channel_id=1, source_target_pairs={{0,8},{4,12},{8,0},{12,4},{1,9},{5,13},{9,1},{13,5},{2,10},{6,14},... | collective-permute-start | bytes 393224 | tf_op jit(solution)/shard_map/ppermute | solution.py:201
  20.4 86.9 %collective-permute-start.2 = (bf16[256,256]{1,0:T(8,128)(2,1)S(1)}, bf16[256,256]{1,0:T(8,128)(2,1)S(1)}, u32[]{:S(2)}, u32[]{:S(2)}) collective-permute-start(bf16[256,256]{1,0:T(8,128)(2,1)S(1)} %bitcast.166), channel_id=1, source_target_pairs={{0,12},{4,0},{8,4},{12,8},{1,13},{5,1},{9,5},{13,9},{2,14},{6,2},{... | collective-permute-start | bytes 393224 | tf_op jit(solution)/shard_map/ppermute | solution.py:201
  23.4 349.5 %all-gather.9.cloned.1.call-start = ((), (), s32[]{:S(2)}) async-start(), calls=%async_computation.4 | async-start | bytes 2293760 | tf_op jit(solution)/shard_map/all_gather | solution.py:296
  111.3 20.6 %collective-permute-start.5 = (bf16[1024,256]{1,0:T(8,128)(2,1)S(1)}, bf16[1024,256]{1,0:T(8,128)(2,1)S(1)}, u32[]{:S(2)}, u32[]{:S(2)}) collective-permute-start(bf16[1024,256]{1,0:T(8,128)(2,1)S(1)} %bitcast.148), channel_id=1, source_target_pairs={{0,3},{1,0},{2,1},{3,2},{4,7},{5,4},{6,5},{7,6},{8,11},{9,8},{10,9... | collective-permute-start | bytes 1572872 | tf_op jit(solution)/shard_map/ppermute | solution.py:201
  178.8 88.7 %collective-permute-start.21 = (bf16[448,896]{1,0:T(8,128)(2,1)}, bf16[448,896]{1,0:T(8,128)(2,1)}, u32[]{:S(2)}, u32[]{:S(2)}) collective-permute-start(bf16[448,896]{1,0:T(8,128)(2,1)} %dynamic_slice.74), channel_id=1, source_target_pairs={{0,4},{4,8},{8,12},{12,0},{1,5},{5,9},{9,13},{13,1},{2,6},{6,10},{... | collective-permute-start | bytes 2408456 | tf_op jit(solution)/shard_map/ppermute | solution.py:201
  197.4 25.4 %collective-permute-start.15 = (bf16[64,896]{1,0:T(8,128)(2,1)S(1)}, bf16[64,896]{1,0:T(8,128)(2,1)S(1)}, u32[]{:S(2)}, u32[]{:S(2)}) collective-permute-start(bf16[64,896]{1,0:T(8,128)(2,1)S(1)} %get-tuple-element.73), channel_id=1, source_target_pairs={{0,4},{4,8},{8,12},{12,0},{1,5},{5,9},{9,13},{13,1},{2,6},{6,10},{... | collective-permute-start | bytes 344072 | tf_op jit(solution)/shard_map/ppermute | solution.py:201
  198.3 48.4 %collective-permute-start.16 = (bf16[64,896]{1,0:T(8,128)(2,1)S(1)}, bf16[64,896]{1,0:T(8,128)(2,1)S(1)}, u32[]{:S(2)}, u32[]{:S(2)}) collective-permute-start(bf16[64,896]{1,0:T(8,128)(2,1)S(1)} %get-tuple-element.72), channel_id=1, source_target_pairs={{0,8},{4,12},{8,0},{12,4},{1,9},{5,13},{9,1},{13,5},{2,10},{6,14},... | collective-permute-start | bytes 344072 | tf_op jit(solution)/shard_map/ppermute | solution.py:201
  202.2 44.5 %collective-permute-start.17 = (bf16[64,896]{1,0:T(8,128)(2,1)S(1)}, bf16[64,896]{1,0:T(8,128)(2,1)S(1)}, u32[]{:S(2)}, u32[]{:S(2)}) collective-permute-start(bf16[64,896]{1,0:T(8,128)(2,1)S(1)} %get-tuple-element.71), channel_id=1, source_target_pairs={{0,12},{4,0},{8,4},{12,8},{1,13},{5,1},{9,5},{13,9},{2,14},{6,2},{... | collective-permute-start | bytes 344072 | tf_op jit(solution)/shard_map/ppermute | solution.py:201
  222.9 66.0 %collective-permute-start.26 = (bf16[448,896]{1,0:T(8,128)(2,1)}, bf16[448,896]{1,0:T(8,128)(2,1)S(1)}, u32[]{:S(2)}, u32[]{:S(2)}) collective-permute-start(bf16[448,896]{1,0:T(8,128)(2,1)} %collective-permute-done.25), channel_id=1, source_target_pairs={{0,16},{16,0},{1,17},{17,1},{2,18},{18,2},{3,19},{19,3},{4,20},{20... | collective-permute-start | bytes 2408456 | tf_op jit(solution)/shard_map/ppermute | solution.py:224
  246.8 25.2 %collective-permute-start.19 = (bf16[4,64,896]{2,1,0:T(8,128)(2,1)S(1)}, bf16[4,64,896]{2,1,0:T(8,128)(2,1)S(1)}, u32[]{:S(2)}, u32[]{:S(2)}) collective-permute-start(bf16[4,64,896]{2,1,0:T(8,128)(2,1)S(1)} %pad_maximum_fusion.5), channel_id=1, source_target_pairs={{0,2},{1,3},{2,0},{3,1},{4,6},{5,7},{6,4},{7,5},{8,10},{9,11},{10,... | collective-permute-start | bytes 1376264 | tf_op jit(solution)/shard_map/ppermute | solution.py:224
  250.7 19.7 %collective-permute-start.34 = (bf16[64,512]{1,0:T(8,128)(2,1)S(1)}, bf16[64,512]{1,0:T(8,128)(2,1)S(1)}, u32[]{:S(2)}, u32[]{:S(2)}) collective-permute-start(bf16[64,512]{1,0:T(8,128)(2,1)S(1)} %get-tuple-element.76), channel_id=1, source_target_pairs={{0,12},{4,0},{8,4},{12,8},{1,13},{5,1},{9,5},{13,9},{2,14},{6,2},{... | collective-permute-start | bytes 196616 | tf_op jit(solution)/shard_map/ppermute | solution.py:201
  270.4 17.8 %collective-permute-start.18 = (bf16[4,64,896]{2,1,0:T(8,128)(2,1)S(1)}, bf16[4,64,896]{2,1,0:T(8,128)(2,1)S(1)}, u32[]{:S(2)}, u32[]{:S(2)}) collective-permute-start(bf16[4,64,896]{2,1,0:T(8,128)(2,1)S(1)} %pad_maximum_fusion.5), channel_id=1, source_target_pairs={{0,1},{1,0},{2,3},{3,2},{4,5},{5,4},{6,7},{7,6},{8,9},{9,8},{10,11... | collective-permute-start | bytes 1376264 | tf_op jit(solution)/shard_map/ppermute | solution.py:224
  272.0 16.3 %collective-permute-start.20 = (bf16[4,64,896]{2,1,0:T(8,128)(2,1)S(1)}, bf16[4,64,896]{2,1,0:T(8,128)(2,1)S(1)}, u32[]{:S(2)}, u32[]{:S(2)}) collective-permute-start(bf16[4,64,896]{2,1,0:T(8,128)(2,1)S(1)} %collective-permute-done.19), channel_id=1, source_target_pairs={{0,1},{1,0},{2,3},{3,2},{4,5},{5,4},{6,7},{7,6},{8,9},{9,8},{10,11... | collective-permute-start | bytes 1376264 | tf_op jit(solution)/shard_map/ppermute | solution.py:224
  280.5 25.2 %collective-permute-start.24 = (bf16[448,896]{1,0:T(8,128)(2,1)}, bf16[448,896]{1,0:T(8,128)(2,1)S(1)}, u32[]{:S(2)}, u32[]{:S(2)}) collective-permute-start(bf16[448,896]{1,0:T(8,128)(2,1)} %collective-permute-done.23), channel_id=1, source_target_pairs={{0,16},{16,0},{1,17},{17,1},{2,18},{18,2},{3,19},{19,3},{4,20},{20... | collective-permute-start | bytes 2408456 | tf_op jit(solution)/shard_map/ppermute | solution.py:224
  286.7 32.7 %collective-permute-start.22 = (bf16[448,896]{1,0:T(8,128)(2,1)}, bf16[448,896]{1,0:T(8,128)(2,1)S(1)}, u32[]{:S(2)}, u32[]{:S(2)}) collective-permute-start(bf16[448,896]{1,0:T(8,128)(2,1)} %collective-permute-done.21), channel_id=1, source_target_pairs={{0,16},{16,0},{1,17},{17,1},{2,18},{18,2},{3,19},{19,3},{4,20},{20... | collective-permute-start | bytes 2408456 | tf_op jit(solution)/shard_map/ppermute | solution.py:224
  288.2 37.9 %collective-permute-start.37 = (bf16[4,64,896]{2,1,0:T(8,128)(2,1)S(1)}, bf16[4,64,896]{2,1,0:T(8,128)(2,1)S(1)}, u32[]{:S(2)}, u32[]{:S(2)}) collective-permute-start(bf16[4,64,896]{2,1,0:T(8,128)(2,1)S(1)} %pad_maximum_fusion.7), channel_id=1, source_target_pairs={{0,2},{1,3},{2,0},{3,1},{4,6},{5,7},{6,4},{7,5},{8,10},{9,11},{10,... | collective-permute-start | bytes 1376264 | tf_op jit(solution)/shard_map/ppermute | solution.py:224
  331.5 83.1 %all-gather.11.cloned.1.call-start = ((), (), s32[]{:S(2)}) async-start(), calls=%async_computation.6 | async-start | bytes 2293760 | tf_op jit(solution)/shard_map/all_gather | solution.py:296
  351.2 132.9 %reduce-scatter.3.cloned.1.call-start = ((), (), s32[]{:S(2)}) async-start(), calls=%async_computation.5 | async-start | bytes 4587520 | tf_op jit(solution)/shard_map/reduce_scatter | solution.py:298
  414.3 140.8 %reduce-scatter.5.cloned.1.call-start = ((), (), s32[]{:S(2)}) async-start(), calls=%async_computation.7 | async-start | bytes 4587520 | tf_op jit(solution)/shard_map/reduce_scatter | solution.py:298
  (61 other events, 719.7 us)
Sparse Core Ops, SparseCore 0:
  9.0 80.4 all-gather.6
  91.1 55.1 all-gather.4
  331.6 41.2 all-gather.8
  374.3 40.1 all-gather.10
  416.7 67.3 reduce-scatter.2
  486.2 68.8 reduce-scatter.4
